TPU v7x, 16 devices: a 4x2x1 block of a 4x4x8 slice. The times are simulated.
16 devices in a mesh: rep: 2 (over y, z), dp: 8 (over x, core).
Axes of the slice: x: 4, y: 2, z: 1, core: 2. Of those that a mesh axis runs over, the one named last changes fastest.
The devices are a block of a 4x4x8 slice.
Arguments:
- x: bfloat16 [16, 2048, 1152], P(('rep', 'dp')), parts along dimension 0
- dy: bfloat16 [16, 2048, 1152], P(('rep', 'dp')), parts along dimension 0
- w_gate: bfloat16 [2, 1152, 4608], replicated
- w_up: bfloat16 [2, 1152, 4608], replicated
- w_down: bfloat16 [2, 4608, 1152], replicated
- m_w_gate: float32 [2, 1152, 4608], P(None, 'dp')
- m_w_up: float32 [2, 1152, 4608], P(None, 'dp')
- m_w_down: float32 [2, 4608, 1152], P(None, 'dp')
- v_w_gate: float32 [2, 1152, 4608], P(None, 'dp')
- v_w_up: float32 [2, 1152, 4608], P(None, 'dp')
- v_w_down: float32 [2, 4608, 1152], P(None, 'dp')
Outputs:
- output 1: bfloat16 [4, 1152, 4608], P('rep'), parts along dimension 0
- output 2: bfloat16 [4, 1152, 4608], P('rep'), parts along dimension 0
- output 3: bfloat16 [4, 4608, 1152], P('rep'), parts along dimension 0
- output 4: float32 [4, 1152, 4608], P('rep', 'dp'), parts along dimension 0
- output 5: float32 [4, 1152, 4608], P('rep', 'dp'), parts along dimension 0
- output 6: float32 [4, 4608, 1152], P('rep', 'dp'), parts along dimension 0
- output 7: float32 [4, 1152, 4608], P('rep', 'dp'), parts along dimension 0
- output 8: float32 [4, 1152, 4608], P('rep', 'dp'), parts along dimension 0
- output 9: float32 [4, 4608, 1152], P('rep', 'dp'), parts along dimension 0
There are 2 independent parts. A program takes and returns all parts, laid end to end along the dimension named above; an argument that names none is the same for every part.
All inputs are finite; a program needn't handle non-finite values.
Results may differ from a plain program's by a relative error of at most 0.022.
Values are sent between devices in bfloat16 or wider.
A program may use at most 768 MiB of HBM per device.

v0:
```python
import functools

import jax
import jax.numpy as jnp
from jax import lax
from jax.experimental import pallas as pl
from jax.experimental.pallas import tpu as pltpu
from jax.sharding import PartitionSpec as P

NAMES = ("w_gate", "w_up", "w_down")
F32, BF16 = jnp.float32, jnp.bfloat16
NN, NT = (((1,), (0,)), ((), ())), (((1,), (1,)), ((), ()))
MESH = pl.DeviceIdType.MESH
ANY = pl.BlockSpec(memory_space=pl.ANY)
LANES = 128
CORES = 2
VMEM_BYTES = 62 << 20
VMEM_MOST = 67_043_328


def dot(a, b, dims=NN):
    return lax.dot_general(a, b, dims, preferred_element_type=F32)


def norm(h):
    wide = h.astype(F32)
    return (wide * lax.rsqrt(jnp.mean(wide**2, -1, keepdims=True) + 1e-6)).astype(BF16)


def strip(start, size):
    return pl.ds(pl.multiple_of(start, size), size)


def forward_kernel(tile, x_ref, wg_ref, wu_ref, wd_ref, a_ref, h_ref, total):
    block, blocks = pl.program_id(0), pl.num_programs(0)
    tiles = x_ref.shape[0] // tile

    @pl.when(block == 0)
    def _():
        def start(t, _):
            rows = strip(t * tile, tile)
            a_ref[0, rows, :] = norm(x_ref[rows, :])
            total[rows, :] = jnp.zeros((tile, total.shape[1]), F32)
            return 0

        lax.fori_loop(0, tiles, start, 0)

    def one(t, _):
        rows = strip(t * tile, tile)
        a = a_ref[0, rows, :]
        gate, up = dot(a, wg_ref[...]), dot(a, wu_ref[...])
        z = (jax.nn.sigmoid(gate) * gate * up).astype(BF16)
        total[rows, :] += dot(z, wd_ref[...])
        return 0

    lax.fori_loop(0, tiles, one, 0)

    @pl.when(block == blocks - 1)
    def _():
        def end(t, _):
            rows = strip(t * tile, tile)
            h = x_ref[rows, :] + total[rows, :].astype(BF16)
            h_ref[rows, :] = h
            a_ref[1, rows, :] = norm(h)
            return 0

        lax.fori_loop(0, tiles, end, 0)


def forward(x, wg, wu, wd, layer, width=512, tile=512):
    tokens, d = x.shape
    ff = wg.shape[2]
    whole = pl.BlockSpec((tokens, d), lambda i: (0, 0))
    return pl.pallas_call(
        functools.partial(forward_kernel, tile),
        grid=(ff // width,),
        out_shape=[jax.ShapeDtypeStruct((2, tokens, d), BF16), jax.ShapeDtypeStruct((tokens, d), BF16)],
        in_specs=[
            whole,
            pl.BlockSpec((None, d, width), lambda i: (layer, 0, i)),
            pl.BlockSpec((None, d, width), lambda i: (layer, 0, i)),
            pl.BlockSpec((None, width, d), lambda i: (layer, i, 0)),
        ],
        out_specs=[pl.BlockSpec((2, tokens, d), lambda i: (0, 0, 0)), whole],
        scratch_shapes=[pltpu.VMEM((tokens, d), F32)],
        compiler_params=pltpu.CompilerParams(dimension_semantics=("arbitrary",), vmem_limit_bytes=VMEM_BYTES),
        cost_estimate=pl.CostEstimate(flops=6 * tokens * d * ff, bytes_accessed=6 * d * ff + 8 * tokens * d, transcendentals=tokens * ff),
        name="forward",
    )(x, wg, wu, wd)


class Pool:
    def __init__(self, number, chips, core, chip, bufs, sems, gathered):
        self.number, self.chips, self.core, self.chip = number, chips, core, chip
        self.mine, self.other, self.cross, self.near, self.out1, self.out2, self.sum, self.new = bufs
        self.dma, self.credit, self.out_sem, self.ag_sem, self.own_sem = sems
        self.gathered = gathered
        self.slots, self.lanes, self.turns = self.mine.shape[0], self.cross.shape[0], self.ag_sem.shape[0]

    def index(self, chip, core):
        return lax.rem(chip + self.chips, self.chips) * CORES + core

    def device(self, hops, core=None):
        return {"dp": self.index(self.chip + hops, self.core if core is None else core)}

    def partner(self):
        return self.device(0, 1 - self.core)

    def hop(self, sems, src, dst, to):
        return pltpu.make_async_remote_copy(src_ref=src, dst_ref=dst, send_sem=sems.at[0], recv_sem=sems.at[1], device_id=to, device_id_type=MESH)

    def copies0(self, n, rows):
        slot = lax.rem(n, self.slots)
        src = self.mine.at[slot, 1 - self.core, :, pl.ds(0, rows), :]
        return [self.hop(self.dma.at[slot, 0], src, self.other.at[slot, :, pl.ds(0, rows), :], self.partner())]

    def copies1(self, n, rows):
        slot, sem, half = lax.rem(n, self.lanes), lax.rem(n, self.slots), pl.ds(0, rows // 2)
        return [
            self.hop(self.dma.at[sem, 1 + side], self.out1.at[slot, side, half, :], self.cross.at[slot, side, half, :], self.device(1 - 2 * side))
            for side in range(2)
        ]

    def copies2(self, n, rows):
        slot, sem, full = lax.rem(n, self.lanes), lax.rem(n, self.slots), pl.ds(0, rows)
        return [
            self.hop(self.dma.at[sem, 3 + side], self.out2.at[slot, side, full, :], self.near.at[slot, side, full, :], self.device(1 - 2 * side))
            for side in range(2)
        ]

    def both(self, n, hops, start, size):
        slot, chip = lax.rem(n, self.slots), lax.rem(self.chip + hops + self.chips, self.chips)
        rows = pl.ds(start, size)
        return self.mine[slot, self.core, chip, rows, :].astype(F32) + self.other[slot, chip, rows, :].astype(F32)

    def give(self, kind, to):
        pl.semaphore_signal(self.credit.at[kind], inc=1, device_id=to, device_id_type=MESH)

    def take(self, when, kinds):
        @pl.when(when)
        def _():
            for kind in kinds:
                pl.semaphore_wait(self.credit.at[kind], 1)

    def event0(self, n, rows):
        self.take(n >= self.slots, (0,))
        for copy in self.copies0(n, rows):
            copy.start()

    def event1(self, n, rows):
        slot, half = lax.rem(n, self.lanes), rows // 2
        for copy in self.copies0(n, rows):
            copy.wait()
        for side in range(2):
            self.out1[slot, side, pl.ds(0, half), :] = self.both(n, 2, side * half, half).astype(BF16)
        self.take(n >= self.lanes, (1, 2))
        for copy in self.copies1(n, rows):
            copy.start()

    def event2(self, n, rows):
        slot, half = lax.rem(n, self.lanes), rows // 2
        for copy in self.copies1(n, rows):
            copy.wait()
        for side in range(2):
            hops, there, here = 1 - 2 * side, pl.ds(side * half, half), pl.ds((1 - side) * half, half)
            passed = self.both(n, hops, side * half, half) + self.cross[slot, side, pl.ds(0, half), :].astype(F32)
            self.out2[slot, side, there, :] = passed.astype(BF16)
            self.out2[slot, side, here, :] = self.both(n, hops, (1 - side) * half, half).astype(BF16)

        @pl.when(n + self.lanes < self.number)
        def _():
            self.give(1, self.device(-1))
            self.give(2, self.device(1))

        self.take(n >= self.lanes, (3, 4))
        for copy in self.copies2(n, rows):
            copy.start()

    def event3(self, n, rows):
        slot = lax.rem(n, self.lanes)
        for copy in self.copies2(n, rows):
            copy.wait()
        total = self.both(n, 0, 0, rows)
        for side in range(2):
            total += self.near[slot, side, pl.ds(0, rows), :].astype(F32)

        @pl.when(n + self.slots < self.number)
        def _():
            self.give(0, self.partner())

        @pl.when(n + self.lanes < self.number)
        def _():
            self.give(3, self.device(-1))
            self.give(4, self.device(1))

        return total.astype(BF16).astype(F32)

    def block(self, n, hops, core, start, size):
        return self.gathered.at[n, self.index(self.chip + hops, core), pl.ds(start, size), :]

    def sems(self, n, kind):
        return self.ag_sem.at[lax.rem(n, self.turns), kind]

    def gathers1(self, n, rows):
        new, own = self.new.at[pl.ds(0, rows), :], self.block(n, 0, self.core, 0, rows)
        to = (self.device(1), self.device(-1), self.partner())
        return [self.hop(self.sems(n, kind), new, own, device) for kind, device in enumerate(to)] + [pltpu.make_async_copy(new, own, self.own_sem)]

    def gathers2(self, n, rows):
        copies = []
        for side in range(2):
            half = self.block(n, 2 * side - 1, self.core, side * (rows // 2), rows // 2)
            full = self.block(n, 2 * side - 1, self.core, 0, rows)
            copies.append(self.hop(self.sems(n, 3 + side), half, half, self.device(1 - 2 * side)))
            copies.append(self.hop(self.sems(n, 5 + side), full, full, self.partner()))
        return copies

    def gathers3(self, n, rows):
        opposite = self.block(n, 2, self.core, 0, rows)
        return [self.hop(self.sems(n, 7), opposite, opposite, self.partner())]

    def gather1(self, n, rows):
        for copy in self.gathers1(n, rows):
            copy.start()

    def gather2(self, n, rows):
        for copy in self.gathers1(n, rows):
            copy.wait()
        for copy in self.gathers2(n, rows):
            copy.start()

    def gather3(self, n, rows):
        for copy in self.gathers2(n, rows):
            copy.wait()
        for copy in self.gathers3(n, rows):
            copy.start()

    def gather4(self, n, rows):
        for copy in self.gathers3(n, rows):
            copy.wait()


def adam(w, m, v, g):
    m = 0.9 * m + 0.1 * g
    v = 0.95 * v + 0.05 * g * g
    w = w.astype(F32)
    return (w - 0.02 * (m * lax.rsqrt(v + 1e-8) + 0.1 * w)).astype(BF16)


def backward_kernel(chips, tile, *refs):
    a_hbm, dy_hbm, h_hbm, wg_hbm, wu_hbm, wd_hbm, mg_hbm, mu_hbm, md_hbm, vg_hbm, vu_hbm, vd_hbm, *refs = refs
    gg_hbm, gu_hbm, gd_hbm, whole_gu, whole_dn, dy0_hbm, *refs = refs
    a_tile, dy_tile, at_ref, dyt_ref, da_ref, wg_ref, wu_ref, wd_ref, z_ref, dgu_ref, m_ref, v_ref, w_ref, *refs = refs
    tile_sem, w_sem, state_sem, *pools = refs
    tokens, d = a_hbm.shape[1:]
    layers, _, ff = wg_hbm.shape
    width = chips * LANES
    blocks = ff // width
    pairs = blocks // 2
    rows = d // (CORES * chips)
    lane_blocks = d // LANES
    me = lax.axis_index("dp")
    chip, core = me // CORES, lax.rem(me, CORES)
    tiles = tokens // tile
    steps = layers * blocks
    full, small = d, d // 2

    gu = Pool(steps, chips, core, chip, pools[0:8], pools[8:13], whole_gu)
    dn = Pool(layers * (pairs + 1), chips, core, chip, pools[13:21], pools[21:26], whole_dn)

    def layer_of(j):
        return layers - 1 - j // blocks

    def block_of(j):
        j = lax.rem(j, blocks)
        return j // 2 + (pairs + 1) * lax.rem(j, 2)

    def columns(c, j):
        return strip(c * blocks * LANES + block_of(j) * LANES, LANES)

    def is_last(j):
        return lax.rem(j, blocks) == blocks - 1

    def gives_down(j):
        return (j >= 0) & (j < steps) & ((lax.rem(lax.rem(j, blocks), 2) == 1) | is_last(j))

    def down_of(j):
        return (j // blocks) * (pairs + 1) + lax.rem(j, blocks) // 2

    def for_down(j, act):
        @pl.when(gives_down(j) & ~is_last(j))
        def _():
            act(down_of(j), full)

        @pl.when(gives_down(j) & is_last(j))
        def _():
            act(down_of(j), small)

    def weight_copies(j):
        layer, slot = layer_of(j), lax.rem(j, 2)
        for c in range(chips):
            there, here = columns(c, j), pl.ds(c * LANES, LANES)
            yield pltpu.make_async_copy(wg_hbm.at[layer, :, there], wg_ref.at[slot, :, here], w_sem.at[slot, 3 * c])
            yield pltpu.make_async_copy(wu_hbm.at[layer, :, there], wu_ref.at[slot, :, here], w_sem.at[slot, 3 * c + 1])
            yield pltpu.make_async_copy(wd_hbm.at[layer, there, :], wd_ref.at[slot, here, :], w_sem.at[slot, 3 * c + 2])

    def load(src, buf, t, which):
        slot = lax.rem(t, 2)
        return pltpu.make_async_copy(src.at[strip(t * tile, tile), :], buf.at[slot], tile_sem.at[slot, which])

    def start_tile(j, t):
        load(a_hbm.at[layer_of(j)], a_tile, t, 0).start()

        @pl.when(layer_of(j) == layers - 1)
        def _():
            load(dy_hbm, dy_tile, t, 1).start()

        @pl.when(layer_of(j) < layers - 1)
        def _():
            load(dy0_hbm, dy_tile, t, 1).start()

    def wait_tile(t):
        load(dy_hbm, a_tile, t, 0).wait()
        load(dy_hbm, dy_tile, t, 1).wait()

    def gu_parts(n):
        for c in range(chips):
            for u in range(2):
                yield u * chips + c, u, pl.ds((u * chips + c) * rows, rows), columns(c, n)

    def gu_outs(n):
        for i, u, here, there in gu_parts(n):
            yield pltpu.make_async_copy(gu.sum.at[here, :], (gg_hbm, gu_hbm)[u].at[layer_of(n), :, there], gu.out_sem.at[i])

    def gu_state(n):
        layer = layer_of(n)
        for i, u, here, there in gu_parts(n):
            for k, (src, buf) in enumerate((((mg_hbm, mu_hbm)[u], m_ref), ((vg_hbm, vu_hbm)[u], v_ref))):
                yield pltpu.make_async_copy(src.at[layer, :, there], buf.at[here, :], state_sem.at[3 * i + k])
            src = (wg_hbm, wu_hbm)[u].at[layer, strip(me * rows, rows), there]
            yield pltpu.make_async_copy(src, w_ref.at[here, :], state_sem.at[3 * i + 2])

    def dn_parts(n, size):
        step = lax.rem(n, pairs + 1)
        start = step * LANES + core * (LANES // 2) if size == full else pairs * LANES * (1 - core)
        height = size // lane_blocks
        for b in range(lane_blocks):
            yield b, layers - 1 - n // (pairs + 1), start, height, pl.ds(b * height, height), pl.ds(b * LANES, LANES)

    def dn_outs(n, size):
        for b, layer, start, height, here, there in dn_parts(n, size):
            at = pl.ds(pl.multiple_of(start, LANES // 2), height)
            yield pltpu.make_async_copy(dn.sum.at[here, :], gd_hbm.at[layer, at, there], dn.out_sem.at[b])

    def dn_state(n, size):
        for b, layer, start, height, here, there in dn_parts(n, size):
            at = pl.ds(pl.multiple_of(start, LANES // 2), height)
            for k, (src, buf) in enumerate(((md_hbm, m_ref), (vd_hbm, v_ref))):
                yield pltpu.make_async_copy(src.at[layer, at, there], buf.at[here, :], state_sem.at[3 * b + k])
            at = pl.ds(pl.multiple_of(me * (d // 2) + start, LANES // 2), height)
            yield pltpu.make_async_copy(wd_hbm.at[layer, at, there], w_ref.at[here, :], state_sem.at[3 * b + 2])

    def start(copies):
        for copy in copies:
            copy.start()

    def wait(copies):
        for copy in copies:
            copy.wait()

    def gu_new(n):
        g = gu.event3(n, full)
        pl.when(n > 0)(lambda: wait(gu_outs(n - 1)))
        gu.sum[...] = g.astype(BF16)
        start(gu_outs(n))
        wait(gu_state(n))
        gu.new[...] = adam(w_ref[...], m_ref[...], v_ref[...], g)
        gu.gather1(n, full)

    def dn_new(n, size):
        g = dn.event3(n, size).T
        half, height = LANES // 2, size // lane_blocks
        if size == small:
            g = jnp.concatenate([g[:half], g[half:]], 1)
        if size == full:
            pl.when((n > 0) & (lax.rem(n, pairs + 1) > 0))(lambda: wait(dn_outs(n - 1, full)))
            pl.when((n > 0) & (lax.rem(n, pairs + 1) == 0))(lambda: wait(dn_outs(n - 1, small)))
        else:
            wait(dn_outs(n - 1, full))
        for b in range(lane_blocks):
            dn.sum[pl.ds(b * height, height), :] = g[:, b * LANES : (b + 1) * LANES].astype(BF16)
        start(dn_outs(n, size))
        wait(dn_state(n, size))
        for b in range(lane_blocks):
            here = pl.ds(b * height, height)
            dn.new[here, :] = adam(w_ref[here, :], m_ref[here, :], v_ref[here, :], g[:, b * LANES : (b + 1) * LANES])
        dn.gather1(n, size)

    def turn(buf, slot, into, part):
        for b in range(lane_blocks):
            into[pl.ds(b * LANES, LANES), part] = buf[slot, :, b * LANES : (b + 1) * LANES].T

    start_tile(0, 0)
    start(weight_copies(0))
    barrier = pltpu.get_barrier_semaphore()
    peers = (gu.partner(), gu.device(1), gu.device(-1))
    for peer in peers:
        pl.semaphore_signal(barrier, inc=1, device_id=peer, device_id_type=MESH)
    pl.semaphore_wait(barrier, len(peers))

    def first(t, _):
        part = strip(t * tile, tile)
        wait_tile(t)
        start_tile(0, lax.rem(t + 1, tiles))
        slot = lax.rem(t, 2)
        turn(a_tile, slot, at_ref, part)
        turn(dy_tile, slot, dyt_ref, part)
        da_ref[part, :] = jnp.zeros((tile, d), F32)
        return 0

    lax.fori_loop(0, tiles, first, 0)

    def compute_tile(j, t):
        slot, here = lax.rem(j, 2), lax.rem(t, 2)
        part = strip(t * tile, tile)
        wait_tile(t)
        pl.when(t + 1 < tiles)(lambda: start_tile(j, t + 1))
        a, dy = a_tile[here], dy_tile[here]
        gate = dot(a, wg_ref[slot])
        up = dot(a, wu_ref[slot])
        dz = dot(dy, wd_ref[slot], NT).astype(BF16).astype(F32)
        s = jax.nn.sigmoid(gate)
        act = s * gate
        z_ref[part, :] = (act * up).astype(BF16)
        dgu_ref[1, part, :] = (dz * act).astype(BF16)
        dgu_ref[0, part, :] = (dz * up * (s + act * (1 - s))).astype(BF16)

    def compute_down(j):
        slot = lax.rem(down_of(j), dn.slots)
        owner = lax.rem(lax.rem(j, blocks), 2)

        def part(h, _):
            g = dot(dyt_ref[...], z_ref[:, strip(h * 2 * LANES, 2 * LANES)]).astype(BF16)
            for c in range(2):
                dn.mine[slot, owner, 2 * h + c, :, :] = g[:, c * LANES : (c + 1) * LANES]
            return 0

        def last(h, _):
            g = dot(dyt_ref[...], z_ref[:, strip(h * 2 * LANES, 2 * LANES)])
            low = lax.broadcasted_iota(jnp.int32, (small, LANES), 1) < LANES // 2
            for c in range(2):
                top, bottom = g[:small, c * LANES : (c + 1) * LANES], g[small:, c * LANES : (c + 1) * LANES]
                dn.mine[slot, 0, 2 * h + c, pl.ds(0, small), :] = jnp.where(low, top, pltpu.roll(bottom, LANES // 2, 1)).astype(BF16)
                dn.mine[slot, 1, 2 * h + c, pl.ds(0, small), :] = jnp.where(low, pltpu.roll(top, LANES // 2, 1), bottom).astype(BF16)
            return 0

        @pl.when(~is_last(j))
        def _():
            lax.fori_loop(0, chips // 2, part, 0)

        @pl.when(is_last(j))
        def _():
            lax.fori_loop(0, chips // 2, last, 0)

    def compute_gate_up(j):
        slot = lax.rem(j, gu.slots)

        def part(s, _):
            u, h = s // (chips // 2), lax.rem(s, chips // 2)
            g = dot(at_ref[...], dgu_ref[u, :, strip(h * 2 * LANES, 2 * LANES)]).astype(BF16)
            for c in range(2):
                at = strip((u * chips + 2 * h + c) * rows, rows)
                for owner in range(CORES * chips):
                    gu.mine[slot, owner % CORES, owner // CORES, at, :] = g[owner * rows : (owner + 1) * rows, c * LANES : (c + 1) * LANES]
            return 0

        lax.fori_loop(0, chips, part, 0)

    def compute_da(j, t):
        slot = lax.rem(j, 2)
        part = strip(t * tile, tile)
        da_ref[part, :] += dot(dgu_ref[0, part, :], wg_ref[slot], NT) + dot(dgu_ref[1, part, :], wu_ref[slot], NT)

    def change_layer():
        size = tile // 4

        def keep(t):
            return pltpu.make_async_copy(dy_tile.at[lax.rem(t, 2)], dy0_hbm.at[strip(t * tile, tile), :], tile_sem.at[lax.rem(t, 2), 2])

        def begin(t):
            load(h_hbm, a_tile, t, 0).start()
            load(dy_hbm, dy_tile, t, 1).start()

        begin(0)

        def one(t, _):
            slot = lax.rem(t, 2)
            wait_tile(t)
            pl.when(t > 0)(lambda: keep(t - 1).wait())
            pl.when(t + 1 < tiles)(lambda: begin(t + 1))

            def piece(i, _):
                here, there = strip(i * size, size), strip(t * tile + i * size, size)
                wide = a_tile[slot, here, :].astype(F32)
                da = da_ref[there, :].astype(BF16).astype(F32)
                scale = lax.rsqrt(jnp.mean(wide * wide, -1, keepdims=True) + 1e-6)
                along = jnp.mean(da * wide, -1, keepdims=True)
                back = (da * scale - wide * (along * scale * scale * scale)).astype(BF16)
                dy_tile[slot, here, :] = dy_tile[slot, here, :] + back
                return 0

            lax.fori_loop(0, tile // size, piece, 0)
            keep(t).start()
            turn(dy_tile, slot, dyt_ref, strip(t * tile, tile))
            return 0

        lax.fori_loop(0, tiles, one, 0)
        keep(tiles - 1).wait()

    def on(j, act):
        pl.when((j >= 0) & (j < steps))(lambda: act(j))

    def step(j, _):
        busy = j < steps
        changes = is_last(j) & (layer_of(j) > 0) & busy

        @pl.when(busy)
        def _():
            wait(weight_copies(j))
            pl.when(j + 1 < steps)(lambda: start(weight_copies(j + 1)))

        def tile_step(t, _):
            pl.when(busy)(lambda: compute_tile(j, t))

            @pl.when(t == 0)
            def _():
                for_down(j - 1, dn.event2)
                for_down(j - 3, dn.gather2)

            @pl.when(t == 1)
            def _():
                on(j - 2, lambda n: gu.gather2(n, full))

            @pl.when(t == 2)
            def _():
                on(j - 1, lambda n: gu.event2(n, full))

            @pl.when(t == 3)
            def _():
                for_down(j - 2, dn_new)
                on(j - 1, lambda n: start(gu_state(n)))

            return 0

        lax.fori_loop(0, tiles, tile_step, 0)

        pl.when(busy)(lambda: compute_down(j))
        for_down(j, dn.event0)

        @pl.when(busy & (j + 1 < steps) & ~changes)
        def _():
            start_tile(j + 1, 0)

        on(j - 2, lambda n: gu.gather3(n, full))
        on(j - 3, lambda n: gu.gather4(n, full))

        @pl.when(busy)
        def _():
            compute_gate_up(j)
            gu.event0(j, full)

        for_down(j, dn.event1)
        on(j - 1, gu_new)
        for_down(j - 1, lambda n, size: start(dn_state(n, size)))

        @pl.when(busy & (layer_of(j) > 0))
        def _():
            def da_step(t, _):
                @pl.when(changes)
                def _():
                    pl.when(t == 0)(lambda: load(a_hbm.at[0], a_tile, 0, 0).start())
                    load(a_hbm.at[0], a_tile, t, 0).wait()
                    pl.when(t + 1 < tiles)(lambda: load(a_hbm.at[0], a_tile, t + 1, 0).start())

                compute_da(j, t)
                pl.when(changes)(lambda: turn(a_tile, lax.rem(t, 2), at_ref, strip(t * tile, tile)))
                return 0

            lax.fori_loop(0, tiles, da_step, 0)

        on(j, lambda n: gu.event1(n, full))
        for_down(j - 3, dn.gather3)
        for_down(j - 4, dn.gather4)

        @pl.when(changes)
        def _():
            change_layer()
            start_tile(j + 1, 0)

        return 0

    lax.fori_loop(0, steps + 4, step, 0)
    wait(gu_outs(steps - 1))
    wait(dn_outs(dn.number - 1, small))


def backward(mesh, a, dy, h, weights, m, v, tile=512):
    tokens, d = dy.shape
    layers, _, ff = weights[0].shape
    chips = mesh.shape["dp"] // CORES
    width = chips * LANES
    blocks = ff // width
    pairs = blocks // 2
    rows = d // (CORES * chips)
    assert layers == 2 and chips == 4 and blocks % 2 == 1 and blocks * width == ff and d % LANES == 0
    shape = lambda *s: jax.ShapeDtypeStruct(s, BF16)
    devices = CORES * chips
    outs = [
        shape(layers, rows, ff),
        shape(layers, rows, ff),
        shape(layers, ff // devices, d),
        shape(layers * blocks, devices, d, LANES),
        shape(layers * (pairs + 1), devices, d, LANES),
        shape(tokens, d),
    ]

    def pool(lanes, outputs):
        return [
            pltpu.VMEM((2, CORES, chips, d, LANES), BF16),
            pltpu.VMEM((2, chips, d, LANES), BF16),
            pltpu.VMEM((lanes, 2, d // 2, LANES), BF16),
            pltpu.VMEM((lanes, 2, d, LANES), BF16),
            pltpu.VMEM((lanes, 2, d // 2, LANES), BF16),
            pltpu.VMEM((lanes, 2, d, LANES), BF16),
            pltpu.VMEM((d, LANES), BF16),
            pltpu.VMEM((d, LANES), BF16),
            pltpu.SemaphoreType.DMA((2, 5, 2)),
            pltpu.SemaphoreType.REGULAR((5,)),
            pltpu.SemaphoreType.DMA((outputs,)),
            pltpu.SemaphoreType.DMA((4, 8, 2)),
            pltpu.SemaphoreType.DMA,
        ]

    return pl.pallas_call(
        functools.partial(backward_kernel, chips, tile),
        out_shape=outs,
        in_specs=[ANY] * 12,
        out_specs=[ANY] * len(outs),
        scratch_shapes=[
            pltpu.VMEM((2, tile, d), BF16),
            pltpu.VMEM((2, tile, d), BF16),
            pltpu.VMEM((d, tokens), BF16),
            pltpu.VMEM((d, tokens), BF16),
            pltpu.VMEM((tokens, d), F32),
            pltpu.VMEM((2, d, width), BF16),
            pltpu.VMEM((2, d, width), BF16),
            pltpu.VMEM((2, width, d), BF16),
            pltpu.VMEM((tokens, width), BF16),
            pltpu.VMEM((2, tokens, width), BF16),
            pltpu.VMEM((d, LANES), F32),
            pltpu.VMEM((d, LANES), F32),
            pltpu.VMEM((d, LANES), BF16),
            pltpu.SemaphoreType.DMA((2, 3)),
            pltpu.SemaphoreType.DMA((2, 3 * chips)),
            pltpu.SemaphoreType.DMA((max(6 * chips, 3 * (d // LANES)),)),
            *pool(1, 2 * chips),
            *pool(2, d // LANES),
        ],
        compiler_params=pltpu.CompilerParams(collective_id=1, has_side_effects=True, vmem_limit_bytes=VMEM_MOST),
        cost_estimate=pl.CostEstimate(flops=28 * tokens * d * ff, bytes_accessed=24 * d * ff, transcendentals=2 * tokens * ff),
        name="backward",
    )(a, dy, h, *weights, *m, *v)


def moments_kernel(m_ref, v_ref, g_ref, new_m, new_v):
    g = g_ref[...].astype(F32)
    new_m[...] = 0.9 * m_ref[...] + 0.1 * g
    new_v[...] = 0.95 * v_ref[...] + 0.05 * g * g


def moments(m, v, g, parts):
    layers, rows, cols = m.shape
    r, c = rows // parts[0], cols // parts[1]
    block = pl.BlockSpec((None, r, c), lambda l, i, j: (l, i, j))
    return pl.pallas_call(
        moments_kernel,
        grid=(layers, *parts),
        in_specs=[block] * 3,
        out_specs=[block] * 2,
        out_shape=[jax.ShapeDtypeStruct(m.shape, F32)] * 2,
        compiler_params=pltpu.CompilerParams(dimension_semantics=("arbitrary",) * 3, vmem_limit_bytes=VMEM_BYTES),
        cost_estimate=pl.CostEstimate(flops=8 * m.size, bytes_accessed=18 * m.size, transcendentals=0),
        name="moments",
    )(m, v, g)


def place_columns_kernel(x_ref, out_ref):
    blocks, devices, rows, _ = x_ref.shape
    for j in range(blocks):
        at = j // 2 + (blocks // 2 + 1) * (j % 2)
        for device in range(devices):
            out_ref[pl.ds(device * rows, rows), pl.ds(at * LANES, LANES)] = x_ref[j, device]


def place_columns(chunks, which, layers, d, ff):
    number, devices, height, _ = chunks.shape
    chips = devices // CORES
    blocks, rows = number // layers, d // devices
    x = chunks.reshape(layers, blocks, devices, 2, chips, rows, LANES)
    return pl.pallas_call(
        place_columns_kernel,
        grid=(layers, chips),
        in_specs=[pl.BlockSpec((None, blocks, devices, None, None, rows, LANES), lambda l, c: (layers - 1 - l, 0, 0, which, c, 0, 0))],
        out_specs=pl.BlockSpec((None, d, ff // chips), lambda l, c: (l, 0, c)),
        out_shape=jax.ShapeDtypeStruct((layers, d, ff), BF16),
        compiler_params=pltpu.CompilerParams(dimension_semantics=("arbitrary",) * 2, vmem_limit_bytes=VMEM_BYTES),
        cost_estimate=pl.CostEstimate(flops=0, bytes_accessed=4 * layers * d * ff, transcendentals=0),
        name="place_columns",
    )(x)


def place_rows_kernel(x_ref, out_ref):
    chunks, height, _ = x_ref.shape
    pairs, cols = chunks - 1, out_ref.shape[1]
    core = lax.rem(pl.program_id(1), CORES)
    half = LANES // 2
    for b in range(cols // LANES):
        there = pl.ds(b * LANES, LANES)
        for n in range(pairs):
            out_ref[pl.ds(pl.multiple_of(n * LANES + core * half, half), LANES), there] = x_ref[n, pl.ds(b * LANES, LANES), :]
        out_ref[pl.ds(pl.multiple_of(pairs * LANES * (1 - core), half), half), there] = x_ref[pairs, pl.ds(b * half, half), :]


def place_rows(chunks, layers, d, ff):
    number, devices, height, _ = chunks.shape
    x = chunks.reshape(layers, number // layers, devices, height, LANES)
    return pl.pallas_call(
        place_rows_kernel,
        grid=(layers, devices),
        in_specs=[pl.BlockSpec((None, number // layers, None, height, LANES), lambda l, i: (layers - 1 - l, 0, i, 0, 0))],
        out_specs=pl.BlockSpec((None, ff // devices, d), lambda l, i: (l, i, 0)),
        out_shape=jax.ShapeDtypeStruct((layers, ff, d), BF16),
        compiler_params=pltpu.CompilerParams(dimension_semantics=("arbitrary",) * 2, vmem_limit_bytes=VMEM_BYTES),
        cost_estimate=pl.CostEstimate(flops=0, bytes_accessed=4 * layers * d * ff, transcendentals=0),
        name="place_rows",
    )(x)


def solution(mesh):
    def step(x, dy, *arrays):
        weights, m, v = (arrays[i : i + 3] for i in (0, 3, 6))
        x, dy = x[0], dy[0]
        layers, d, ff = weights[0].shape
        a, h = forward(x, *weights, 0)
        *sums, columns, rows, _ = backward(mesh, a, dy, h, weights, m, v)
        new = [place_columns(columns, which, layers, d, ff) for which in range(2)] + [place_rows(rows, layers, d, ff)]
        states = [moments(*mvg, parts) for *mvg, parts in zip(m, v, sums, ((1, 3), (1, 3), (3, 1)))]
        return (*new, *(state[0] for state in states), *(state[1] for state in states))

    seq, whole, rows = P(("rep", "dp"), None, None), P(None, None, None), P(None, "dp", None)
    return jax.shard_map(
        step,
        mesh=mesh,
        in_specs=(seq, seq, whole, whole, whole) + (rows,) * 6,
        out_specs=(P("rep", None, None),) * 3 + (P("rep", "dp", None),) * 6,
        check_vma=False,
    )
```

profile of v0, /device:TPU:113, one launch (start us, length us, event | category | flops | bytes accessed | tf_op | source)
XLA Modules:
  0.0 789.6 jit_solution(16778140630576013197)
XLA Ops:
  0.6 92.8 %forward.1 = (bf16[2,2048,1152]{2,1,0:T(8,128)(2,1)}, bf16[2048,1152]{1,0:T(8,128)(2,1)}) custom-call(bf16[2048,1152]{1,0:T(8,128)(2,1)} %bitcast.7, bf16[2,1152,4608]{2,1,0:T(8,128)(2,1)} %refs_3_.1, bf16[2,1152,4608]{2,1,0:T(8,128)(2,1)} %refs_4_.1, bf16[2,4608,1152]{2,1,0:T(8,128)(2,1)} %refs_5_.1), custom_call_target="tpu_custom_call" | custom-call | flops 65229815808 | bytes 50724864 | tf_op jit(solution)/shard_map/forward/pallas_call | solution.py:74
  93.4 610.6 %backward.1 = (bf16[2,144,4608]{2,1,0:T(8,128)(2,1)}, bf16[2,144,4608]{2,1,0:T(8,128)(2,1)}, bf16[2,576,1152]{2,1,0:T(8,128)(2,1)}, bf16[18,8,1152,128]{3,2,1,0:...) custom-call(bf16[2,2048,1152]{2,1,0:T(8,128)(2,1)} %get-tuple-element.22.refs_0_, ...), custom_call_target="tpu_custom_call" | custom-call | flops 304405807104 | bytes 127401984 | tf_op jit(solution)/shard_map/backward/pallas_call | solution.py:644
  704.1 17.3 %place_columns.2 = bf16[2,1152,4608]{2,1,0:T(8,128)(2,1)} custom-call(bf16[2,9,8,2,4,144,128]{6,5,4,3,2,1,0:T(8,128)(2,1)} %bitcast.4), custom_call_target="tpu_custom_call" | custom-call | bytes 42467328 | tf_op jit(solution)/shard_map/place_columns/pallas_call | solution.py:710
  721.3 17.2 %place_columns.3 = bf16[2,1152,4608]{2,1,0:T(8,128)(2,1)} custom-call(bf16[2,9,8,2,4,144,128]{6,5,4,3,2,1,0:T(8,128)(2,1)} %bitcast.5), custom_call_target="tpu_custom_call" | custom-call | bytes 42467328 | tf_op jit(solution)/shard_map/place_columns/pallas_call | solution.py:710
  738.6 21.5 %place_rows.1 = bf16[2,4608,1152]{2,1,0:T(8,128)(2,1)} custom-call(bf16[2,5,8,1152,128]{4,3,2,1,0:T(8,128)(2,1)} %bitcast.6), custom_call_target="tpu_custom_call" | custom-call | bytes 42467328 | tf_op jit(solution)/shard_map/place_rows/pallas_call | solution.py:737
  760.0 9.8 %moments.3 = (f32[2,144,4608]{2,1,0:T(8,128)}, f32[2,144,4608]{2,1,0:T(8,128)}) custom-call(f32[2,144,4608]{2,1,0:T(8,128)} %m_ref.3, f32[2,144,4608]{2,1,0:T(8,128)} %v_ref.3, bf16[2,144,4608]{2,1,0:T(8,128)(2,1)} %get-tuple-element.26.g_ref), custom_call_target="tpu_custom_call" | custom-call | flops 10616832 | bytes 23887872 | tf_op jit(solution)/shard_map/moments/pallas_call | solution.py:685
  769.9 9.8 %moments.4 = (f32[2,144,4608]{2,1,0:T(8,128)}, f32[2,144,4608]{2,1,0:T(8,128)}) custom-call(f32[2,144,4608]{2,1,0:T(8,128)} %m_ref.4, f32[2,144,4608]{2,1,0:T(8,128)} %v_ref.4, bf16[2,144,4608]{2,1,0:T(8,128)(2,1)} %get-tuple-element.28.g_ref), custom_call_target="tpu_custom_call" | custom-call | flops 10616832 | bytes 23887872 | tf_op jit(solution)/shard_map/moments/pallas_call | solution.py:685
  779.7 9.8 %moments.5 = (f32[2,576,1152]{2,1,0:T(8,128)}, f32[2,576,1152]{2,1,0:T(8,128)}) custom-call(f32[2,576,1152]{2,1,0:T(8,128)} %m_ref.5, f32[2,576,1152]{2,1,0:T(8,128)} %v_ref.5, bf16[2,576,1152]{2,1,0:T(8,128)(2,1)} %get-tuple-element.30.g_ref), custom_call_target="tpu_custom_call" | custom-call | flops 10616832 | bytes 23887872 | tf_op jit(solution)/shard_map/moments/pallas_call | solution.py:685
where the time goes:
time: 791 us; the launch traced here: 790 us
  Pallas kernels  789 us (100%)
    pallas_call x1, Pallas kernels, backward(): pl.pallas_call(functools.partial(backward_kernel, chips, tile), out_shape...  611 us
    pallas_call x1, Pallas kernels, forward(): pl.pallas_call(functools.partial(forward_kernel, tile), grid=(ff // width...  92.8 us
    pallas_call x2, Pallas kernels, place_columns(): pl.pallas_call(place_columns_kernel, grid=(layers, chips), in_specs=[pl.B...  34.5 us
    pallas_call x3, Pallas kernels, moments(): pl.pallas_call(moments_kernel, grid=(layers, *parts), in_specs=[block] *...  29.5 us
    pallas_call x1, Pallas kernels, place_rows(): pl.pallas_call(place_rows_kernel, grid=(layers, devices), in_specs=[pl.Bl...  21.5 us

commit v1 on v0

--- a/solution.py
+++ b/solution.py
@@ -31,58 +31,85 @@
     return pl.ds(pl.multiple_of(start, size), size)
 
 
-def forward_kernel(tile, x_ref, wg_ref, wu_ref, wd_ref, a_ref, h_ref, total):
+def forward_kernel(tile, x_ref, wg_ref, wu_ref, wd_ref, a_hbm, h_hbm, a_ref, total, ends, a_sem, end_sem):
     block, blocks = pl.program_id(0), pl.num_programs(0)
     tiles = x_ref.shape[0] // tile
+
+    def keep(t):
+        rows = strip(t * tile, tile)
+        return pltpu.make_async_copy(a_ref.at[rows, :], a_hbm.at[0, rows, :], a_sem.at[t])
+
+    def finish(t):
+        slot, rows = lax.rem(t, 2), strip(t * tile, tile)
+        yield pltpu.make_async_copy(ends.at[slot, 0], h_hbm.at[rows, :], end_sem.at[slot, 0])
+        yield pltpu.make_async_copy(ends.at[slot, 1], a_hbm.at[1, rows, :], end_sem.at[slot, 1])
 
     @pl.when(block == 0)
     def _():
         def start(t, _):
             rows = strip(t * tile, tile)
-            a_ref[0, rows, :] = norm(x_ref[rows, :])
+            a_ref[rows, :] = norm(x_ref[rows, :])
             total[rows, :] = jnp.zeros((tile, total.shape[1]), F32)
+            keep(t).start()
             return 0
 
         lax.fori_loop(0, tiles, start, 0)
 
     def one(t, _):
         rows = strip(t * tile, tile)
-        a = a_ref[0, rows, :]
+        a = a_ref[rows, :]
         gate, up = dot(a, wg_ref[...]), dot(a, wu_ref[...])
         z = (jax.nn.sigmoid(gate) * gate * up).astype(BF16)
         total[rows, :] += dot(z, wd_ref[...])
+
+        @pl.when(block == blocks - 1)
+        def _():
+            slot = lax.rem(t, 2)
+            keep(t).wait()
+
+            @pl.when(t >= 2)
+            def _():
+                for copy in finish(t - 2):
+                    copy.wait()
+
+            h = x_ref[rows, :] + total[rows, :].astype(BF16)
+            ends[slot, 0] = h
+            ends[slot, 1] = norm(h)
+            for copy in finish(t):
+                copy.start()
+
         return 0
 
     lax.fori_loop(0, tiles, one, 0)
 
     @pl.when(block == blocks - 1)
     def _():
-        def end(t, _):
-            rows = strip(t * tile, tile)
-            h = x_ref[rows, :] + total[rows, :].astype(BF16)
-            h_ref[rows, :] = h
-            a_ref[1, rows, :] = norm(h)
-            return 0
-
-        lax.fori_loop(0, tiles, end, 0)
-
-
-def forward(x, wg, wu, wd, layer, width=512, tile=512):
+        for t in (tiles - 2, tiles - 1):
+            for copy in finish(t):
+                copy.wait()
+
+
+def forward(x, wg, wu, wd, layer, width=768, tile=512):
     tokens, d = x.shape
     ff = wg.shape[2]
-    whole = pl.BlockSpec((tokens, d), lambda i: (0, 0))
     return pl.pallas_call(
         functools.partial(forward_kernel, tile),
         grid=(ff // width,),
         out_shape=[jax.ShapeDtypeStruct((2, tokens, d), BF16), jax.ShapeDtypeStruct((tokens, d), BF16)],
         in_specs=[
-            whole,
+            pl.BlockSpec((tokens, d), lambda i: (0, 0)),
             pl.BlockSpec((None, d, width), lambda i: (layer, 0, i)),
             pl.BlockSpec((None, d, width), lambda i: (layer, 0, i)),
             pl.BlockSpec((None, width, d), lambda i: (layer, i, 0)),
         ],
-        out_specs=[pl.BlockSpec((2, tokens, d), lambda i: (0, 0, 0)), whole],
-        scratch_shapes=[pltpu.VMEM((tokens, d), F32)],
+        out_specs=[ANY, ANY],
+        scratch_shapes=[
+            pltpu.VMEM((tokens, d), BF16),
+            pltpu.VMEM((tokens, d), F32),
+            pltpu.VMEM((2, 2, tile, d), BF16),
+            pltpu.SemaphoreType.DMA((tokens // tile,)),
+            pltpu.SemaphoreType.DMA((2, 2)),
+        ],
         compiler_params=pltpu.CompilerParams(dimension_semantics=("arbitrary",), vmem_limit_bytes=VMEM_BYTES),
         cost_estimate=pl.CostEstimate(flops=6 * tokens * d * ff, bytes_accessed=6 * d * ff + 8 * tokens * d, transcendentals=tokens * ff),
         name="forward",
@@ -368,14 +395,14 @@
         for copy in copies:
             copy.wait()
 
-    def gu_new(n):
-        g = gu.event3(n, full)
+    def gu_new(n, rows):
+        g = gu.event3(n, rows)
         pl.when(n > 0)(lambda: wait(gu_outs(n - 1)))
         gu.sum[...] = g.astype(BF16)
         start(gu_outs(n))
         wait(gu_state(n))
         gu.new[...] = adam(w_ref[...], m_ref[...], v_ref[...], g)
-        gu.gather1(n, full)
+        gu.gather1(n, rows)
 
     def dn_new(n, size):
         g = dn.event3(n, size).T
@@ -408,18 +435,6 @@
         pl.semaphore_signal(barrier, inc=1, device_id=peer, device_id_type=MESH)
     pl.semaphore_wait(barrier, len(peers))
 
-    def first(t, _):
-        part = strip(t * tile, tile)
-        wait_tile(t)
-        start_tile(0, lax.rem(t + 1, tiles))
-        slot = lax.rem(t, 2)
-        turn(a_tile, slot, at_ref, part)
-        turn(dy_tile, slot, dyt_ref, part)
-        da_ref[part, :] = jnp.zeros((tile, d), F32)
-        return 0
-
-    lax.fori_loop(0, tiles, first, 0)
-
     def compute_tile(j, t):
         slot, here = lax.rem(j, 2), lax.rem(t, 2)
         part = strip(t * tile, tile)
@@ -435,46 +450,38 @@
         dgu_ref[1, part, :] = (dz * act).astype(BF16)
         dgu_ref[0, part, :] = (dz * up * (s + act * (1 - s))).astype(BF16)
 
-    def compute_down(j):
+        @pl.when(j == 0)
+        def _():
+            turn(a_tile, here, at_ref, part)
+            turn(dy_tile, here, dyt_ref, part)
+            da_ref[part, :] = jnp.zeros((tile, d), F32)
+
+    def compute_gate_up(j, s):
+        slot, u, h = lax.rem(j, gu.slots), s // (chips // 2), lax.rem(s, chips // 2)
+        g = dot(at_ref[...], dgu_ref[u, :, strip(h * 2 * LANES, 2 * LANES)]).astype(BF16)
+        for c in range(2):
+            at = strip((u * chips + 2 * h + c) * rows, rows)
+            for owner in range(CORES * chips):
+                gu.mine[slot, owner % CORES, owner // CORES, at, :] = g[owner * rows : (owner + 1) * rows, c * LANES : (c + 1) * LANES]
+
+    def compute_down(j, h):
         slot = lax.rem(down_of(j), dn.slots)
         owner = lax.rem(lax.rem(j, blocks), 2)
 
-        def part(h, _):
+        @pl.when(~is_last(j))
+        def _():
             g = dot(dyt_ref[...], z_ref[:, strip(h * 2 * LANES, 2 * LANES)]).astype(BF16)
             for c in range(2):
                 dn.mine[slot, owner, 2 * h + c, :, :] = g[:, c * LANES : (c + 1) * LANES]
-            return 0
-
-        def last(h, _):
+
+        @pl.when(is_last(j))
+        def _():
             g = dot(dyt_ref[...], z_ref[:, strip(h * 2 * LANES, 2 * LANES)])
             low = lax.broadcasted_iota(jnp.int32, (small, LANES), 1) < LANES // 2
             for c in range(2):
                 top, bottom = g[:small, c * LANES : (c + 1) * LANES], g[small:, c * LANES : (c + 1) * LANES]
                 dn.mine[slot, 0, 2 * h + c, pl.ds(0, small), :] = jnp.where(low, top, pltpu.roll(bottom, LANES // 2, 1)).astype(BF16)
                 dn.mine[slot, 1, 2 * h + c, pl.ds(0, small), :] = jnp.where(low, pltpu.roll(top, LANES // 2, 1), bottom).astype(BF16)
-            return 0
-
-        @pl.when(~is_last(j))
-        def _():
-            lax.fori_loop(0, chips // 2, part, 0)
-
-        @pl.when(is_last(j))
-        def _():
-            lax.fori_loop(0, chips // 2, last, 0)
-
-    def compute_gate_up(j):
-        slot = lax.rem(j, gu.slots)
-
-        def part(s, _):
-            u, h = s // (chips // 2), lax.rem(s, chips // 2)
-            g = dot(at_ref[...], dgu_ref[u, :, strip(h * 2 * LANES, 2 * LANES)]).astype(BF16)
-            for c in range(2):
-                at = strip((u * chips + 2 * h + c) * rows, rows)
-                for owner in range(CORES * chips):
-                    gu.mine[slot, owner % CORES, owner // CORES, at, :] = g[owner * rows : (owner + 1) * rows, c * LANES : (c + 1) * LANES]
-            return 0
-
-        lax.fori_loop(0, chips, part, 0)
 
     def compute_da(j, t):
         slot = lax.rem(j, 2)
@@ -518,79 +525,64 @@
         keep(tiles - 1).wait()
 
     def on(j, act):
-        pl.when((j >= 0) & (j < steps))(lambda: act(j))
+        pl.when((j >= 0) & (j < steps))(lambda: act(j, full))
+
+    events = {
+        "tile": {0: [(on, gu.event2, 1)], 1: [(for_down, dn.gather3, 3)], 3: [(on, gu.gather2, 2)]},
+        "gate_up": {
+            0: [(for_down, dn.event2, 1)],
+            1: [(on, gu.gather4, 3), (for_down, dn.gather2, 2)],
+            2: [(on, lambda n, _: start(gu_state(n)), 1)],
+            3: [(on, gu.event0, 0)],
+        },
+        "down": {1: [(for_down, dn.event0, 0), (on, gu.event1, 0)]},
+        "da": {
+            0: [(for_down, dn.gather4, 3), (on, gu_new, 1), (for_down, lambda n, size: start(dn_state(n, size)), 1)],
+            2: [(on, gu.gather3, 2), (for_down, dn.event1, 0)],
+            3: [(for_down, dn_new, 1)],
+        },
+    }
+    longest = max(ago for part in events.values() for these in part.values() for _, _, ago in these)
 
     def step(j, _):
         busy = j < steps
-        changes = is_last(j) & (layer_of(j) > 0) & busy
+        lower = layer_of(j) > 0
+        changes = is_last(j) & lower & busy
 
         @pl.when(busy)
         def _():
             wait(weight_copies(j))
             pl.when(j + 1 < steps)(lambda: start(weight_copies(j + 1)))
 
-        def tile_step(t, _):
-            pl.when(busy)(lambda: compute_tile(j, t))
-
-            @pl.when(t == 0)
+        def parts(name, number, active, compute):
+            def one(t, _):
+                pl.when(active)(lambda: compute(j, t))
+                for at, these in events[name].items():
+
+                    @pl.when(t == at)
+                    def _():
+                        for stream, act, ago in these:
+                            stream(j - ago, act)
+
+                return 0
+
+            lax.fori_loop(0, number, one, 0)
+
+        def da_tile(j, t):
+            @pl.when(changes)
             def _():
-                for_down(j - 1, dn.event2)
-                for_down(j - 3, dn.gather2)
-
-            @pl.when(t == 1)
-            def _():
-                on(j - 2, lambda n: gu.gather2(n, full))
-
-            @pl.when(t == 2)
-            def _():
-                on(j - 1, lambda n: gu.event2(n, full))
-
-            @pl.when(t == 3)
-            def _():
-                for_down(j - 2, dn_new)
-                on(j - 1, lambda n: start(gu_state(n)))
-
-            return 0
-
-        lax.fori_loop(0, tiles, tile_step, 0)
-
-        pl.when(busy)(lambda: compute_down(j))
-        for_down(j, dn.event0)
-
-        @pl.when(busy & (j + 1 < steps) & ~changes)
-        def _():
-            start_tile(j + 1, 0)
-
-        on(j - 2, lambda n: gu.gather3(n, full))
-        on(j - 3, lambda n: gu.gather4(n, full))
-
-        @pl.when(busy)
-        def _():
-            compute_gate_up(j)
-            gu.event0(j, full)
-
-        for_down(j, dn.event1)
-        on(j - 1, gu_new)
-        for_down(j - 1, lambda n, size: start(dn_state(n, size)))
-
-        @pl.when(busy & (layer_of(j) > 0))
-        def _():
-            def da_step(t, _):
-                @pl.when(changes)
-                def _():
-                    pl.when(t == 0)(lambda: load(a_hbm.at[0], a_tile, 0, 0).start())
-                    load(a_hbm.at[0], a_tile, t, 0).wait()
-                    pl.when(t + 1 < tiles)(lambda: load(a_hbm.at[0], a_tile, t + 1, 0).start())
-
-                compute_da(j, t)
-                pl.when(changes)(lambda: turn(a_tile, lax.rem(t, 2), at_ref, strip(t * tile, tile)))
-                return 0
-
-            lax.fori_loop(0, tiles, da_step, 0)
-
-        on(j, lambda n: gu.event1(n, full))
-        for_down(j - 3, dn.gather3)
-        for_down(j - 4, dn.gather4)
+                pl.when(t == 0)(lambda: load(a_hbm.at[0], a_tile, 0, 0).start())
+                load(a_hbm.at[0], a_tile, t, 0).wait()
+                pl.when(t + 1 < tiles)(lambda: load(a_hbm.at[0], a_tile, t + 1, 0).start())
+
+            compute_da(j, t)
+            pl.when(changes)(lambda: turn(a_tile, lax.rem(t, 2), at_ref, strip(t * tile, tile)))
+
+        parts("tile", tiles, busy, compute_tile)
+        pl.when(busy & (j + 1 < steps) & ~changes)(lambda: start_tile(j + 1, 0))
+        parts("gate_up", chips, busy, compute_gate_up)
+        parts("down", chips // 2, busy, compute_down)
+        parts("da", tiles, busy & lower, da_tile)
 
         @pl.when(changes)
         def _():
@@ -599,7 +591,7 @@
 
         return 0
 
-    lax.fori_loop(0, steps + 4, step, 0)
+    lax.fori_loop(0, steps + longest, step, 0)
     wait(gu_outs(steps - 1))
     wait(dn_outs(dn.number - 1, small))
 
@@ -672,49 +664,56 @@
     )(a, dy, h, *weights, *m, *v)
 
 
-def moments_kernel(m_ref, v_ref, g_ref, new_m, new_v):
-    g = g_ref[...].astype(F32)
-    new_m[...] = 0.9 * m_ref[...] + 0.1 * g
-    new_v[...] = 0.95 * v_ref[...] + 0.05 * g * g
+def moments_kernel(*refs):
+    number = len(refs) // 5
+    for i in range(number):
+        m_ref, v_ref, g_ref, new_m, new_v = refs[i::number]
+        g = g_ref[...].astype(F32)
+        new_m[...] = 0.9 * m_ref[...] + 0.1 * g
+        new_v[...] = 0.95 * v_ref[...] + 0.05 * g * g
 
 
 def moments(m, v, g, parts):
-    layers, rows, cols = m.shape
-    r, c = rows // parts[0], cols // parts[1]
-    block = pl.BlockSpec((None, r, c), lambda l, i, j: (l, i, j))
-    return pl.pallas_call(
+    blocks = []
+    for one, (r, c) in zip(m, parts):
+        blocks.append(pl.BlockSpec((None, one.shape[1] // r, one.shape[2] // c), (lambda l, i: (l, i, 0)) if r > 1 else (lambda l, i: (l, 0, i))))
+    size = sum(one.size for one in m)
+    new = pl.pallas_call(
         moments_kernel,
-        grid=(layers, *parts),
-        in_specs=[block] * 3,
-        out_specs=[block] * 2,
-        out_shape=[jax.ShapeDtypeStruct(m.shape, F32)] * 2,
-        compiler_params=pltpu.CompilerParams(dimension_semantics=("arbitrary",) * 3, vmem_limit_bytes=VMEM_BYTES),
-        cost_estimate=pl.CostEstimate(flops=8 * m.size, bytes_accessed=18 * m.size, transcendentals=0),
+        grid=(m[0].shape[0], max(parts[0])),
+        in_specs=blocks * 3,
+        out_specs=blocks * 2,
+        out_shape=[jax.ShapeDtypeStruct(one.shape, F32) for one in m] * 2,
+        compiler_params=pltpu.CompilerParams(dimension_semantics=("arbitrary",) * 2, vmem_limit_bytes=VMEM_BYTES),
+        cost_estimate=pl.CostEstimate(flops=8 * size, bytes_accessed=18 * size, transcendentals=0),
         name="moments",
-    )(m, v, g)
-
-
-def place_columns_kernel(x_ref, out_ref):
-    blocks, devices, rows, _ = x_ref.shape
+    )(*m, *v, *g)
+    return new
+
+
+def place_columns_kernel(x_ref, gate_ref, up_ref):
+    blocks, devices, _, rows, _ = x_ref.shape
     for j in range(blocks):
         at = j // 2 + (blocks // 2 + 1) * (j % 2)
         for device in range(devices):
-            out_ref[pl.ds(device * rows, rows), pl.ds(at * LANES, LANES)] = x_ref[j, device]
-
-
-def place_columns(chunks, which, layers, d, ff):
+            for u, out_ref in enumerate((gate_ref, up_ref)):
+                out_ref[pl.ds(device * rows, rows), pl.ds(at * LANES, LANES)] = x_ref[j, device, u]
+
+
+def place_columns(chunks, layers, d, ff):
     number, devices, height, _ = chunks.shape
     chips = devices // CORES
     blocks, rows = number // layers, d // devices
     x = chunks.reshape(layers, blocks, devices, 2, chips, rows, LANES)
+    out = pl.BlockSpec((None, d // 2, ff // chips), lambda l, c, h: (l, h, c))
     return pl.pallas_call(
         place_columns_kernel,
-        grid=(layers, chips),
-        in_specs=[pl.BlockSpec((None, blocks, devices, None, None, rows, LANES), lambda l, c: (layers - 1 - l, 0, 0, which, c, 0, 0))],
-        out_specs=pl.BlockSpec((None, d, ff // chips), lambda l, c: (l, 0, c)),
-        out_shape=jax.ShapeDtypeStruct((layers, d, ff), BF16),
-        compiler_params=pltpu.CompilerParams(dimension_semantics=("arbitrary",) * 2, vmem_limit_bytes=VMEM_BYTES),
-        cost_estimate=pl.CostEstimate(flops=0, bytes_accessed=4 * layers * d * ff, transcendentals=0),
+        grid=(layers, chips, 2),
+        in_specs=[pl.BlockSpec((None, blocks, devices // 2, 2, None, rows, LANES), lambda l, c, h: (layers - 1 - l, 0, h, 0, c, 0, 0))],
+        out_specs=[out, out],
+        out_shape=[jax.ShapeDtypeStruct((layers, d, ff), BF16)] * 2,
+        compiler_params=pltpu.CompilerParams(dimension_semantics=("arbitrary",) * 3, vmem_limit_bytes=VMEM_BYTES),
+        cost_estimate=pl.CostEstimate(flops=0, bytes_accessed=8 * layers * d * ff, transcendentals=0),
         name="place_columns",
     )(x)
 
@@ -753,9 +752,9 @@
         layers, d, ff = weights[0].shape
         a, h = forward(x, *weights, 0)
         *sums, columns, rows, _ = backward(mesh, a, dy, h, weights, m, v)
-        new = [place_columns(columns, which, layers, d, ff) for which in range(2)] + [place_rows(rows, layers, d, ff)]
-        states = [moments(*mvg, parts) for *mvg, parts in zip(m, v, sums, ((1, 3), (1, 3), (3, 1)))]
-        return (*new, *(state[0] for state in states), *(state[1] for state in states))
+        new = (*place_columns(columns, layers, d, ff), place_rows(rows, layers, d, ff))
+        states = moments(m, v, sums, ((1, 9), (1, 9), (9, 1)))
+        return (*new, *states)
 
     seq, whole, rows = P(("rep", "dp"), None, None), P(None, None, None), P(None, "dp", None)
     return jax.shard_map(

time: 791 us -> 740 us (0.936)
  Pallas kernels: 789 us -> 738 us
    pallas_call x1, Pallas kernels: 611 us -> 566 us  [backward(): pl.pallas_call(functools.partial(backward_kernel, chips, tile), out_shape...]
    pallas_call x5 -> x2, Pallas kernels: 64 us -> 62.5 us  [the longest x1 34.1 us: place_columns(): pl.pallas_call(place_columns_kernel, grid=(layers, chips, 2), in_specs=[p...]
where the time goes in v1:
time: 740 us; the launch traced here: 739 us
  Pallas kernels  738 us (100%)
    pallas_call x1, Pallas kernels, backward(): pl.pallas_call(functools.partial(backward_kernel, chips, tile), out_shape...  566 us
    pallas_call x1, Pallas kernels, forward(): pl.pallas_call(functools.partial(forward_kernel, tile), grid=(ff // width...  87.3 us
    pallas_call x1, Pallas kernels, place_columns(): pl.pallas_call(place_columns_kernel, grid=(layers, chips, 2), in_specs=[p...  34.1 us
    pallas_call x1, Pallas kernels, moments(): pl.pallas_call(moments_kernel, grid=(m[0].shape[0], max(parts[0])), in_sp...  28.5 us
    pallas_call x1, Pallas kernels, place_rows(): pl.pallas_call(place_rows_kernel, grid=(layers, devices), in_specs=[pl.Bl...  21.5 us

profile of v1, /device:TPU:113, one launch (start us, length us, event | category | flops | bytes accessed | tf_op | source)
XLA Modules:
  0.0 738.5 jit_solution(18289836886454598955)
XLA Ops:
  0.6 87.3 %forward.1 = (bf16[2,2048,1152]{2,1,0:T(8,128)(2,1)}, bf16[2048,1152]{1,0:T(8,128)(2,1)}) custom-call(bf16[2048,1152]{1,0:T(8,128)(2,1)} %bitcast.6, bf16[2,1152,4608]{2,1,0:T(8,128)(2,1)} %refs_3_.2, bf16[2,1152,4608]{2,1,0:T(8,128)(2,1)} %refs_4_.2, bf16[2,4608,1152]{2,1,0:T(8,128)(2,1)} %refs_5_.2), custom_call_target="tpu_custom_call" | custom-call | flops 65229815808 | bytes 50724864 | tf_op jit(solution)/shard_map/forward/pallas_call | solution.py:95
  88.0 566.4 %backward.1 = (bf16[2,144,4608]{2,1,0:T(8,128)(2,1)}, bf16[2,144,4608]{2,1,0:T(8,128)(2,1)}, bf16[2,576,1152]{2,1,0:T(8,128)(2,1)}, bf16[18,8,1152,128]{3,2,1,0:...) custom-call(bf16[2,2048,1152]{2,1,0:T(8,128)(2,1)} %get-tuple-element.24.refs_0_, ...), custom_call_target="tpu_custom_call" | custom-call | flops 304405807104 | bytes 127401984 | tf_op jit(solution)/shard_map/backward/pallas_call | solution.py:636
  654.4 21.5 %place_rows.1 = bf16[2,4608,1152]{2,1,0:T(8,128)(2,1)} custom-call(bf16[2,5,8,1152,128]{4,3,2,1,0:T(8,128)(2,1)} %bitcast.5), custom_call_target="tpu_custom_call" | custom-call | bytes 42467328 | tf_op jit(solution)/shard_map/place_rows/pallas_call | solution.py:736
  675.8 34.1 %place_columns.1 = (bf16[2,1152,4608]{2,1,0:T(8,128)(2,1)}, bf16[2,1152,4608]{2,1,0:T(8,128)(2,1)}) custom-call(bf16[2,9,8,2,4,144,128]{6,5,4,3,2,1,0:T(8,128)(2,1)} %bitcast.4), custom_call_target="tpu_custom_call" | custom-call | bytes 84934656 | tf_op jit(solution)/shard_map/place_columns/pallas_call | solution.py:709
  709.9 28.5 %moments.1 = (f32[2,144,4608]{2,1,0:T(8,128)}, f32[2,144,4608]{2,1,0:T(8,128)}, f32[2,576,1152]{2,1,0:T(8,128)}, f32[2,144,4608]{2,1,0:T(8,128)}, f32[2,144,4608]{2,1,0:T(8,128)}, /*index=5*/f32[2,576,1152]{2,1,0:T(8,128)}) custom-call(f32[2,144,4608]{2,1,0:T(8,128)} %refs_0_.1, f32[2,144,4608]{2,1,0:T(8,128)} %refs_1_.1, f32[2,576,1152]{2,1,0:T(8,128)} %refs_2_.1, ...), custom_call_target="tpu_custom_call" | custom-call | flops 31850496 | bytes 71663616 | tf_op jit(solution)/shard_map/moments/pallas_call | solution.py:681

commit v2 on v1

--- a/solution.py
+++ b/solution.py
@@ -16,6 +16,7 @@
 CORES = 2
 VMEM_BYTES = 62 << 20
 VMEM_MOST = 67_043_328
+COPY_FLOPS = 64
 
 
 def dot(a, b, dims=NN):
@@ -276,9 +277,9 @@
 
 def backward_kernel(chips, tile, *refs):
     a_hbm, dy_hbm, h_hbm, wg_hbm, wu_hbm, wd_hbm, mg_hbm, mu_hbm, md_hbm, vg_hbm, vu_hbm, vd_hbm, *refs = refs
-    gg_hbm, gu_hbm, gd_hbm, whole_gu, whole_dn, dy0_hbm, *refs = refs
+    gg_hbm, gu_hbm, gd_hbm, whole_gu, whole_dn, own_hbm, dy0_hbm, *refs = refs
     a_tile, dy_tile, at_ref, dyt_ref, da_ref, wg_ref, wu_ref, wd_ref, z_ref, dgu_ref, m_ref, v_ref, w_ref, *refs = refs
-    tile_sem, w_sem, state_sem, *pools = refs
+    tile_sem, w_sem, state_sem, rows_sem, *pools = refs
     tokens, d = a_hbm.shape[1:]
     layers, _, ff = wg_hbm.shape
     width = chips * LANES
@@ -378,6 +379,11 @@
         for b, layer, start, height, here, there in dn_parts(n, size):
             at = pl.ds(pl.multiple_of(start, LANES // 2), height)
             yield pltpu.make_async_copy(dn.sum.at[here, :], gd_hbm.at[layer, at, there], dn.out_sem.at[b])
+
+    def own_outs(n, size):
+        for b, _, start, height, here, there in dn_parts(n, size):
+            at = pl.ds(pl.multiple_of(start, LANES // 2), height)
+            yield pltpu.make_async_copy(dn.new.at[here, :], own_hbm.at[at, there], rows_sem.at[b])
 
     def dn_state(n, size):
         for b, layer, start, height, here, there in dn_parts(n, size):
@@ -418,10 +424,13 @@
             dn.sum[pl.ds(b * height, height), :] = g[:, b * LANES : (b + 1) * LANES].astype(BF16)
         start(dn_outs(n, size))
         wait(dn_state(n, size))
+        upper = n < (layers - 1) * (pairs + 1)
+        pl.when(n > (layers - 1) * (pairs + 1))(lambda: wait(own_outs(n - 1, full)))
         for b in range(lane_blocks):
             here = pl.ds(b * height, height)
             dn.new[here, :] = adam(w_ref[here, :], m_ref[here, :], v_ref[here, :], g[:, b * LANES : (b + 1) * LANES])
-        dn.gather1(n, size)
+        pl.when(upper)(lambda: dn.gather1(n, size))
+        pl.when(~upper)(lambda: start(own_outs(n, size)))
 
     def turn(buf, slot, into, part):
         for b in range(lane_blocks):
@@ -527,19 +536,25 @@
     def on(j, act):
         pl.when((j >= 0) & (j < steps))(lambda: act(j, full))
 
+    def upper_down(j, act):
+        pl.when(j < (layers - 1) * blocks)(lambda: for_down(j, act))
+
     events = {
-        "tile": {0: [(on, gu.event2, 1)], 1: [(for_down, dn.gather3, 3)], 3: [(on, gu.gather2, 2)]},
+        "tile": {
+            0: [(on, gu.gather4, 4), (upper_down, dn.gather2, 3)],
+            1: [(on, gu.event2, 1)],
+            2: [(for_down, dn.event1, 1)],
+        },
         "gate_up": {
-            0: [(for_down, dn.event2, 1)],
-            1: [(on, gu.gather4, 3), (for_down, dn.gather2, 2)],
-            2: [(on, lambda n, _: start(gu_state(n)), 1)],
-            3: [(on, gu.event0, 0)],
+            0: [(on, gu.gather2, 2)],
+            2: [(for_down, dn_new, 2)],
+            3: [(on, gu.event0, 0), (on, lambda n, _: start(gu_state(n)), 1)],
         },
-        "down": {1: [(for_down, dn.event0, 0), (on, gu.event1, 0)]},
+        "down": {1: [(for_down, dn.event0, 0), (upper_down, dn.gather3, 3), (on, gu.event1, 0)]},
         "da": {
-            0: [(for_down, dn.gather4, 3), (on, gu_new, 1), (for_down, lambda n, size: start(dn_state(n, size)), 1)],
-            2: [(on, gu.gather3, 2), (for_down, dn.event1, 0)],
-            3: [(for_down, dn_new, 1)],
+            0: [(on, gu.gather3, 3), (on, gu_new, 1)],
+            1: [(upper_down, dn.gather4, 3), (for_down, lambda n, size: start(dn_state(n, size)), 1)],
+            2: [(for_down, dn.event2, 1)],
         },
     }
     longest = max(ago for part in events.values() for these in part.values() for _, _, ago in these)
@@ -594,6 +609,7 @@
     lax.fori_loop(0, steps + longest, step, 0)
     wait(gu_outs(steps - 1))
     wait(dn_outs(dn.number - 1, small))
+    wait(own_outs(dn.number - 1, small))
 
 
 def backward(mesh, a, dy, h, weights, m, v, tile=512):
@@ -612,7 +628,8 @@
         shape(layers, rows, ff),
         shape(layers, ff // devices, d),
         shape(layers * blocks, devices, d, LANES),
-        shape(layers * (pairs + 1), devices, d, LANES),
+        shape((layers - 1) * (pairs + 1), devices, d, LANES),
+        shape(ff // devices, d),
         shape(tokens, d),
     ]
 
@@ -655,6 +672,7 @@
             pltpu.SemaphoreType.DMA((2, 3)),
             pltpu.SemaphoreType.DMA((2, 3 * chips)),
             pltpu.SemaphoreType.DMA((max(6 * chips, 3 * (d // LANES)),)),
+            pltpu.SemaphoreType.DMA((d // LANES,)),
             *pool(1, 2 * chips),
             *pool(2, d // LANES),
         ],
@@ -664,97 +682,280 @@
     )(a, dy, h, *weights, *m, *v)
 
 
-def moments_kernel(*refs):
-    number = len(refs) // 5
-    for i in range(number):
-        m_ref, v_ref, g_ref, new_m, new_v = refs[i::number]
-        g = g_ref[...].astype(F32)
-        new_m[...] = 0.9 * m_ref[...] + 0.1 * g
-        new_v[...] = 0.95 * v_ref[...] + 0.05 * g * g
-
-
-def moments(m, v, g, parts):
-    blocks = []
-    for one, (r, c) in zip(m, parts):
-        blocks.append(pl.BlockSpec((None, one.shape[1] // r, one.shape[2] // c), (lambda l, i: (l, i, 0)) if r > 1 else (lambda l, i: (l, 0, i))))
+class Ring:
+    def __init__(self, units, slots, loads, stores, work):
+        self.units, self.slots, self.loads, self.stores, self.work = units, slots, loads, stores, work
+
+    def begin(self):
+        for unit in range(self.slots):
+            for copy in self.loads(unit, unit):
+                copy.start()
+
+    def run(self):
+        def one(unit, _):
+            slot = lax.rem(unit, self.slots)
+            for copy in self.loads(unit, slot):
+                copy.wait()
+
+            @pl.when(unit >= self.slots)
+            def _():
+                for copy in self.stores(unit - self.slots, slot):
+                    copy.wait()
+
+            self.work(unit, slot)
+            for copy in self.stores(unit, slot):
+                copy.start()
+
+            @pl.when(unit + self.slots < self.units)
+            def _():
+                for copy in self.loads(unit + self.slots, slot):
+                    copy.start()
+
+            return 0
+
+        lax.fori_loop(0, self.units, one, 0)
+
+    def end(self):
+        for unit in range(self.units - self.slots, self.units):
+            for copy in self.stores(unit, unit % self.slots):
+                copy.wait()
+
+
+def place_columns_kernel(layers, slots, x_hbm, gate_hbm, up_hbm, c_in, c_out, sem):
+    _, blocks, devices, _, chips, rows, _ = x_hbm.shape
+    wide, some = blocks * LANES, c_in.shape[2]
+    turns = devices // some
+
+    def place(unit):
+        return unit // (chips * turns), lax.rem(unit, chips * turns) // turns, lax.rem(unit, turns) * some
+
+    def loads(unit, slot):
+        layer, chip, owners = place(unit)
+        return [pltpu.make_async_copy(x_hbm.at[layers - 1 - layer, :, pl.ds(owners, some), :, chip], c_in.at[slot], sem.at[slot, 0])]
+
+    def stores(unit, slot):
+        layer, chip, owners = place(unit)
+        at = layer, strip(owners * rows, some * rows), strip(chip * wide, wide)
+        return [pltpu.make_async_copy(c_out.at[slot, u], out.at[at], sem.at[slot, 1 + u]) for u, out in enumerate((gate_hbm, up_hbm))]
+
+    def work(unit, slot):
+        for j in range(blocks):
+            at = pl.ds((j // 2 + (blocks // 2 + 1) * (j % 2)) * LANES, LANES)
+            for owner in range(some):
+                for u in range(2):
+                    c_out[slot, u, pl.ds(owner * rows, rows), at] = c_in[slot, j, owner, u]
+
+    ring = Ring(layers * chips * turns, slots, loads, stores, work)
+    ring.begin()
+    ring.run()
+    ring.end()
+
+
+def place_columns(chunks, layers, d, ff, slots=4, some=2):
+    devices = chunks.shape[1]
+    chips, rows = devices // CORES, d // devices
+    x = chunks.reshape(layers, -1, devices, 2, chips, rows, LANES)
+    return pl.pallas_call(
+        functools.partial(place_columns_kernel, layers, slots),
+        in_specs=[ANY],
+        out_specs=[ANY] * 2,
+        out_shape=[jax.ShapeDtypeStruct((layers, d, ff), BF16)] * 2,
+        scratch_shapes=[
+            pltpu.VMEM((slots, x.shape[1], some, 2, rows, LANES), BF16),
+            pltpu.VMEM((slots, 2, some * rows, ff // chips), BF16),
+            pltpu.SemaphoreType.DMA((slots, 3)),
+        ],
+        compiler_params=pltpu.CompilerParams(vmem_limit_bytes=VMEM_BYTES),
+        cost_estimate=pl.CostEstimate(flops=COPY_FLOPS * 8 * layers * d * ff, bytes_accessed=8 * layers * d * ff, transcendentals=0),
+        name="place_columns",
+    )(x)
+
+
+def moments_kernel(layers, parts, slots, *refs):
+    states, news, s_in, g_in, s_out, sem = refs[:9], refs[9:15], refs[15:18], refs[18:21], refs[21:24], refs[24]
+
+    def at(i, unit):
+        layer, part = unit // parts, lax.rem(unit, parts)
+        _, r, c = states[i].shape
+        return (layer, strip(part * (r // parts), r // parts), slice(None)) if i == 2 else (layer, slice(None), strip(part * (c // parts), c // parts))
+
+    def loads(unit, slot):
+        copies = []
+        for i in range(3):
+            for k in range(2):
+                copies.append(pltpu.make_async_copy(states[3 * k + i].at[at(i, unit)], s_in[i].at[slot, k], sem.at[slot, 5 * i + k]))
+            copies.append(pltpu.make_async_copy(states[6 + i].at[at(i, unit)], g_in[i].at[slot], sem.at[slot, 5 * i + 2]))
+        return copies
+
+    def stores(unit, slot):
+        return [
+            pltpu.make_async_copy(s_out[i].at[slot, k], news[3 * k + i].at[at(i, unit)], sem.at[slot, 5 * i + 3 + k]) for i in range(3) for k in range(2)
+        ]
+
+    def work(unit, slot):
+        for i in range(3):
+            g = g_in[i][slot].astype(F32)
+            s_out[i][slot, 0] = 0.9 * s_in[i][slot, 0] + 0.1 * g
+            s_out[i][slot, 1] = 0.95 * s_in[i][slot, 1] + 0.05 * g * g
+
+    ring = Ring(layers * parts, slots, loads, stores, work)
+    ring.begin()
+    ring.run()
+    ring.end()
+
+
+def moments(m, v, g, parts=9, slots=4):
+    layers = m[0].shape[0]
+    shapes = [(one.shape[1], one.shape[2] // parts) for one in m[:2]] + [(m[2].shape[1] // parts, m[2].shape[2])]
     size = sum(one.size for one in m)
-    new = pl.pallas_call(
-        moments_kernel,
-        grid=(m[0].shape[0], max(parts[0])),
-        in_specs=blocks * 3,
-        out_specs=blocks * 2,
+    return pl.pallas_call(
+        functools.partial(moments_kernel, layers, parts, slots),
+        in_specs=[ANY] * 9,
+        out_specs=[ANY] * 6,
         out_shape=[jax.ShapeDtypeStruct(one.shape, F32) for one in m] * 2,
-        compiler_params=pltpu.CompilerParams(dimension_semantics=("arbitrary",) * 2, vmem_limit_bytes=VMEM_BYTES),
-        cost_estimate=pl.CostEstimate(flops=8 * size, bytes_accessed=18 * size, transcendentals=0),
+        scratch_shapes=[
+            *(pltpu.VMEM((slots, 2, *shape), F32) for shape in shapes),
+            *(pltpu.VMEM((slots, *shape), BF16) for shape in shapes),
+            *(pltpu.VMEM((slots, 2, *shape), F32) for shape in shapes),
+            pltpu.SemaphoreType.DMA((slots, 15)),
+        ],
+        compiler_params=pltpu.CompilerParams(vmem_limit_bytes=VMEM_BYTES),
+        cost_estimate=pl.CostEstimate(flops=COPY_FLOPS * 18 * size, bytes_accessed=18 * size, transcendentals=0),
         name="moments",
     )(*m, *v, *g)
-    return new
-
-
-def place_columns_kernel(x_ref, gate_ref, up_ref):
-    blocks, devices, _, rows, _ = x_ref.shape
-    for j in range(blocks):
-        at = j // 2 + (blocks // 2 + 1) * (j % 2)
-        for device in range(devices):
-            for u, out_ref in enumerate((gate_ref, up_ref)):
-                out_ref[pl.ds(device * rows, rows), pl.ds(at * LANES, LANES)] = x_ref[j, device, u]
-
-
-def place_columns(chunks, layers, d, ff):
-    number, devices, height, _ = chunks.shape
+
+
+def place_rows_kernel(layers, slots, me_ref, x_hbm, *refs):
+    pieces, down_hbm, (r_in, r_out, held, sem, held_sem) = refs[:-6], refs[-6], refs[-5:]
+    devices = x_hbm.shape[2]
+    pairs = x_hbm.shape[1] - 1
+    height, d = r_out.shape[1:]
     chips = devices // CORES
-    blocks, rows = number // layers, d // devices
-    x = chunks.reshape(layers, blocks, devices, 2, chips, rows, LANES)
-    out = pl.BlockSpec((None, d // 2, ff // chips), lambda l, c, h: (l, h, c))
+    half = LANES // 2
+    chip, core = me_ref[0] // CORES, lax.rem(me_ref[0], CORES)
+
+    def owner(hops, flip):
+        return lax.rem(chip + hops + chips, chips) * CORES + (1 - core if flip else core)
+
+    starts = [owner(hops, flip) * height for flip in (0, 1) for hops in (0, -1, 1)] + [owner(2, 0) * height + part * (height // 2) for part in (0, 1)]
+    fetch, put = [], []
+    for i, (piece, start) in enumerate(zip(pieces, starts)):
+        size = piece.shape[0]
+        fetch.append(pltpu.make_async_copy(piece, held.at[i, pl.ds(0, size)], held_sem.at[i, 0]))
+        put.append(pltpu.make_async_copy(held.at[i, pl.ds(0, size)], down_hbm.at[0, pl.ds(pl.multiple_of(start, 32), size), :], held_sem.at[i, 1]))
+
+    def loads(unit, slot):
+        layer, device = layers - 2 - unit // devices, lax.rem(unit, devices)
+        return [
+            pltpu.make_async_copy(x_hbm.at[layer, pl.ds(0, pairs), device], r_in.at[slot, pl.ds(0, pairs)], sem.at[slot, 0]),
+            pltpu.make_async_copy(x_hbm.at[layer, pairs, device, pl.ds(0, d // 2)], r_in.at[slot, pairs, pl.ds(0, d // 2)], sem.at[slot, 1]),
+        ]
+
+    def stores(unit, slot):
+        layer, device = unit // devices + 1, lax.rem(unit, devices)
+        return [pltpu.make_async_copy(r_out.at[slot], down_hbm.at[layer, strip(device * height, height), :], sem.at[slot, 2])]
+
+    def work(unit, slot):
+        low = lax.rem(unit, CORES)
+        for b in range(d // LANES):
+            there = pl.ds(b * LANES, LANES)
+            for n in range(pairs):
+                r_out[slot, pl.ds(pl.multiple_of(n * LANES + low * half, half), LANES), there] = r_in[slot, n, pl.ds(b * LANES, LANES), :]
+            r_out[slot, pl.ds(pl.multiple_of(pairs * LANES * (1 - low), half), half), there] = r_in[slot, pairs, pl.ds(b * half, half), :]
+
+    for copy in fetch:
+        copy.start()
+    ring = Ring((layers - 1) * devices, slots, loads, stores, work)
+    ring.begin()
+    for one, other in zip(fetch, put):
+        one.wait()
+        other.start()
+    ring.run()
+    ring.end()
+    for copy in put:
+        copy.wait()
+
+
+def place_rows(me, chunks, pieces, layers, d, ff, slots=4):
+    number, devices, _, _ = chunks.shape
+    x = chunks.reshape(layers - 1, -1, devices, d, LANES)
+    height = ff // devices
     return pl.pallas_call(
-        place_columns_kernel,
-        grid=(layers, chips, 2),
-        in_specs=[pl.BlockSpec((None, blocks, devices // 2, 2, None, rows, LANES), lambda l, c, h: (layers - 1 - l, 0, h, 0, c, 0, 0))],
-        out_specs=[out, out],
-        out_shape=[jax.ShapeDtypeStruct((layers, d, ff), BF16)] * 2,
-        compiler_params=pltpu.CompilerParams(dimension_semantics=("arbitrary",) * 3, vmem_limit_bytes=VMEM_BYTES),
-        cost_estimate=pl.CostEstimate(flops=0, bytes_accessed=8 * layers * d * ff, transcendentals=0),
-        name="place_columns",
-    )(x)
-
-
-def place_rows_kernel(x_ref, out_ref):
-    chunks, height, _ = x_ref.shape
-    pairs, cols = chunks - 1, out_ref.shape[1]
-    core = lax.rem(pl.program_id(1), CORES)
-    half = LANES // 2
-    for b in range(cols // LANES):
-        there = pl.ds(b * LANES, LANES)
-        for n in range(pairs):
-            out_ref[pl.ds(pl.multiple_of(n * LANES + core * half, half), LANES), there] = x_ref[n, pl.ds(b * LANES, LANES), :]
-        out_ref[pl.ds(pl.multiple_of(pairs * LANES * (1 - core), half), half), there] = x_ref[pairs, pl.ds(b * half, half), :]
-
-
-def place_rows(chunks, layers, d, ff):
-    number, devices, height, _ = chunks.shape
-    x = chunks.reshape(layers, number // layers, devices, height, LANES)
+        functools.partial(place_rows_kernel, layers, slots),
+        in_specs=[pl.BlockSpec(memory_space=pltpu.SMEM)] + [ANY] * (1 + len(pieces)),
+        out_specs=ANY,
+        out_shape=jax.ShapeDtypeStruct((layers, ff, d), BF16),
+        scratch_shapes=[
+            pltpu.VMEM((slots, x.shape[1], d, LANES), BF16),
+            pltpu.VMEM((slots, height, d), BF16),
+            pltpu.VMEM((len(pieces), height, d), BF16),
+            pltpu.SemaphoreType.DMA((slots, 3)),
+            pltpu.SemaphoreType.DMA((len(pieces), 2)),
+        ],
+        compiler_params=pltpu.CompilerParams(vmem_limit_bytes=VMEM_BYTES),
+        cost_estimate=pl.CostEstimate(flops=COPY_FLOPS * 4 * layers * d * ff, bytes_accessed=4 * layers * d * ff, transcendentals=0),
+        name="place_rows",
+    )(me, x, *pieces)
+
+
+def place_last_kernel(me_ref, top_hbm, bottom_hbm, _, down_hbm, held, sem):
+    half = top_hbm.shape[0]
+    chips = down_hbm.shape[1] // (2 * half * CORES)
+    owner = lax.rem(me_ref[0] // CORES + 2, chips) * CORES + 1 - lax.rem(me_ref[0], CORES)
+    fetch, put = [], []
+    for i, piece in enumerate((top_hbm, bottom_hbm)):
+        fetch.append(pltpu.make_async_copy(piece, held.at[i], sem.at[i, 0]))
+        put.append(pltpu.make_async_copy(held.at[i], down_hbm.at[0, pl.ds(pl.multiple_of((2 * owner + i) * half, 32), half), :], sem.at[i, 1]))
+    for copy in fetch:
+        copy.start()
+    for one, other in zip(fetch, put):
+        one.wait()
+        other.start()
+    for copy in put:
+        copy.wait()
+
+
+def place_last(me, top, bottom, down):
     return pl.pallas_call(
-        place_rows_kernel,
-        grid=(layers, devices),
-        in_specs=[pl.BlockSpec((None, number // layers, None, height, LANES), lambda l, i: (layers - 1 - l, 0, i, 0, 0))],
-        out_specs=pl.BlockSpec((None, ff // devices, d), lambda l, i: (l, i, 0)),
-        out_shape=jax.ShapeDtypeStruct((layers, ff, d), BF16),
-        compiler_params=pltpu.CompilerParams(dimension_semantics=("arbitrary",) * 2, vmem_limit_bytes=VMEM_BYTES),
-        cost_estimate=pl.CostEstimate(flops=0, bytes_accessed=4 * layers * d * ff, transcendentals=0),
-        name="place_rows",
-    )(x)
+        place_last_kernel,
+        in_specs=[pl.BlockSpec(memory_space=pltpu.SMEM)] + [ANY] * 3,
+        out_specs=ANY,
+        out_shape=jax.ShapeDtypeStruct(down.shape, BF16),
+        input_output_aliases={3: 0},
+        scratch_shapes=[pltpu.VMEM((2, *top.shape), BF16), pltpu.SemaphoreType.DMA((2, 2))],
+        cost_estimate=pl.CostEstimate(flops=COPY_FLOPS * 4 * top.size, bytes_accessed=8 * top.size, transcendentals=0),
+        name="place_last",
+    )(me, top, bottom, down)
 
 
 def solution(mesh):
+    group = mesh.shape["dp"]
+    swap = [(i, i ^ 1) for i in range(group)]
+    right = [(i, (i + CORES) % group) for i in range(group)]
+    left = [(i, (i - CORES) % group) for i in range(group)]
+
     def step(x, dy, *arrays):
         weights, m, v = (arrays[i : i + 3] for i in (0, 3, 6))
+        layers, d, ff = weights[0].shape
         x, dy = x[0], dy[0]
-        layers, d, ff = weights[0].shape
+        me = lax.axis_index("dp").reshape(1)
         a, h = forward(x, *weights, 0)
-        *sums, columns, rows, _ = backward(mesh, a, dy, h, weights, m, v)
-        new = (*place_columns(columns, layers, d, ff), place_rows(rows, layers, d, ff))
-        states = moments(m, v, sums, ((1, 9), (1, 9), (9, 1)))
-        return (*new, *states)
+        *sums, columns, rows, own, _ = backward(mesh, a, dy, h, weights, m, v)
+
+        def send(block, to):
+            return lax.ppermute(block, "dp", to)
+
+        near = [own, send(own, right), send(own, left)]
+        gate, up = place_columns(columns, layers, d, ff)
+        gate, *near[1:] = lax.optimization_barrier((gate, *near[1:]))
+        half = own.shape[0] // 2
+        far = [send(near[1][:half], right), send(near[2][half:], left)]
+        other = [send(block, swap) for block in near]
+        first, *states = moments(m, v, sums)
+        first, *far = lax.optimization_barrier((first, *far))
+        last = [send(block, swap) for block in far]
+        down = place_rows(me, rows, near + other + far, layers, d, ff)
+        return (gate, up, place_last(me, *last, down), first, *states)
 
     seq, whole, rows = P(("rep", "dp"), None, None), P(None, None, None), P(None, "dp", None)
     return jax.shard_map(

time: 740 us -> 701 us (0.947)
  Pallas kernels: 738 us -> 689 us
    pallas_call x1, Pallas kernels: 566 us -> 531 us  [backward(): pl.pallas_call(functools.partial(backward_kernel, chips, tile), out_shape...]
    pallas_call x3 -> x4, Pallas kernels: 84 us -> 70.6 us  [the longest x1 28.9 us: place_columns(): pl.pallas_call(functools.partial(place_columns_kernel, layers, slots), in...]
  transfers between devices with their start and end apart: 0 -> 9, of which waited for: 0 -> 1; matrix products, arithmetic and copies ran while one was open for 0% -> 0% of each run, Pallas kernels for 0% -> 10%
where the time goes in v2:
time: 701 us
  Pallas kernels  689 us (98%)
    pallas_call x1, Pallas kernels, backward(): pl.pallas_call(functools.partial(backward_kernel, chips, tile), out_shape...  531 us
    pallas_call x1, Pallas kernels, forward(): pl.pallas_call(functools.partial(forward_kernel, tile), grid=(ff // width...  87.3 us
    pallas_call x1, Pallas kernels, place_columns(): pl.pallas_call(functools.partial(place_columns_kernel, layers, slots), in...  28.9 us
    pallas_call x1, Pallas kernels, moments(): pl.pallas_call(functools.partial(moments_kernel, layers, parts, slots), i...  24.6 us
    pallas_call x1, Pallas kernels, place_rows(): pl.pallas_call(functools.partial(place_rows_kernel, layers, slots), in_sp...  14.9 us
  transfers between devices with their start and end apart: 9, of which 1 were waited for; matrix products, arithmetic and copies ran while one was open for 0% of the time, Pallas kernels for 10%

profile of v2, /device:TPU:113, one launch (start us, length us, event | category | flops | bytes accessed | tf_op | source)
XLA Modules:
  0.0 701.0 jit_solution(8460988700694828617)
XLA Ops:
  0.6 87.3 %forward.1 = (bf16[2,2048,1152]{2,1,0:T(8,128)(2,1)}, bf16[2048,1152]{1,0:T(8,128)(2,1)}) custom-call(bf16[2048,1152]{1,0:T(8,128)(2,1)} %bitcast.7, bf16[2,1152,4608]{2,1,0:T(8,128)(2,1)} %refs_3_.2, bf16[2,1152,4608]{2,1,0:T(8,128)(2,1)} %refs_4_.2, bf16[2,4608,1152]{2,1,0:T(8,128)(2,1)} %refs_5_.2), custom_call_target="tpu_custom_call" | custom-call | flops 65229815808 | bytes 50724864 | tf_op jit(solution)/shard_map/forward/pallas_call | solution.py:96
  88.0 531.2 %backward.1 = (bf16[2,144,4608]{2,1,0:T(8,128)(2,1)}, bf16[2,144,4608]{2,1,0:T(8,128)(2,1)}, bf16[2,576,1152]{2,1,0:T(8,128)(2,1)}, bf16[18,8,1152,128]{3,2,1,0:...) custom-call(bf16[2,2048,1152]{2,1,0:T(8,128)(2,1)} %get-tuple-element.31.ref, ...), custom_call_target="tpu_custom_call" | custom-call | flops 304405807104 | bytes 127401984 | tf_op jit(solution)/shard_map/backward/pallas_call | solution.py:653
  619.2 1.2 collective-permute-start.1
  620.4 0.4 collective-permute-start
  620.8 0.7 collective-permute-start.6
  621.5 28.9 %place_columns.1 = (bf16[2,1152,4608]{2,1,0:T(8,128)(2,1)}, bf16[2,1152,4608]{2,1,0:T(8,128)(2,1)}) custom-call(bf16[2,9,8,2,4,144,128]{6,5,4,3,2,1,0:T(8,128)(2,1)} %bitcast.5), custom_call_target="tpu_custom_call" | custom-call | flops 5435817984 | bytes 84934656 | tf_op jit(solution)/shard_map/place_columns/pallas_call | solution.py:758
  650.4 0.0 collective-permute-done.1.refs_2_
  650.4 0.0 copy-start
  650.4 1.8 collective-permute-done.refs_1_
  652.2 1.3 collective-permute-start.7
  653.5 0.0 collective-permute-start.8
  653.5 2.0 slice.6
  655.4 0.9 slice.7
  656.3 0.0 collective-permute-start.3
  656.3 1.5 collective-permute-start.2
  657.8 24.6 %moments.1 = (f32[2,144,4608]{2,1,0:T(8,128)}, f32[2,144,4608]{2,1,0:T(8,128)}, f32[2,576,1152]{2,1,0:T(8,128)}, f32[2,144,4608]{2,1,0:T(8,128)}, f32[2,144,4608]{2,1,0:T(8,128)}, /*index=5*/f32[2,576,1152]{2,1,0:T(8,128)}) custom-call(f32[2,144,4608]{2,1,0:T(8,128)} %refs_0_.1, f32[2,144,4608]{2,1,0:T(8,128)} %refs_1_.1, f32[2,576,1152]{2,1,0:T(8,128)} %refs_2_.1, ...), custom_call_target="tpu_custom_call" | custom-call | flops 4586471424 | bytes 71663616 | tf_op jit(solution)/shard_map/moments/pallas_call | solution.py:811
  682.4 0.0 copy-done
  682.4 0.0 collective-permute-done.3.refs_7_
  682.4 0.0 copy-start.1
  682.4 0.0 collective-permute-done.2.refs_6_
  682.4 1.1 collective-permute-start.4
  683.5 0.1 collective-permute-start.5
  683.6 0.0 collective-permute-done.6.refs_3_
  683.6 0.0 collective-permute-done.7.refs_4_
  683.6 0.0 collective-permute-done.8.refs_5_
  683.6 0.0 copy-done.1
  683.7 14.9 %place_rows.1._ = bf16[2,4608,1152]{2,1,0:T(8,128)(2,1)} custom-call(s32[1]{0:T(128)} %bitcast.3.me_ref, bf16[1,5,8,1152,128]{4,3,2,1,0:T(8,128)(2,1)} %bitcast.6, bf16[576,1152]{1,0:T(8,128)(2,1)} %get-tuple-element.35.refs_0_, bf16[576,1152]{1,0:T(8,128)(2,1)} %collective-permute-done.refs_1_, bf16[576,1152]{1,0:T(8,128)(2,1)} %copy-done, ...), custom_call_target="tpu_custom_call" | custom-call | flops 2717908992 | bytes 42467328 | tf_op jit(solution)/shard_map/place_rows/pallas_call | solution.py:883
  698.6 0.0 collective-permute-done.4.top_hbm
  698.6 0.0 collective-permute-done.5.bottom_hbm
  698.6 2.2 place_last.1
Async XLA Ops:
  619.2 31.2 %collective-permute-start.1 = (bf16[576,1152]{1,0:T(8,128)(2,1)}, bf16[576,1152]{1,0:T(8,128)(2,1)S(1)}, u32[]{:S(2)}, u32[]{:S(2)}) collective-permute-start(bf16[576,1152]{1,0:T(8,128)(2,1)} %get-tuple-element.35.refs_0_), channel_id=1, source_target_pairs={{0,6},{1,7},{2,0},{3,1},{4,2},{5,3},{6,4},{7,5},{8,14},{9,15},{10,... | collective-permute-start | bytes 3981320 | tf_op jit(solution)/shard_map/ppermute | solution.py:946
  620.4 31.8 %collective-permute-start = (bf16[576,1152]{1,0:T(8,128)(2,1)}, bf16[576,1152]{1,0:T(8,128)(2,1)}, u32[]{:S(2)}, u32[]{:S(2)}) collective-permute-start(bf16[576,1152]{1,0:T(8,128)(2,1)} %get-tuple-element.35.refs_0_), channel_id=1, source_target_pairs={{0,2},{1,3},{2,4},{3,5},{4,6},{5,7},{6,0},{7,1},{8,10},{9,11},{10,... | collective-permute-start | bytes 3981320 | tf_op jit(solution)/shard_map/ppermute | solution.py:946
  620.8 62.9 %collective-permute-start.6 = (bf16[576,1152]{1,0:T(8,128)(2,1)}, bf16[576,1152]{1,0:T(8,128)(2,1)}, u32[]{:S(2)}, u32[]{:S(2)}) collective-permute-start(bf16[576,1152]{1,0:T(8,128)(2,1)} %get-tuple-element.35.refs_0_), channel_id=1, source_target_pairs={{0,1},{1,0},{2,3},{3,2},{4,5},{5,4},{6,7},{7,6},{8,9},{9,8},{10,11... | collective-permute-start | bytes 3981320 | tf_op jit(solution)/shard_map/ppermute | solution.py:946
  650.4 32.0 %copy-start = (bf16[576,1152]{1,0:T(8,128)(2,1)}, bf16[576,1152]{1,0:T(8,128)(2,1)S(1)}, u32[]{:S(2)}) copy-start(bf16[576,1152]{1,0:T(8,128)(2,1)S(1)} %collective-permute-done.1.refs_2_) | copy-start | bytes 3981316
  652.2 31.5 %collective-permute-start.7 = (bf16[576,1152]{1,0:T(8,128)(2,1)}, bf16[576,1152]{1,0:T(8,128)(2,1)}, u32[]{:S(2)}, u32[]{:S(2)}) collective-permute-start(bf16[576,1152]{1,0:T(8,128)(2,1)} %collective-permute-done.refs_1_), channel_id=1, source_target_pairs={{0,1},{1,0},{2,3},{3,2},{4,5},{5,4},{6,7},{7,6},{8,9},{9,8},{10,11... | collective-permute-start | bytes 3981320 | tf_op jit(solution)/shard_map/ppermute | solution.py:946
  653.5 30.2 %collective-permute-start.8 = (bf16[576,1152]{1,0:T(8,128)(2,1)S(1)}, bf16[576,1152]{1,0:T(8,128)(2,1)}, u32[]{:S(2)}, u32[]{:S(2)}) collective-permute-start(bf16[576,1152]{1,0:T(8,128)(2,1)S(1)} %collective-permute-done.1.refs_2_), channel_id=1, source_target_pairs={{0,1},{1,0},{2,3},{3,2},{4,5},{5,4},{6,7},{7,6},{8,9},{9,8},{10,11... | collective-permute-start | bytes 3981320 | tf_op jit(solution)/shard_map/ppermute | solution.py:946
  656.3 26.0 %collective-permute-start.3 = (bf16[288,1152]{1,0:T(8,128)(2,1)}, bf16[288,1152]{1,0:T(8,128)(2,1)S(1)}, u32[]{:S(2)}, u32[]{:S(2)}) collective-permute-start(bf16[288,1152]{1,0:T(8,128)(2,1)} %slice.7), channel_id=1, source_target_pairs={{0,6},{1,7},{2,0},{3,1},{4,2},{5,3},{6,4},{7,5},{8,14},{9,15},{10,... | collective-permute-start | bytes 1990664 | tf_op jit(solution)/shard_map/ppermute | solution.py:946
  656.3 26.1 %collective-permute-start.2 = (bf16[288,1152]{1,0:T(8,128)(2,1)}, bf16[288,1152]{1,0:T(8,128)(2,1)}, u32[]{:S(2)}, u32[]{:S(2)}) collective-permute-start(bf16[288,1152]{1,0:T(8,128)(2,1)} %slice.6), channel_id=1, source_target_pairs={{0,2},{1,3},{2,4},{3,5},{4,6},{5,7},{6,0},{7,1},{8,10},{9,11},{10,... | collective-permute-start | bytes 1990664 | tf_op jit(solution)/shard_map/ppermute | solution.py:946
  682.4 1.3 copy-start.1
  682.4 16.2 %collective-permute-start.4 = (bf16[288,1152]{1,0:T(8,128)(2,1)}, bf16[288,1152]{1,0:T(8,128)(2,1)}, u32[]{:S(2)}, u32[]{:S(2)}) collective-permute-start(bf16[288,1152]{1,0:T(8,128)(2,1)} %collective-permute-done.2.refs_6_), channel_id=1, source_target_pairs={{0,1},{1,0},{2,3},{3,2},{4,5},{5,4},{6,7},{7,6},{8,9},{9,8},{10,11... | collective-permute-start | bytes 1990664 | tf_op jit(solution)/shard_map/ppermute | solution.py:946
  683.5 15.1 %collective-permute-start.5 = (bf16[288,1152]{1,0:T(8,128)(2,1)S(1)}, bf16[288,1152]{1,0:T(8,128)(2,1)}, u32[]{:S(2)}, u32[]{:S(2)}) collective-permute-start(bf16[288,1152]{1,0:T(8,128)(2,1)S(1)} %collective-permute-done.3.refs_7_), channel_id=1, source_target_pairs={{0,1},{1,0},{2,3},{3,2},{4,5},{5,4},{6,7},{7,6},{8,9},{9,8},{10,11... | collective-permute-start | bytes 1990664 | tf_op jit(solution)/shard_map/ppermute | solution.py:946

commit v3 on v2

--- a/solution.py
+++ b/solution.py
@@ -7,16 +7,15 @@
 from jax.experimental.pallas import tpu as pltpu
 from jax.sharding import PartitionSpec as P
 
-NAMES = ("w_gate", "w_up", "w_down")
 F32, BF16 = jnp.float32, jnp.bfloat16
 NN, NT = (((1,), (0,)), ((), ())), (((1,), (1,)), ((), ()))
 MESH = pl.DeviceIdType.MESH
 ANY = pl.BlockSpec(memory_space=pl.ANY)
 LANES = 128
 CORES = 2
-VMEM_BYTES = 62 << 20
-VMEM_MOST = 67_043_328
+VMEM_BYTES = 67_043_328
 COPY_FLOPS = 64
+SIDES = (0, 1), (1, -1)
 
 
 def dot(a, b, dims=NN):
@@ -32,29 +31,56 @@
     return pl.ds(pl.multiple_of(start, size), size)
 
 
+def head(size):
+    return pl.ds(0, size)
+
+
+def parity(n):
+    return lax.rem(n, 2)
+
+
+def lanes(n):
+    return pl.ds(n * LANES, LANES)
+
+
+def start(copies):
+    for copy in copies:
+        copy.start()
+
+
+def wait(copies):
+    for copy in copies:
+        copy.wait()
+
+
+def cost(flops, moved):
+    return pl.CostEstimate(flops=flops, bytes_accessed=moved, transcendentals=moved)
+
+
 def forward_kernel(tile, x_ref, wg_ref, wu_ref, wd_ref, a_hbm, h_hbm, a_ref, total, ends, a_sem, end_sem):
-    block, blocks = pl.program_id(0), pl.num_programs(0)
+    block = pl.program_id(0)
+    first, last = block == 0, block == pl.num_programs(0) - 1
     tiles = x_ref.shape[0] // tile
 
     def keep(t):
         rows = strip(t * tile, tile)
-        return pltpu.make_async_copy(a_ref.at[rows, :], a_hbm.at[0, rows, :], a_sem.at[t])
+        return pltpu.make_async_copy(a_ref.at[rows], a_hbm.at[0, rows], a_sem.at[t])
 
     def finish(t):
-        slot, rows = lax.rem(t, 2), strip(t * tile, tile)
-        yield pltpu.make_async_copy(ends.at[slot, 0], h_hbm.at[rows, :], end_sem.at[slot, 0])
-        yield pltpu.make_async_copy(ends.at[slot, 1], a_hbm.at[1, rows, :], end_sem.at[slot, 1])
-
-    @pl.when(block == 0)
+        rows = strip(t * tile, tile)
+        for i, out in enumerate((h_hbm, a_hbm.at[1])):
+            yield pltpu.make_async_copy(ends.at[parity(t), i], out.at[rows], end_sem.at[parity(t), i])
+
+    @pl.when(first)
     def _():
-        def start(t, _):
+        def begin(t, _):
             rows = strip(t * tile, tile)
             a_ref[rows, :] = norm(x_ref[rows, :])
             total[rows, :] = jnp.zeros((tile, total.shape[1]), F32)
             keep(t).start()
-            return 0
-
-        lax.fori_loop(0, tiles, start, 0)
+            return t
+
+        lax.fori_loop(0, tiles, begin, 0)
 
     def one(t, _):
         rows = strip(t * tile, tile)
@@ -63,56 +89,45 @@
         z = (jax.nn.sigmoid(gate) * gate * up).astype(BF16)
         total[rows, :] += dot(z, wd_ref[...])
 
-        @pl.when(block == blocks - 1)
-        def _():
-            slot = lax.rem(t, 2)
+        @pl.when(last)
+        def _():
             keep(t).wait()
-
-            @pl.when(t >= 2)
-            def _():
-                for copy in finish(t - 2):
-                    copy.wait()
-
+            pl.when(t >= 2)(lambda: wait(finish(t - 2)))
             h = x_ref[rows, :] + total[rows, :].astype(BF16)
-            ends[slot, 0] = h
-            ends[slot, 1] = norm(h)
-            for copy in finish(t):
-                copy.start()
-
-        return 0
+            for i, end in enumerate((h, norm(h))):
+                ends[parity(t), i] = end
+            start(finish(t))
+
+        return t
 
     lax.fori_loop(0, tiles, one, 0)
 
-    @pl.when(block == blocks - 1)
+    @pl.when(last)
     def _():
-        for t in (tiles - 2, tiles - 1):
-            for copy in finish(t):
-                copy.wait()
+        for t in range(tiles - 2, tiles):
+            wait(finish(t))
 
 
 def forward(x, wg, wu, wd, layer, width=768, tile=512):
     tokens, d = x.shape
     ff = wg.shape[2]
+    state = jax.ShapeDtypeStruct((tokens, d), BF16)
+    columns = pl.BlockSpec((None, d, width), lambda i: (layer, 0, i))
     return pl.pallas_call(
         functools.partial(forward_kernel, tile),
         grid=(ff // width,),
-        out_shape=[jax.ShapeDtypeStruct((2, tokens, d), BF16), jax.ShapeDtypeStruct((tokens, d), BF16)],
-        in_specs=[
-            pl.BlockSpec((tokens, d), lambda i: (0, 0)),
-            pl.BlockSpec((None, d, width), lambda i: (layer, 0, i)),
-            pl.BlockSpec((None, d, width), lambda i: (layer, 0, i)),
-            pl.BlockSpec((None, width, d), lambda i: (layer, i, 0)),
-        ],
-        out_specs=[ANY, ANY],
+        out_shape=[jax.ShapeDtypeStruct((2, tokens, d), BF16), state],
+        in_specs=[pl.BlockSpec(x.shape, lambda i: (0, 0)), columns, columns, pl.BlockSpec((None, width, d), lambda i: (layer, i, 0))],
+        out_specs=[ANY] * 2,
         scratch_shapes=[
-            pltpu.VMEM((tokens, d), BF16),
-            pltpu.VMEM((tokens, d), F32),
+            pltpu.VMEM(x.shape, BF16),
+            pltpu.VMEM(x.shape, F32),
             pltpu.VMEM((2, 2, tile, d), BF16),
             pltpu.SemaphoreType.DMA((tokens // tile,)),
             pltpu.SemaphoreType.DMA((2, 2)),
         ],
-        compiler_params=pltpu.CompilerParams(dimension_semantics=("arbitrary",), vmem_limit_bytes=VMEM_BYTES),
-        cost_estimate=pl.CostEstimate(flops=6 * tokens * d * ff, bytes_accessed=6 * d * ff + 8 * tokens * d, transcendentals=tokens * ff),
+        compiler_params=pltpu.CompilerParams(vmem_limit_bytes=VMEM_BYTES),
+        cost_estimate=cost(6 * tokens * d * ff, 6 * d * ff),
         name="forward",
     )(x, wg, wu, wd)
 
@@ -139,22 +154,16 @@
 
     def copies0(self, n, rows):
         slot = lax.rem(n, self.slots)
-        src = self.mine.at[slot, 1 - self.core, :, pl.ds(0, rows), :]
-        return [self.hop(self.dma.at[slot, 0], src, self.other.at[slot, :, pl.ds(0, rows), :], self.partner())]
+        src = self.mine.at[slot, 1 - self.core, :, head(rows), :]
+        return [self.hop(self.dma.at[slot, 0], src, self.other.at[slot, :, head(rows), :], self.partner())]
 
     def copies1(self, n, rows):
-        slot, sem, half = lax.rem(n, self.lanes), lax.rem(n, self.slots), pl.ds(0, rows // 2)
-        return [
-            self.hop(self.dma.at[sem, 1 + side], self.out1.at[slot, side, half, :], self.cross.at[slot, side, half, :], self.device(1 - 2 * side))
-            for side in range(2)
-        ]
+        slot, sem, half = lax.rem(n, self.lanes), lax.rem(n, self.slots), head(rows // 2)
+        return [self.hop(self.dma.at[sem, 1 + side], self.out1.at[slot, side, half], self.cross.at[slot, side, half], self.device(hop)) for side, hop in SIDES]
 
     def copies2(self, n, rows):
-        slot, sem, full = lax.rem(n, self.lanes), lax.rem(n, self.slots), pl.ds(0, rows)
-        return [
-            self.hop(self.dma.at[sem, 3 + side], self.out2.at[slot, side, full, :], self.near.at[slot, side, full, :], self.device(1 - 2 * side))
-            for side in range(2)
-        ]
+        slot, sem, full = lax.rem(n, self.lanes), lax.rem(n, self.slots), head(rows)
+        return [self.hop(self.dma.at[sem, 3 + side], self.out2.at[slot, side, full], self.near.at[slot, side, full], self.device(hop)) for side, hop in SIDES]
 
     def both(self, n, hops, start, size):
         slot, chip = lax.rem(n, self.slots), lax.rem(self.chip + hops + self.chips, self.chips)
@@ -172,54 +181,44 @@
 
     def event0(self, n, rows):
         self.take(n >= self.slots, (0,))
-        for copy in self.copies0(n, rows):
-            copy.start()
+        start(self.copies0(n, rows))
 
     def event1(self, n, rows):
         slot, half = lax.rem(n, self.lanes), rows // 2
-        for copy in self.copies0(n, rows):
-            copy.wait()
-        for side in range(2):
-            self.out1[slot, side, pl.ds(0, half), :] = self.both(n, 2, side * half, half).astype(BF16)
+        wait(self.copies0(n, rows))
+        for side, _ in SIDES:
+            self.out1[slot, side, head(half)] = self.both(n, 2, side * half, half).astype(BF16)
         self.take(n >= self.lanes, (1, 2))
-        for copy in self.copies1(n, rows):
-            copy.start()
+        start(self.copies1(n, rows))
 
     def event2(self, n, rows):
         slot, half = lax.rem(n, self.lanes), rows // 2
-        for copy in self.copies1(n, rows):
-            copy.wait()
-        for side in range(2):
-            hops, there, here = 1 - 2 * side, pl.ds(side * half, half), pl.ds((1 - side) * half, half)
-            passed = self.both(n, hops, side * half, half) + self.cross[slot, side, pl.ds(0, half), :].astype(F32)
-            self.out2[slot, side, there, :] = passed.astype(BF16)
-            self.out2[slot, side, here, :] = self.both(n, hops, (1 - side) * half, half).astype(BF16)
+        wait(self.copies1(n, rows))
+        for side, hop in SIDES:
+            passed = self.both(n, hop, side * half, half) + self.cross[slot, side, head(half)].astype(F32)
+            self.out2[slot, side, pl.ds(side * half, half), :] = passed.astype(BF16)
+            self.out2[slot, side, pl.ds(half - side * half, half), :] = self.both(n, hop, half - side * half, half).astype(BF16)
 
         @pl.when(n + self.lanes < self.number)
         def _():
-            self.give(1, self.device(-1))
-            self.give(2, self.device(1))
+            for side, hop in SIDES:
+                self.give(1 + side, self.device(-hop))
 
         self.take(n >= self.lanes, (3, 4))
-        for copy in self.copies2(n, rows):
-            copy.start()
+        start(self.copies2(n, rows))
 
     def event3(self, n, rows):
         slot = lax.rem(n, self.lanes)
-        for copy in self.copies2(n, rows):
-            copy.wait()
+        wait(self.copies2(n, rows))
         total = self.both(n, 0, 0, rows)
-        for side in range(2):
-            total += self.near[slot, side, pl.ds(0, rows), :].astype(F32)
-
-        @pl.when(n + self.slots < self.number)
-        def _():
-            self.give(0, self.partner())
+        for side, _ in SIDES:
+            total += self.near[slot, side, head(rows)].astype(F32)
+        pl.when(n + self.slots < self.number)(lambda: self.give(0, self.partner()))
 
         @pl.when(n + self.lanes < self.number)
         def _():
-            self.give(3, self.device(-1))
-            self.give(4, self.device(1))
+            for side, hop in SIDES:
+                self.give(3 + side, self.device(-hop))
 
         return total.astype(BF16).astype(F32)
 
@@ -230,57 +229,53 @@
         return self.ag_sem.at[lax.rem(n, self.turns), kind]
 
     def gathers1(self, n, rows):
-        new, own = self.new.at[pl.ds(0, rows), :], self.block(n, 0, self.core, 0, rows)
-        to = (self.device(1), self.device(-1), self.partner())
-        return [self.hop(self.sems(n, kind), new, own, device) for kind, device in enumerate(to)] + [pltpu.make_async_copy(new, own, self.own_sem)]
+        new, own = self.new.at[head(rows)], self.block(n, 0, self.core, 0, rows)
+        copies = [self.hop(self.sems(n, side), new, own, self.device(hop)) for side, hop in SIDES]
+        return [*copies, self.hop(self.sems(n, 7), new, own, self.partner()), pltpu.make_async_copy(new, own, self.own_sem)]
 
     def gathers2(self, n, rows):
-        copies = []
-        for side in range(2):
-            half = self.block(n, 2 * side - 1, self.core, side * (rows // 2), rows // 2)
-            full = self.block(n, 2 * side - 1, self.core, 0, rows)
-            copies.append(self.hop(self.sems(n, 3 + side), half, half, self.device(1 - 2 * side)))
-            copies.append(self.hop(self.sems(n, 5 + side), full, full, self.partner()))
+        copies, half = [], rows // 2
+        for side, hop in SIDES:
+            part, full = (self.block(n, -hop, self.core, *which) for which in ((side * half, half), (0, rows)))
+            copies.append(self.hop(self.sems(n, 2 + side), part, part, self.device(hop)))
+            copies.append(self.hop(self.sems(n, 4 + side), full, full, self.partner()))
         return copies
 
     def gathers3(self, n, rows):
         opposite = self.block(n, 2, self.core, 0, rows)
-        return [self.hop(self.sems(n, 7), opposite, opposite, self.partner())]
+        return [self.hop(self.sems(n, 6), opposite, opposite, self.partner())]
 
     def gather1(self, n, rows):
-        for copy in self.gathers1(n, rows):
-            copy.start()
+        start(self.gathers1(n, rows))
 
     def gather2(self, n, rows):
-        for copy in self.gathers1(n, rows):
-            copy.wait()
-        for copy in self.gathers2(n, rows):
-            copy.start()
+        wait(self.gathers1(n, rows))
+        start(self.gathers2(n, rows))
 
     def gather3(self, n, rows):
-        for copy in self.gathers2(n, rows):
-            copy.wait()
-        for copy in self.gathers3(n, rows):
-            copy.start()
+        wait(self.gathers2(n, rows))
+        start(self.gathers3(n, rows))
 
     def gather4(self, n, rows):
-        for copy in self.gathers3(n, rows):
-            copy.wait()
+        wait(self.gathers3(n, rows))
+
+
+def moment(m, v, g):
+    return 0.9 * m + 0.1 * g, 0.95 * v + 0.05 * g * g
 
 
 def adam(w, m, v, g):
-    m = 0.9 * m + 0.1 * g
-    v = 0.95 * v + 0.05 * g * g
+    m, v = moment(m, v, g)
     w = w.astype(F32)
     return (w - 0.02 * (m * lax.rsqrt(v + 1e-8) + 0.1 * w)).astype(BF16)
 
 
 def backward_kernel(chips, tile, *refs):
-    a_hbm, dy_hbm, h_hbm, wg_hbm, wu_hbm, wd_hbm, mg_hbm, mu_hbm, md_hbm, vg_hbm, vu_hbm, vd_hbm, *refs = refs
+    a_hbm, h_hbm, dy_hbm, wg_hbm, wu_hbm, wd_hbm, mg_hbm, mu_hbm, md_hbm, vg_hbm, vu_hbm, vd_hbm, *refs = refs
     gg_hbm, gu_hbm, gd_hbm, whole_gu, whole_dn, own_hbm, dy0_hbm, *refs = refs
     a_tile, dy_tile, at_ref, dyt_ref, da_ref, wg_ref, wu_ref, wd_ref, z_ref, dgu_ref, m_ref, v_ref, w_ref, *refs = refs
     tile_sem, w_sem, state_sem, rows_sem, *pools = refs
-    tokens, d = a_hbm.shape[1:]
+    tokens, d = dy_hbm.shape
     layers, _, ff = wg_hbm.shape
     width = chips * LANES
     blocks = ff // width
@@ -291,7 +286,7 @@
     chip, core = me // CORES, lax.rem(me, CORES)
     tiles = tokens // tile
     steps = layers * blocks
-    full, small = d, d // 2
+    full, small, small_tile = d, d // 2, tile // 4
 
     gu = Pool(steps, chips, core, chip, pools[0:8], pools[8:13], whole_gu)
     dn = Pool(layers * (pairs + 1), chips, core, chip, pools[13:21], pools[21:26], whole_dn)
@@ -301,7 +296,7 @@
 
     def block_of(j):
         j = lax.rem(j, blocks)
-        return j // 2 + (pairs + 1) * lax.rem(j, 2)
+        return j // 2 + (pairs + 1) * parity(j)
 
     def columns(c, j):
         return strip(c * blocks * LANES + block_of(j) * LANES, LANES)
@@ -310,7 +305,7 @@
         return lax.rem(j, blocks) == blocks - 1
 
     def gives_down(j):
-        return (j >= 0) & (j < steps) & ((lax.rem(lax.rem(j, blocks), 2) == 1) | is_last(j))
+        return (j >= 0) & (j < steps) & ((parity(lax.rem(j, blocks)) == 1) | is_last(j))
 
     def down_of(j):
         return (j // blocks) * (pairs + 1) + lax.rem(j, blocks) // 2
@@ -325,15 +320,15 @@
             act(down_of(j), small)
 
     def weight_copies(j):
-        layer, slot = layer_of(j), lax.rem(j, 2)
+        layer, slot = layer_of(j), parity(j)
         for c in range(chips):
-            there, here = columns(c, j), pl.ds(c * LANES, LANES)
+            there, here = columns(c, j), lanes(c)
             yield pltpu.make_async_copy(wg_hbm.at[layer, :, there], wg_ref.at[slot, :, here], w_sem.at[slot, 3 * c])
             yield pltpu.make_async_copy(wu_hbm.at[layer, :, there], wu_ref.at[slot, :, here], w_sem.at[slot, 3 * c + 1])
             yield pltpu.make_async_copy(wd_hbm.at[layer, there, :], wd_ref.at[slot, here, :], w_sem.at[slot, 3 * c + 2])
 
     def load(src, buf, t, which):
-        slot = lax.rem(t, 2)
+        slot = parity(t)
         return pltpu.make_async_copy(src.at[strip(t * tile, tile), :], buf.at[slot], tile_sem.at[slot, which])
 
     def start_tile(j, t):
@@ -373,7 +368,7 @@
         start = step * LANES + core * (LANES // 2) if size == full else pairs * LANES * (1 - core)
         height = size // lane_blocks
         for b in range(lane_blocks):
-            yield b, layers - 1 - n // (pairs + 1), start, height, pl.ds(b * height, height), pl.ds(b * LANES, LANES)
+            yield b, layers - 1 - n // (pairs + 1), start, height, pl.ds(b * height, height), lanes(b)
 
     def dn_outs(n, size):
         for b, layer, start, height, here, there in dn_parts(n, size):
@@ -392,14 +387,6 @@
                 yield pltpu.make_async_copy(src.at[layer, at, there], buf.at[here, :], state_sem.at[3 * b + k])
             at = pl.ds(pl.multiple_of(me * (d // 2) + start, LANES // 2), height)
             yield pltpu.make_async_copy(wd_hbm.at[layer, at, there], w_ref.at[here, :], state_sem.at[3 * b + 2])
-
-    def start(copies):
-        for copy in copies:
-            copy.start()
-
-    def wait(copies):
-        for copy in copies:
-            copy.wait()
 
     def gu_new(n, rows):
         g = gu.event3(n, rows)
@@ -434,7 +421,7 @@
 
     def turn(buf, slot, into, part):
         for b in range(lane_blocks):
-            into[pl.ds(b * LANES, LANES), part] = buf[slot, :, b * LANES : (b + 1) * LANES].T
+            into[lanes(b), part] = buf[slot, :, b * LANES : (b + 1) * LANES].T
 
     start_tile(0, 0)
     start(weight_copies(0))
@@ -444,8 +431,12 @@
         pl.semaphore_signal(barrier, inc=1, device_id=peer, device_id_type=MESH)
     pl.semaphore_wait(barrier, len(peers))
 
+    def keep(t):
+        slot = parity(t)
+        return pltpu.make_async_copy(dy_tile.at[slot], dy0_hbm.at[strip(t * tile, tile)], tile_sem.at[slot, 2])
+
     def compute_tile(j, t):
-        slot, here = lax.rem(j, 2), lax.rem(t, 2)
+        slot, here = parity(j), parity(t)
         part = strip(t * tile, tile)
         wait_tile(t)
         pl.when(t + 1 < tiles)(lambda: start_tile(j, t + 1))
@@ -465,44 +456,42 @@
             turn(dy_tile, here, dyt_ref, part)
             da_ref[part, :] = jnp.zeros((tile, d), F32)
 
-    def compute_gate_up(j, s):
-        slot, u, h = lax.rem(j, gu.slots), s // (chips // 2), lax.rem(s, chips // 2)
-        g = dot(at_ref[...], dgu_ref[u, :, strip(h * 2 * LANES, 2 * LANES)]).astype(BF16)
-        for c in range(2):
-            at = strip((u * chips + 2 * h + c) * rows, rows)
+    def compute_gate_up(j, u):
+        slot = lax.rem(j, gu.slots)
+        g = dot(at_ref[...], dgu_ref[u]).astype(BF16)
+        for c in range(chips):
+            at = strip((u * chips + c) * rows, rows)
             for owner in range(CORES * chips):
                 gu.mine[slot, owner % CORES, owner // CORES, at, :] = g[owner * rows : (owner + 1) * rows, c * LANES : (c + 1) * LANES]
 
     def compute_down(j, h):
         slot = lax.rem(down_of(j), dn.slots)
-        owner = lax.rem(lax.rem(j, blocks), 2)
+        owner = parity(lax.rem(j, blocks))
+        chips_here = [2 * h, 2 * h + 1]
+        z = strip(chips_here[0] * LANES, 2 * LANES)
 
         @pl.when(~is_last(j))
         def _():
-            g = dot(dyt_ref[...], z_ref[:, strip(h * 2 * LANES, 2 * LANES)]).astype(BF16)
-            for c in range(2):
-                dn.mine[slot, owner, 2 * h + c, :, :] = g[:, c * LANES : (c + 1) * LANES]
+            g = dot(dyt_ref[...], z_ref[:, z]).astype(BF16)
+            for c, at in enumerate(chips_here):
+                dn.mine[slot, owner, at, :, :] = g[:, c * LANES : (c + 1) * LANES]
 
         @pl.when(is_last(j))
         def _():
-            g = dot(dyt_ref[...], z_ref[:, strip(h * 2 * LANES, 2 * LANES)])
-            low = lax.broadcasted_iota(jnp.int32, (small, LANES), 1) < LANES // 2
-            for c in range(2):
-                top, bottom = g[:small, c * LANES : (c + 1) * LANES], g[small:, c * LANES : (c + 1) * LANES]
-                dn.mine[slot, 0, 2 * h + c, pl.ds(0, small), :] = jnp.where(low, top, pltpu.roll(bottom, LANES // 2, 1)).astype(BF16)
-                dn.mine[slot, 1, 2 * h + c, pl.ds(0, small), :] = jnp.where(low, pltpu.roll(top, LANES // 2, 1), bottom).astype(BF16)
+            g = dot(dyt_ref[...], z_ref[:, z])
+            half = LANES // 2
+            low = lax.broadcasted_iota(jnp.int32, (small, LANES), 1) < half
+            for c, at in enumerate(chips_here):
+                both = g[:, c * LANES : (c + 1) * LANES]
+                turned = pltpu.roll(both, half, 1)
+                dn.mine[slot, 0, at, head(small), :] = jnp.where(low, both[:small], turned[small:]).astype(BF16)
+                dn.mine[slot, 1, at, head(small), :] = jnp.where(low, turned[:small], both[small:]).astype(BF16)
 
     def compute_da(j, t):
-        slot = lax.rem(j, 2)
-        part = strip(t * tile, tile)
+        slot, part = parity(j), strip(t * tile, tile)
         da_ref[part, :] += dot(dgu_ref[0, part, :], wg_ref[slot], NT) + dot(dgu_ref[1, part, :], wu_ref[slot], NT)
 
     def change_layer():
-        size = tile // 4
-
-        def keep(t):
-            return pltpu.make_async_copy(dy_tile.at[lax.rem(t, 2)], dy0_hbm.at[strip(t * tile, tile), :], tile_sem.at[lax.rem(t, 2), 2])
-
         def begin(t):
             load(h_hbm, a_tile, t, 0).start()
             load(dy_hbm, dy_tile, t, 1).start()
@@ -510,13 +499,13 @@
         begin(0)
 
         def one(t, _):
-            slot = lax.rem(t, 2)
+            slot = parity(t)
             wait_tile(t)
             pl.when(t > 0)(lambda: keep(t - 1).wait())
             pl.when(t + 1 < tiles)(lambda: begin(t + 1))
 
             def piece(i, _):
-                here, there = strip(i * size, size), strip(t * tile + i * size, size)
+                here, there = strip(i * small_tile, small_tile), strip(t * tile + i * small_tile, small_tile)
                 wide = a_tile[slot, here, :].astype(F32)
                 da = da_ref[there, :].astype(BF16).astype(F32)
                 scale = lax.rsqrt(jnp.mean(wide * wide, -1, keepdims=True) + 1e-6)
@@ -525,7 +514,7 @@
                 dy_tile[slot, here, :] = dy_tile[slot, here, :] + back
                 return 0
 
-            lax.fori_loop(0, tile // size, piece, 0)
+            lax.fori_loop(0, tile // small_tile, piece, 0)
             keep(t).start()
             turn(dy_tile, slot, dyt_ref, strip(t * tile, tile))
             return 0
@@ -539,25 +528,24 @@
     def upper_down(j, act):
         pl.when(j < (layers - 1) * blocks)(lambda: for_down(j, act))
 
+    def gu_load(n, rows):
+        start(gu_state(n))
+
+    def dn_load(n, rows):
+        start(dn_state(n, rows))
+
     events = {
-        "tile": {
-            0: [(on, gu.gather4, 4), (upper_down, dn.gather2, 3)],
-            1: [(on, gu.event2, 1)],
-            2: [(for_down, dn.event1, 1)],
-        },
-        "gate_up": {
-            0: [(on, gu.gather2, 2)],
-            2: [(for_down, dn_new, 2)],
-            3: [(on, gu.event0, 0), (on, lambda n, _: start(gu_state(n)), 1)],
-        },
-        "down": {1: [(for_down, dn.event0, 0), (upper_down, dn.gather3, 3), (on, gu.event1, 0)]},
-        "da": {
-            0: [(on, gu.gather3, 3), (on, gu_new, 1)],
-            1: [(upper_down, dn.gather4, 3), (for_down, lambda n, size: start(dn_state(n, size)), 1)],
-            2: [(for_down, dn.event2, 1)],
-        },
+        "tile0": [(on, gu.gather4, 4)],
+        "tile1": [(for_down, dn_new, 2)],
+        "tile2": [(on, gu.event2, 1)],
+        "gate0": [(for_down, dn.event2, 1), (on, gu_load, 1)],
+        "gate1": [(on, gu.event0), (upper_down, dn.gather3, 3)],
+        "down1": [(for_down, dn.event0), (upper_down, dn.gather2, 2)],
+        "back0": [(on, gu.event1)],
+        "back2": [(upper_down, dn.gather4, 3), (on, gu.gather3, 3), (on, gu.gather2, 2), (for_down, dn.event1)],
+        "back3": [(on, gu_new, 1), (for_down, dn_load, 1)],
     }
-    longest = max(ago for part in events.values() for these in part.values() for _, _, ago in these)
+    longest = max(sum(ago) for these in events.values() for _, _, *ago in these)
 
     def step(j, _):
         busy = j < steps
@@ -572,32 +560,32 @@
         def parts(name, number, active, compute):
             def one(t, _):
                 pl.when(active)(lambda: compute(j, t))
-                for at, these in events[name].items():
+                for at in range(number):
 
                     @pl.when(t == at)
                     def _():
-                        for stream, act, ago in these:
-                            stream(j - ago, act)
+                        for stream, act, *ago in events.get(f"{name}{at}", ()):
+                            stream(j - sum(ago), act)
 
                 return 0
 
             lax.fori_loop(0, number, one, 0)
 
         def da_tile(j, t):
+            fetch = load(a_hbm.at[0], a_tile, t, 0)
+            pl.when(changes)(fetch.start)
+            compute_da(j, t)
+
             @pl.when(changes)
             def _():
-                pl.when(t == 0)(lambda: load(a_hbm.at[0], a_tile, 0, 0).start())
-                load(a_hbm.at[0], a_tile, t, 0).wait()
-                pl.when(t + 1 < tiles)(lambda: load(a_hbm.at[0], a_tile, t + 1, 0).start())
-
-            compute_da(j, t)
-            pl.when(changes)(lambda: turn(a_tile, lax.rem(t, 2), at_ref, strip(t * tile, tile)))
+                fetch.wait()
+                turn(a_tile, parity(t), at_ref, strip(t * tile, tile))
 
         parts("tile", tiles, busy, compute_tile)
         pl.when(busy & (j + 1 < steps) & ~changes)(lambda: start_tile(j + 1, 0))
-        parts("gate_up", chips, busy, compute_gate_up)
+        parts("gate", 2, busy, compute_gate_up)
         parts("down", chips // 2, busy, compute_down)
-        parts("da", tiles, busy & lower, da_tile)
+        parts("back", tiles, busy & lower, da_tile)
 
         @pl.when(changes)
         def _():
@@ -612,7 +600,7 @@
     wait(own_outs(dn.number - 1, small))
 
 
-def backward(mesh, a, dy, h, weights, m, v, tile=512):
+def backward(mesh, a, h, dy, weights, m, v, tile=512):
     tokens, d = dy.shape
     layers, _, ff = weights[0].shape
     chips = mesh.shape["dp"] // CORES
@@ -676,10 +664,10 @@
             *pool(1, 2 * chips),
             *pool(2, d // LANES),
         ],
-        compiler_params=pltpu.CompilerParams(collective_id=1, has_side_effects=True, vmem_limit_bytes=VMEM_MOST),
-        cost_estimate=pl.CostEstimate(flops=28 * tokens * d * ff, bytes_accessed=24 * d * ff, transcendentals=2 * tokens * ff),
+        compiler_params=pltpu.CompilerParams(collective_id=1, has_side_effects=True, vmem_limit_bytes=VMEM_BYTES),
+        cost_estimate=cost(28 * tokens * d * ff, 24 * d * ff),
         name="backward",
-    )(a, dy, h, *weights, *m, *v)
+    )(a, h, dy, *weights, *m, *v)
 
 
 class Ring:
@@ -766,7 +754,7 @@
             pltpu.SemaphoreType.DMA((slots, 3)),
         ],
         compiler_params=pltpu.CompilerParams(vmem_limit_bytes=VMEM_BYTES),
-        cost_estimate=pl.CostEstimate(flops=COPY_FLOPS * 8 * layers * d * ff, bytes_accessed=8 * layers * d * ff, transcendentals=0),
+        cost_estimate=cost(COPY_FLOPS * 8 * layers * d * ff, 8 * layers * d * ff),
         name="place_columns",
     )(x)
 
@@ -795,8 +783,7 @@
     def work(unit, slot):
         for i in range(3):
             g = g_in[i][slot].astype(F32)
-            s_out[i][slot, 0] = 0.9 * s_in[i][slot, 0] + 0.1 * g
-            s_out[i][slot, 1] = 0.95 * s_in[i][slot, 1] + 0.05 * g * g
+            s_out[i][slot, 0], s_out[i][slot, 1] = moment(s_in[i][slot, 0], s_in[i][slot, 1], g)
 
     ring = Ring(layers * parts, slots, loads, stores, work)
     ring.begin()
@@ -820,7 +807,7 @@
             pltpu.SemaphoreType.DMA((slots, 15)),
         ],
         compiler_params=pltpu.CompilerParams(vmem_limit_bytes=VMEM_BYTES),
-        cost_estimate=pl.CostEstimate(flops=COPY_FLOPS * 18 * size, bytes_accessed=18 * size, transcendentals=0),
+        cost_estimate=cost(COPY_FLOPS * 18 * size, 18 * size),
         name="moments",
     )(*m, *v, *g)
 
@@ -834,21 +821,16 @@
     half = LANES // 2
     chip, core = me_ref[0] // CORES, lax.rem(me_ref[0], CORES)
 
-    def owner(hops, flip):
-        return lax.rem(chip + hops + chips, chips) * CORES + (1 - core if flip else core)
-
-    starts = [owner(hops, flip) * height for flip in (0, 1) for hops in (0, -1, 1)] + [owner(2, 0) * height + part * (height // 2) for part in (0, 1)]
-    fetch, put = [], []
-    for i, (piece, start) in enumerate(zip(pieces, starts)):
-        size = piece.shape[0]
-        fetch.append(pltpu.make_async_copy(piece, held.at[i, pl.ds(0, size)], held_sem.at[i, 0]))
-        put.append(pltpu.make_async_copy(held.at[i, pl.ds(0, size)], down_hbm.at[0, pl.ds(pl.multiple_of(start, 32), size), :], held_sem.at[i, 1]))
+    owners = [lax.rem(chip + hops + chips, chips) * CORES + (1 - core if flip else core) for flip in range(2) for hops in (0, -1, 1)]
+    owners.append(lax.rem(chip + 2, chips) * CORES + core)
+    fetch = [pltpu.make_async_copy(piece, held.at[i], held_sem.at[i, 0]) for i, piece in enumerate(pieces)]
+    put = [pltpu.make_async_copy(held.at[i], down_hbm.at[0, strip(owner * height, height), :], held_sem.at[i, 1]) for i, owner in enumerate(owners)]
 
     def loads(unit, slot):
         layer, device = layers - 2 - unit // devices, lax.rem(unit, devices)
         return [
-            pltpu.make_async_copy(x_hbm.at[layer, pl.ds(0, pairs), device], r_in.at[slot, pl.ds(0, pairs)], sem.at[slot, 0]),
-            pltpu.make_async_copy(x_hbm.at[layer, pairs, device, pl.ds(0, d // 2)], r_in.at[slot, pairs, pl.ds(0, d // 2)], sem.at[slot, 1]),
+            pltpu.make_async_copy(x_hbm.at[layer, head(pairs), device], r_in.at[slot, head(pairs)], sem.at[slot, 0]),
+            pltpu.make_async_copy(x_hbm.at[layer, pairs, device, head(d // 2)], r_in.at[slot, pairs, head(d // 2)], sem.at[slot, 1]),
         ]
 
     def stores(unit, slot):
@@ -858,22 +840,30 @@
     def work(unit, slot):
         low = lax.rem(unit, CORES)
         for b in range(d // LANES):
-            there = pl.ds(b * LANES, LANES)
+            there = lanes(b)
             for n in range(pairs):
-                r_out[slot, pl.ds(pl.multiple_of(n * LANES + low * half, half), LANES), there] = r_in[slot, n, pl.ds(b * LANES, LANES), :]
+                r_out[slot, pl.ds(pl.multiple_of(n * LANES + low * half, half), LANES), there] = r_in[slot, n, lanes(b), :]
             r_out[slot, pl.ds(pl.multiple_of(pairs * LANES * (1 - low), half), half), there] = r_in[slot, pairs, pl.ds(b * half, half), :]
 
-    for copy in fetch:
-        copy.start()
+    both = fetch[len(owners) - 1 :]
+    start(fetch[: len(owners) - 1])
+    for k in range(CORES):
+        pl.when(core == k)(both[k].start)
     ring = Ring((layers - 1) * devices, slots, loads, stores, work)
     ring.begin()
-    for one, other in zip(fetch, put):
+    for one, other in zip(fetch, put[:-1]):
         one.wait()
         other.start()
+    for k in range(CORES):
+
+        @pl.when(core == k)
+        def _():
+            both[k].wait()
+            pltpu.make_async_copy(held.at[len(owners) - 1 + k], put[-1].dst_ref, held_sem.at[len(owners) - 1, 1]).start()
+
     ring.run()
     ring.end()
-    for copy in put:
-        copy.wait()
+    wait(put)
 
 
 def place_rows(me, chunks, pieces, layers, d, ff, slots=4):
@@ -893,39 +883,40 @@
             pltpu.SemaphoreType.DMA((len(pieces), 2)),
         ],
         compiler_params=pltpu.CompilerParams(vmem_limit_bytes=VMEM_BYTES),
-        cost_estimate=pl.CostEstimate(flops=COPY_FLOPS * 4 * layers * d * ff, bytes_accessed=4 * layers * d * ff, transcendentals=0),
+        cost_estimate=cost(COPY_FLOPS * 4 * layers * d * ff, 4 * layers * d * ff),
         name="place_rows",
     )(me, x, *pieces)
 
 
-def place_last_kernel(me_ref, top_hbm, bottom_hbm, _, down_hbm, held, sem):
-    half = top_hbm.shape[0]
-    chips = down_hbm.shape[1] // (2 * half * CORES)
-    owner = lax.rem(me_ref[0] // CORES + 2, chips) * CORES + 1 - lax.rem(me_ref[0], CORES)
-    fetch, put = [], []
-    for i, piece in enumerate((top_hbm, bottom_hbm)):
-        fetch.append(pltpu.make_async_copy(piece, held.at[i], sem.at[i, 0]))
-        put.append(pltpu.make_async_copy(held.at[i], down_hbm.at[0, pl.ds(pl.multiple_of((2 * owner + i) * half, 32), half), :], sem.at[i, 1]))
-    for copy in fetch:
-        copy.start()
-    for one, other in zip(fetch, put):
-        one.wait()
-        other.start()
-    for copy in put:
-        copy.wait()
-
-
-def place_last(me, top, bottom, down):
+def place_last_kernel(me_ref, even_hbm, odd_hbm, _, down_hbm, held, sem):
+    height = even_hbm.shape[0]
+    chips = down_hbm.shape[1] // (height * CORES)
+    core = lax.rem(me_ref[0], CORES)
+    owner = lax.rem(me_ref[0] // CORES + 2, chips) * CORES + 1 - core
+    for k, piece in enumerate((odd_hbm, even_hbm)):
+
+        @pl.when(core == k)
+        def _():
+            fetch = pltpu.make_async_copy(piece, held, sem)
+            fetch.start()
+            fetch.wait()
+
+    put = pltpu.make_async_copy(held, down_hbm.at[0, strip(owner * height, height), :], sem)
+    put.start()
+    put.wait()
+
+
+def place_last(me, even, odd, down):
     return pl.pallas_call(
         place_last_kernel,
         in_specs=[pl.BlockSpec(memory_space=pltpu.SMEM)] + [ANY] * 3,
         out_specs=ANY,
         out_shape=jax.ShapeDtypeStruct(down.shape, BF16),
         input_output_aliases={3: 0},
-        scratch_shapes=[pltpu.VMEM((2, *top.shape), BF16), pltpu.SemaphoreType.DMA((2, 2))],
-        cost_estimate=pl.CostEstimate(flops=COPY_FLOPS * 4 * top.size, bytes_accessed=8 * top.size, transcendentals=0),
+        scratch_shapes=[pltpu.VMEM(even.shape, BF16), pltpu.SemaphoreType.DMA],
+        cost_estimate=cost(COPY_FLOPS * 4 * even.size, 4 * even.size),
         name="place_last",
-    )(me, top, bottom, down)
+    )(me, even, odd, down)
 
 
 def solution(mesh):
@@ -937,10 +928,8 @@
     def step(x, dy, *arrays):
         weights, m, v = (arrays[i : i + 3] for i in (0, 3, 6))
         layers, d, ff = weights[0].shape
-        x, dy = x[0], dy[0]
         me = lax.axis_index("dp").reshape(1)
-        a, h = forward(x, *weights, 0)
-        *sums, columns, rows, own, _ = backward(mesh, a, dy, h, weights, m, v)
+        *sums, columns, rows, own, _ = backward(mesh, *forward(x[0], *weights, 0), dy[0], weights, m, v)
 
         def send(block, to):
             return lax.ppermute(block, "dp", to)
@@ -948,12 +937,11 @@
         near = [own, send(own, right), send(own, left)]
         gate, up = place_columns(columns, layers, d, ff)
         gate, *near[1:] = lax.optimization_barrier((gate, *near[1:]))
-        half = own.shape[0] // 2
-        far = [send(near[1][:half], right), send(near[2][half:], left)]
+        far = [send(near[1], right[::CORES]), send(near[2], left[1::CORES])]
         other = [send(block, swap) for block in near]
         first, *states = moments(m, v, sums)
         first, *far = lax.optimization_barrier((first, *far))
-        last = [send(block, swap) for block in far]
+        last = [send(block, swap[k::CORES]) for k, block in enumerate(far)]
         down = place_rows(me, rows, near + other + far, layers, d, ff)
         return (gate, up, place_last(me, *last, down), first, *states)
 

time: 701 us -> 706 us (level)
  starting transfers between devices: 6.22 us -> 16.1 us
    ppermute x9, starting transfers between devices: 6.22 us -> 16.1 us  [send(): return lax.ppermute(block, 'dp', to)]
where the time goes in v3:
time: 706 us
  Pallas kernels  688 us (97%)
  starting transfers between devices  16.1 us (2%)
    pallas_call x1, Pallas kernels, backward(): pl.pallas_call(functools.partial(backward_kernel, chips, tile), out_shape...  530 us
    pallas_call x1, Pallas kernels, forward(): pl.pallas_call(functools.partial(forward_kernel, tile), grid=(ff // width...  87.3 us
    pallas_call x1, Pallas kernels, place_columns(): pl.pallas_call(functools.partial(place_columns_kernel, layers, slots), in...  28.9 us
    pallas_call x1, Pallas kernels, moments(): pl.pallas_call(functools.partial(moments_kernel, layers, parts, slots), i...  24.6 us
    ppermute x9, starting transfers between devices, send(): return lax.ppermute(block, 'dp', to)  16.1 us
    pallas_call x1, Pallas kernels, place_rows(): pl.pallas_call(functools.partial(place_rows_kernel, layers, slots), in_sp...  15.3 us
  transfers between devices with their start and end apart: 9, of which 1 were waited for; matrix products, arithmetic and copies ran while one was open for 0% of the time, Pallas kernels for 10%

profile of v3, /device:TPU:113, one launch (start us, length us, event | category | flops | bytes accessed | tf_op | source)
XLA Modules:
  0.0 705.7 jit_solution(17300934099447407323)
XLA Ops:
  0.6 87.3 %forward.1 = (bf16[2,2048,1152]{2,1,0:T(8,128)(2,1)}, bf16[2048,1152]{1,0:T(8,128)(2,1)}) custom-call(bf16[2048,1152]{1,0:T(8,128)(2,1)} %bitcast.5, bf16[2,1152,4608]{2,1,0:T(8,128)(2,1)} %refs_3_.2, bf16[2,1152,4608]{2,1,0:T(8,128)(2,1)} %refs_4_.2, bf16[2,4608,1152]{2,1,0:T(8,128)(2,1)} %refs_5_.2), custom_call_target="tpu_custom_call" | custom-call | flops 65229815808 | bytes 31850496 | tf_op jit(solution)/shard_map/forward/pallas_call | solution.py:116
  88.0 529.7 %backward.1 = (bf16[2,144,4608]{2,1,0:T(8,128)(2,1)}, bf16[2,144,4608]{2,1,0:T(8,128)(2,1)}, bf16[2,576,1152]{2,1,0:T(8,128)(2,1)}, bf16[18,8,1152,128]{3,2,1,0:...) custom-call(bf16[2,2048,1152]{2,1,0:T(8,128)(2,1)} %get-tuple-element.31.ref, ...), custom_call_target="tpu_custom_call" | custom-call | flops 304405807104 | bytes 127401984 | tf_op jit(solution)/shard_map/backward/pallas_call | solution.py:641
  617.7 0.8 collective-permute-start
  618.4 2.0 collective-permute-start.1
  620.5 28.9 %place_columns.1 = (bf16[2,1152,4608]{2,1,0:T(8,128)(2,1)}, bf16[2,1152,4608]{2,1,0:T(8,128)(2,1)}) custom-call(bf16[2,9,8,2,4,144,128]{6,5,4,3,2,1,0:T(8,128)(2,1)} %bitcast.7), custom_call_target="tpu_custom_call" | custom-call | flops 5435817984 | bytes 84934656 | tf_op jit(solution)/shard_map/place_columns/pallas_call | solution.py:746
  649.4 0.5 collective-permute-done.refs_1_
  649.8 0.0 collective-permute-done.1.refs_2_
  649.9 1.7 collective-permute-start.2
  651.6 4.3 collective-permute-start.3
  655.9 0.1 collective-permute-start.6
  656.0 0.5 collective-permute-start.7
  656.5 0.1 collective-permute-start.8
  656.6 24.6 %moments.1 = (f32[2,144,4608]{2,1,0:T(8,128)}, f32[2,144,4608]{2,1,0:T(8,128)}, f32[2,576,1152]{2,1,0:T(8,128)}, f32[2,144,4608]{2,1,0:T(8,128)}, f32[2,144,4608]{2,1,0:T(8,128)}, /*index=5*/f32[2,576,1152]{2,1,0:T(8,128)}) custom-call(f32[2,144,4608]{2,1,0:T(8,128)} %refs_0_.1, f32[2,144,4608]{2,1,0:T(8,128)} %refs_1_.1, f32[2,576,1152]{2,1,0:T(8,128)} %refs_2_.1, ...), custom_call_target="tpu_custom_call" | custom-call | flops 4586471424 | bytes 71663616 | tf_op jit(solution)/shard_map/moments/pallas_call | solution.py:798
  681.1 0.0 collective-permute-done.2.refs_6_
  681.2 0.0 collective-permute-done.3.refs_7_
  681.2 1.3 collective-permute-start.4
  682.5 5.3 collective-permute-start.5
  687.8 0.0 collective-permute-done.6.refs_3_
  687.8 0.0 collective-permute-done.7.refs_4_
  687.8 0.0 collective-permute-done.8.refs_5_
  687.8 15.3 %place_rows.1._ = bf16[2,4608,1152]{2,1,0:T(8,128)(2,1)} custom-call(s32[1]{0:T(128)} %bitcast.3.me_ref, bf16[1,5,8,1152,128]{4,3,2,1,0:T(8,128)(2,1)} %bitcast.8, bf16[576,1152]{1,0:T(8,128)(2,1)} %get-tuple-element.35.refs_0_, bf16[576,1152]{1,0:T(8,128)(2,1)} %collective-permute-done.refs_1_, bf16[576,1152]{1,0:T(8,128)(2,1)} %collective-permute-done.1.refs_2_, ...), custom_call_target="tpu_custom_call" | custom-call | flops 2717908992 | bytes 42467328 | tf_op jit(solution)/shard_map/place_rows/pallas_call | solution.py:873
  703.1 0.0 collective-permute-done.4.even_hbm
  703.1 0.0 collective-permute-done.5.odd_hbm
  703.2 2.4 place_last.1
Async XLA Ops:
  617.7 32.1 %collective-permute-start = (bf16[576,1152]{1,0:T(8,128)(2,1)}, bf16[576,1152]{1,0:T(8,128)(2,1)}, u32[]{:S(2)}, u32[]{:S(2)}) collective-permute-start(bf16[576,1152]{1,0:T(8,128)(2,1)} %get-tuple-element.35.refs_0_), channel_id=1, source_target_pairs={{0,2},{1,3},{2,4},{3,5},{4,6},{5,7},{6,0},{7,1},{8,10},{9,11},{10,... | collective-permute-start | bytes 3981320 | tf_op jit(solution)/shard_map/ppermute | solution.py:935
  618.4 31.4 %collective-permute-start.1 = (bf16[576,1152]{1,0:T(8,128)(2,1)}, bf16[576,1152]{1,0:T(8,128)(2,1)}, u32[]{:S(2)}, u32[]{:S(2)}) collective-permute-start(bf16[576,1152]{1,0:T(8,128)(2,1)} %get-tuple-element.35.refs_0_), channel_id=1, source_target_pairs={{0,6},{1,7},{2,0},{3,1},{4,2},{5,3},{6,4},{7,5},{8,14},{9,15},{10,... | collective-permute-start | bytes 3981320 | tf_op jit(solution)/shard_map/ppermute | solution.py:935
  649.9 31.3 %collective-permute-start.2 = (bf16[576,1152]{1,0:T(8,128)(2,1)}, bf16[576,1152]{1,0:T(8,128)(2,1)}, u32[]{:S(2)}, u32[]{:S(2)}) collective-permute-start(bf16[576,1152]{1,0:T(8,128)(2,1)} %collective-permute-done.refs_1_), channel_id=1, source_target_pairs={{0,2},{2,4},{4,6},{6,0},{8,10},{10,12},{12,14},{14,8}} | collective-permute-start | bytes 3981320 | tf_op jit(solution)/shard_map/ppermute | solution.py:935
  651.6 29.6 %collective-permute-start.3 = (bf16[576,1152]{1,0:T(8,128)(2,1)}, bf16[576,1152]{1,0:T(8,128)(2,1)}, u32[]{:S(2)}, u32[]{:S(2)}) collective-permute-start(bf16[576,1152]{1,0:T(8,128)(2,1)} %collective-permute-done.1.refs_2_), channel_id=1, source_target_pairs={{1,7},{3,1},{5,3},{7,5},{9,15},{11,9},{13,11},{15,13}} | collective-permute-start | bytes 3981320 | tf_op jit(solution)/shard_map/ppermute | solution.py:935
  655.9 31.9 %collective-permute-start.6 = (bf16[576,1152]{1,0:T(8,128)(2,1)}, bf16[576,1152]{1,0:T(8,128)(2,1)}, u32[]{:S(2)}, u32[]{:S(2)}) collective-permute-start(bf16[576,1152]{1,0:T(8,128)(2,1)} %get-tuple-element.35.refs_0_), channel_id=1, source_target_pairs={{0,1},{1,0},{2,3},{3,2},{4,5},{5,4},{6,7},{7,6},{8,9},{9,8},{10,11... | collective-permute-start | bytes 3981320 | tf_op jit(solution)/shard_map/ppermute | solution.py:935
  656.0 31.8 %collective-permute-start.7 = (bf16[576,1152]{1,0:T(8,128)(2,1)}, bf16[576,1152]{1,0:T(8,128)(2,1)}, u32[]{:S(2)}, u32[]{:S(2)}) collective-permute-start(bf16[576,1152]{1,0:T(8,128)(2,1)} %collective-permute-done.refs_1_), channel_id=1, source_target_pairs={{0,1},{1,0},{2,3},{3,2},{4,5},{5,4},{6,7},{7,6},{8,9},{9,8},{10,11... | collective-permute-start | bytes 3981320 | tf_op jit(solution)/shard_map/ppermute | solution.py:935
  656.5 31.3 %collective-permute-start.8 = (bf16[576,1152]{1,0:T(8,128)(2,1)}, bf16[576,1152]{1,0:T(8,128)(2,1)}, u32[]{:S(2)}, u32[]{:S(2)}) collective-permute-start(bf16[576,1152]{1,0:T(8,128)(2,1)} %collective-permute-done.1.refs_2_), channel_id=1, source_target_pairs={{0,1},{1,0},{2,3},{3,2},{4,5},{5,4},{6,7},{7,6},{8,9},{9,8},{10,11... | collective-permute-start | bytes 3981320 | tf_op jit(solution)/shard_map/ppermute | solution.py:935
  681.2 22.0 %collective-permute-start.4 = (bf16[576,1152]{1,0:T(8,128)(2,1)}, bf16[576,1152]{1,0:T(8,128)(2,1)}, u32[]{:S(2)}, u32[]{:S(2)}) collective-permute-start(bf16[576,1152]{1,0:T(8,128)(2,1)} %collective-permute-done.2.refs_6_), channel_id=1, source_target_pairs={{0,1},{2,3},{4,5},{6,7},{8,9},{10,11},{12,13},{14,15}} | collective-permute-start | bytes 3981320 | tf_op jit(solution)/shard_map/ppermute | solution.py:935
  682.5 20.7 %collective-permute-start.5 = (bf16[576,1152]{1,0:T(8,128)(2,1)}, bf16[576,1152]{1,0:T(8,128)(2,1)}, u32[]{:S(2)}, u32[]{:S(2)}) collective-permute-start(bf16[576,1152]{1,0:T(8,128)(2,1)} %collective-permute-done.3.refs_7_), channel_id=1, source_target_pairs={{1,0},{3,2},{5,4},{7,6},{9,8},{11,10},{13,12},{15,14}} | collective-permute-start | bytes 3981320 | tf_op jit(solution)/shard_map/ppermute | solution.py:935

commit v4 on v3

--- a/solution.py
+++ b/solution.py
@@ -207,20 +207,22 @@
         self.take(n >= self.lanes, (3, 4))
         start(self.copies2(n, rows))
 
+    def total(self, n, start, size):
+        total = self.both(n, 0, start, size)
+        for side, _ in SIDES:
+            total += self.near[lax.rem(n, self.lanes), side, pl.ds(start, size), :].astype(F32)
+        return total.astype(BF16).astype(F32)
+
     def event3(self, n, rows):
-        slot = lax.rem(n, self.lanes)
         wait(self.copies2(n, rows))
-        total = self.both(n, 0, 0, rows)
-        for side, _ in SIDES:
-            total += self.near[slot, side, head(rows)].astype(F32)
+
+    def after3(self, n):
         pl.when(n + self.slots < self.number)(lambda: self.give(0, self.partner()))
 
         @pl.when(n + self.lanes < self.number)
         def _():
             for side, hop in SIDES:
                 self.give(3 + side, self.device(-hop))
-
-        return total.astype(BF16).astype(F32)
 
     def block(self, n, hops, core, start, size):
         return self.gathered.at[n, self.index(self.chip + hops, core), pl.ds(start, size), :]
@@ -388,34 +390,57 @@
             at = pl.ds(pl.multiple_of(me * (d // 2) + start, LANES // 2), height)
             yield pltpu.make_async_copy(wd_hbm.at[layer, at, there], w_ref.at[here, :], state_sem.at[3 * b + 2])
 
-    def gu_new(n, rows):
-        g = gu.event3(n, rows)
+    some = d // 3
+
+    def gu_new(n, size):
+        gu.event3(n, size)
         pl.when(n > 0)(lambda: wait(gu_outs(n - 1)))
-        gu.sum[...] = g.astype(BF16)
+        wait(gu_state(n))
+
+        def piece(i, _):
+            at = strip(i * some, some)
+            g = gu.total(n, i * some, some)
+            gu.sum[at, :] = g.astype(BF16)
+            gu.new[at, :] = adam(w_ref[at, :], m_ref[at, :], v_ref[at, :], g)
+            return i
+
+        lax.fori_loop(0, size // some, piece, 0)
+        gu.after3(n)
         start(gu_outs(n))
-        wait(gu_state(n))
-        gu.new[...] = adam(w_ref[...], m_ref[...], v_ref[...], g)
-        gu.gather1(n, rows)
+        gu.gather1(n, size)
 
     def dn_new(n, size):
-        g = dn.event3(n, size).T
         half, height = LANES // 2, size // lane_blocks
-        if size == small:
-            g = jnp.concatenate([g[:half], g[half:]], 1)
+        dn.event3(n, size)
         if size == full:
-            pl.when((n > 0) & (lax.rem(n, pairs + 1) > 0))(lambda: wait(dn_outs(n - 1, full)))
-            pl.when((n > 0) & (lax.rem(n, pairs + 1) == 0))(lambda: wait(dn_outs(n - 1, small)))
+            begins = lax.rem(n, pairs + 1) == 0
+            pl.when((n > 0) & ~begins)(lambda: wait(dn_outs(n - 1, full)))
+            pl.when((n > 0) & begins)(lambda: wait(dn_outs(n - 1, small)))
         else:
             wait(dn_outs(n - 1, full))
-        for b in range(lane_blocks):
-            dn.sum[pl.ds(b * height, height), :] = g[:, b * LANES : (b + 1) * LANES].astype(BF16)
-        start(dn_outs(n, size))
         wait(dn_state(n, size))
         upper = n < (layers - 1) * (pairs + 1)
         pl.when(n > (layers - 1) * (pairs + 1))(lambda: wait(own_outs(n - 1, full)))
-        for b in range(lane_blocks):
-            here = pl.ds(b * height, height)
-            dn.new[here, :] = adam(w_ref[here, :], m_ref[here, :], v_ref[here, :], g[:, b * LANES : (b + 1) * LANES])
+
+        def finish(at, g):
+            dn.sum[at, :] = g.astype(BF16)
+            dn.new[at, :] = adam(w_ref[at, :], m_ref[at, :], v_ref[at, :], g)
+
+        if size == full:
+
+            def piece(i, _):
+                for start in range(0, some, LANES):
+                    finish(strip(i * some + start, LANES), dn.total(n, i * some + start, LANES).T)
+                return i
+
+            lax.fori_loop(0, size // some, piece, 0)
+        else:
+            g = dn.total(n, 0, size).T
+            g = jnp.concatenate([g[:half], g[half:]], 1)
+            for b in range(lane_blocks):
+                finish(pl.ds(b * height, height), g[:, b * LANES : (b + 1) * LANES])
+        dn.after3(n)
+        start(dn_outs(n, size))
         pl.when(upper)(lambda: dn.gather1(n, size))
         pl.when(~upper)(lambda: start(own_outs(n, size)))
 
@@ -456,11 +481,11 @@
             turn(dy_tile, here, dyt_ref, part)
             da_ref[part, :] = jnp.zeros((tile, d), F32)
 
-    def compute_gate_up(j, u):
-        slot = lax.rem(j, gu.slots)
-        g = dot(at_ref[...], dgu_ref[u]).astype(BF16)
-        for c in range(chips):
-            at = strip((u * chips + c) * rows, rows)
+    def compute_gate_up(j, s):
+        slot, u, h = lax.rem(j, gu.slots), s // (chips // 2), 2 * lax.rem(s, chips // 2)
+        g = dot(at_ref[...], dgu_ref[u, :, strip(h * LANES, 2 * LANES)]).astype(BF16)
+        for c in range(2):
+            at = strip((u * chips + h + c) * rows, rows)
             for owner in range(CORES * chips):
                 gu.mine[slot, owner % CORES, owner // CORES, at, :] = g[owner * rows : (owner + 1) * rows, c * LANES : (c + 1) * LANES]
 
@@ -535,15 +560,16 @@
         start(dn_state(n, rows))
 
     events = {
-        "tile0": [(on, gu.gather4, 4)],
         "tile1": [(for_down, dn_new, 2)],
-        "tile2": [(on, gu.event2, 1)],
-        "gate0": [(for_down, dn.event2, 1), (on, gu_load, 1)],
-        "gate1": [(on, gu.event0), (upper_down, dn.gather3, 3)],
-        "down1": [(for_down, dn.event0), (upper_down, dn.gather2, 2)],
-        "back0": [(on, gu.event1)],
-        "back2": [(upper_down, dn.gather4, 3), (on, gu.gather3, 3), (on, gu.gather2, 2), (for_down, dn.event1)],
-        "back3": [(on, gu_new, 1), (for_down, dn_load, 1)],
+        "tile3": [(on, gu.gather3, 3), (on, gu.event2, 1)],
+        "gate0": [(on, gu_load, 1)],
+        "gate3": [(on, gu.event0), (for_down, dn.event2, 1)],
+        "down0": [(on, gu.gather4, 3)],
+        "down1": [(for_down, dn.event0), (upper_down, dn.gather3, 3)],
+        "back0": [(on, gu.gather2, 2)],
+        "back1": [(upper_down, dn.gather2, 2)],
+        "back2": [(on, gu.event1), (for_down, dn.event1)],
+        "back3": [(upper_down, dn.gather4, 3), (on, gu_new, 1), (for_down, dn_load, 1)],
     }
     longest = max(sum(ago) for these in events.values() for _, _, *ago in these)
 
@@ -583,7 +609,7 @@
 
         parts("tile", tiles, busy, compute_tile)
         pl.when(busy & (j + 1 < steps) & ~changes)(lambda: start_tile(j + 1, 0))
-        parts("gate", 2, busy, compute_gate_up)
+        parts("gate", chips, busy, compute_gate_up)
         parts("down", chips // 2, busy, compute_down)
         parts("back", tiles, busy & lower, da_tile)
 
@@ -739,7 +765,7 @@
     ring.end()
 
 
-def place_columns(chunks, layers, d, ff, slots=4, some=2):
+def place_columns(chunks, layers, d, ff, slots=8, some=2):
     devices = chunks.shape[1]
     chips, rows = devices // CORES, d // devices
     x = chunks.reshape(layers, -1, devices, 2, chips, rows, LANES)
@@ -791,7 +817,7 @@
     ring.end()
 
 
-def moments(m, v, g, parts=9, slots=4):
+def moments(m, v, g, parts=9, slots=8):
     layers = m[0].shape[0]
     shapes = [(one.shape[1], one.shape[2] // parts) for one in m[:2]] + [(m[2].shape[1] // parts, m[2].shape[2])]
     size = sum(one.size for one in m)
@@ -812,19 +838,11 @@
     )(*m, *v, *g)
 
 
-def place_rows_kernel(layers, slots, me_ref, x_hbm, *refs):
-    pieces, down_hbm, (r_in, r_out, held, sem, held_sem) = refs[:-6], refs[-6], refs[-5:]
+def place_rows_kernel(layers, slots, x_hbm, down_hbm, r_in, r_out, sem):
     devices = x_hbm.shape[2]
     pairs = x_hbm.shape[1] - 1
     height, d = r_out.shape[1:]
-    chips = devices // CORES
     half = LANES // 2
-    chip, core = me_ref[0] // CORES, lax.rem(me_ref[0], CORES)
-
-    owners = [lax.rem(chip + hops + chips, chips) * CORES + (1 - core if flip else core) for flip in range(2) for hops in (0, -1, 1)]
-    owners.append(lax.rem(chip + 2, chips) * CORES + core)
-    fetch = [pltpu.make_async_copy(piece, held.at[i], held_sem.at[i, 0]) for i, piece in enumerate(pieces)]
-    put = [pltpu.make_async_copy(held.at[i], down_hbm.at[0, strip(owner * height, height), :], held_sem.at[i, 1]) for i, owner in enumerate(owners)]
 
     def loads(unit, slot):
         layer, device = layers - 2 - unit // devices, lax.rem(unit, devices)
@@ -835,88 +853,72 @@
 
     def stores(unit, slot):
         layer, device = unit // devices + 1, lax.rem(unit, devices)
-        return [pltpu.make_async_copy(r_out.at[slot], down_hbm.at[layer, strip(device * height, height), :], sem.at[slot, 2])]
+        return [pltpu.make_async_copy(r_out.at[slot], down_hbm.at[layer, strip(device * height, height)], sem.at[slot, 2])]
 
     def work(unit, slot):
         low = lax.rem(unit, CORES)
         for b in range(d // LANES):
-            there = lanes(b)
             for n in range(pairs):
-                r_out[slot, pl.ds(pl.multiple_of(n * LANES + low * half, half), LANES), there] = r_in[slot, n, lanes(b), :]
-            r_out[slot, pl.ds(pl.multiple_of(pairs * LANES * (1 - low), half), half), there] = r_in[slot, pairs, pl.ds(b * half, half), :]
-
-    both = fetch[len(owners) - 1 :]
-    start(fetch[: len(owners) - 1])
-    for k in range(CORES):
-        pl.when(core == k)(both[k].start)
+                r_out[slot, pl.ds(pl.multiple_of(n * LANES + low * half, half), LANES), lanes(b)] = r_in[slot, n, lanes(b), :]
+            r_out[slot, pl.ds(pl.multiple_of(pairs * LANES * (1 - low), half), half), lanes(b)] = r_in[slot, pairs, pl.ds(b * half, half), :]
+
     ring = Ring((layers - 1) * devices, slots, loads, stores, work)
     ring.begin()
-    for one, other in zip(fetch, put[:-1]):
-        one.wait()
-        other.start()
-    for k in range(CORES):
-
-        @pl.when(core == k)
-        def _():
-            both[k].wait()
-            pltpu.make_async_copy(held.at[len(owners) - 1 + k], put[-1].dst_ref, held_sem.at[len(owners) - 1, 1]).start()
-
     ring.run()
     ring.end()
-    wait(put)
-
-
-def place_rows(me, chunks, pieces, layers, d, ff, slots=4):
-    number, devices, _, _ = chunks.shape
+
+
+def place_rows(chunks, layers, d, ff, slots=8):
+    devices = chunks.shape[1]
     x = chunks.reshape(layers - 1, -1, devices, d, LANES)
     height = ff // devices
     return pl.pallas_call(
         functools.partial(place_rows_kernel, layers, slots),
-        in_specs=[pl.BlockSpec(memory_space=pltpu.SMEM)] + [ANY] * (1 + len(pieces)),
+        in_specs=[ANY],
         out_specs=ANY,
         out_shape=jax.ShapeDtypeStruct((layers, ff, d), BF16),
         scratch_shapes=[
             pltpu.VMEM((slots, x.shape[1], d, LANES), BF16),
             pltpu.VMEM((slots, height, d), BF16),
-            pltpu.VMEM((len(pieces), height, d), BF16),
             pltpu.SemaphoreType.DMA((slots, 3)),
-            pltpu.SemaphoreType.DMA((len(pieces), 2)),
         ],
         compiler_params=pltpu.CompilerParams(vmem_limit_bytes=VMEM_BYTES),
-        cost_estimate=cost(COPY_FLOPS * 4 * layers * d * ff, 4 * layers * d * ff),
+        cost_estimate=cost(COPY_FLOPS * 4 * d * ff, 4 * d * ff),
         name="place_rows",
-    )(me, x, *pieces)
-
-
-def place_last_kernel(me_ref, even_hbm, odd_hbm, _, down_hbm, held, sem):
-    height = even_hbm.shape[0]
+    )(x)
+
+
+def place_blocks_kernel(wheres, me_ref, *refs):
+    blocks, (down_hbm, held, sem) = refs[:-4], refs[-3:]
+    height = held.shape[1]
     chips = down_hbm.shape[1] // (height * CORES)
-    core = lax.rem(me_ref[0], CORES)
-    owner = lax.rem(me_ref[0] // CORES + 2, chips) * CORES + 1 - core
-    for k, piece in enumerate((odd_hbm, even_hbm)):
-
-        @pl.when(core == k)
-        def _():
-            fetch = pltpu.make_async_copy(piece, held, sem)
-            fetch.start()
-            fetch.wait()
-
-    put = pltpu.make_async_copy(held, down_hbm.at[0, strip(owner * height, height), :], sem)
-    put.start()
-    put.wait()
-
-
-def place_last(me, even, odd, down):
+    chip, core = me_ref[0] // CORES, lax.rem(me_ref[0], CORES)
+    fetch, put = [], []
+    for i, (block, (hops, flip)) in enumerate(zip(blocks, wheres)):
+        owner = lax.rem(chip + hops + chips, chips) * CORES + (1 - core if flip else core)
+        fetch.append(pltpu.make_async_copy(block, held.at[i], sem.at[i, 0]))
+        put.append(pltpu.make_async_copy(held.at[i], down_hbm.at[0, strip(owner * height, height)], sem.at[i, 1]))
+    start(fetch)
+    for one, other in zip(fetch, put):
+        one.wait()
+        other.start()
+    wait(put)
+
+
+def place_blocks(me, blocks, down):
+    wheres, blocks = tuple(blocks), list(blocks.values())
+    size = blocks[0].size * len(blocks)
     return pl.pallas_call(
-        place_last_kernel,
-        in_specs=[pl.BlockSpec(memory_space=pltpu.SMEM)] + [ANY] * 3,
+        functools.partial(place_blocks_kernel, wheres),
+        in_specs=[pl.BlockSpec(memory_space=pltpu.SMEM)] + [ANY] * (len(blocks) + 1),
         out_specs=ANY,
         out_shape=jax.ShapeDtypeStruct(down.shape, BF16),
-        input_output_aliases={3: 0},
-        scratch_shapes=[pltpu.VMEM(even.shape, BF16), pltpu.SemaphoreType.DMA],
-        cost_estimate=cost(COPY_FLOPS * 4 * even.size, 4 * even.size),
-        name="place_last",
-    )(me, even, odd, down)
+        input_output_aliases={len(blocks) + 1: 0},
+        scratch_shapes=[pltpu.VMEM((len(blocks), *blocks[0].shape), BF16), pltpu.SemaphoreType.DMA((len(blocks), 2))],
+        compiler_params=pltpu.CompilerParams(vmem_limit_bytes=VMEM_BYTES),
+        cost_estimate=cost(COPY_FLOPS * 4 * size, 4 * size),
+        name="place_blocks",
+    )(me, *blocks, down)
 
 
 def solution(mesh):
@@ -934,16 +936,19 @@
         def send(block, to):
             return lax.ppermute(block, "dp", to)
 
-        near = [own, send(own, right), send(own, left)]
+        from_left, from_right = send(own, right), send(own, left)
         gate, up = place_columns(columns, layers, d, ff)
-        gate, *near[1:] = lax.optimization_barrier((gate, *near[1:]))
-        far = [send(near[1], right[::CORES]), send(near[2], left[1::CORES])]
-        other = [send(block, swap) for block in near]
+        gate, from_left, from_right = lax.optimization_barrier((gate, from_left, from_right))
+        opposite = send(from_left, right)
+        near = {(0, 0): own, (-1, 0): from_left, (1, 0): from_right}
+        other = {(hops, 1): send(block, swap) for (hops, _), block in near.items()}
         first, *states = moments(m, v, sums)
-        first, *far = lax.optimization_barrier((first, *far))
-        last = [send(block, swap[k::CORES]) for k, block in enumerate(far)]
-        down = place_rows(me, rows, near + other + far, layers, d, ff)
-        return (gate, up, place_last(me, *last, down), first, *states)
+        first, rows = lax.optimization_barrier((first, rows))
+        down = place_rows(rows, layers, d, ff)
+        down, opposite = lax.optimization_barrier((down, opposite))
+        last = {(2, 1): send(opposite, swap)}
+        down = place_blocks(me, {**near, **other, (2, 0): opposite}, down)
+        return (gate, up, place_blocks(me, last, down), first, *states)
 
     seq, whole, rows = P(("rep", "dp"), None, None), P(None, None, None), P(None, "dp", None)
     return jax.shard_map(

time: 706 us -> 699 us (0.990)
  starting transfers between devices: 16.1 us -> 4.46 us
    ppermute x9 -> x7, starting transfers between devices: 16.1 us -> 4.46 us  [send(): return lax.ppermute(block, 'dp', to)]
    pallas_call x1, Pallas kernels: 15.3 us -> 7.96 us  [place_rows(): pl.pallas_call(functools.partial(place_rows_kernel, layers, slots), in_sp...]
    pallas_call x1 -> x2, Pallas kernels: 2.41 us -> 9.48 us  [place_blocks(): pl.pallas_call(functools.partial(place_blocks_kernel, wheres), in_specs=[...]
  transfers between devices with their start and end apart: 9 -> 7, of which waited for: 1 -> 1; matrix products, arithmetic and copies ran while one was open for 0% -> 0% of each run, Pallas kernels for 10% -> 10%
where the time goes in v4:
time: 699 us
  Pallas kernels  690 us (99%)
    pallas_call x1, Pallas kernels, backward(): pl.pallas_call(functools.partial(backward_kernel, chips, tile), out_shape...  531 us
    pallas_call x1, Pallas kernels, forward(): pl.pallas_call(functools.partial(forward_kernel, tile), grid=(ff // width...  87.3 us
    pallas_call x1, Pallas kernels, place_columns(): pl.pallas_call(functools.partial(place_columns_kernel, layers, slots), in...  28.7 us
    pallas_call x1, Pallas kernels, moments(): pl.pallas_call(functools.partial(moments_kernel, layers, parts, slots), i...  25.7 us
  transfers between devices with their start and end apart: 7, of which 1 were waited for; matrix products, arithmetic and copies ran while one was open for 0% of the time, Pallas kernels for 10%

profile of v4, /device:TPU:113, one launch (start us, length us, event | category | flops | bytes accessed | tf_op | source)
XLA Modules:
  0.0 698.7 jit_solution(6998156881226226091)
XLA Ops:
  0.6 87.3 %forward.1 = (bf16[2,2048,1152]{2,1,0:T(8,128)(2,1)}, bf16[2048,1152]{1,0:T(8,128)(2,1)}) custom-call(bf16[2048,1152]{1,0:T(8,128)(2,1)} %bitcast.5, bf16[2,1152,4608]{2,1,0:T(8,128)(2,1)} %refs_3_.2, bf16[2,1152,4608]{2,1,0:T(8,128)(2,1)} %refs_4_.2, bf16[2,4608,1152]{2,1,0:T(8,128)(2,1)} %refs_5_.2), custom_call_target="tpu_custom_call" | custom-call | flops 65229815808 | bytes 31850496 | tf_op jit(solution)/shard_map/forward/pallas_call | solution.py:116
  88.0 531.2 %backward.1 = (bf16[2,144,4608]{2,1,0:T(8,128)(2,1)}, bf16[2,144,4608]{2,1,0:T(8,128)(2,1)}, bf16[2,576,1152]{2,1,0:T(8,128)(2,1)}, bf16[18,8,1152,128]{3,2,1,0:...) custom-call(bf16[2,2048,1152]{2,1,0:T(8,128)(2,1)} %get-tuple-element.32.ref, ...), custom_call_target="tpu_custom_call" | custom-call | flops 304405807104 | bytes 127401984 | tf_op jit(solution)/shard_map/backward/pallas_call | solution.py:667
  619.2 2.4 collective-permute-start.1
  621.6 0.0 collective-permute-start
  621.6 28.7 %place_columns.1 = (bf16[2,1152,4608]{2,1,0:T(8,128)(2,1)}, bf16[2,1152,4608]{2,1,0:T(8,128)(2,1)}) custom-call(bf16[2,9,8,2,4,144,128]{6,5,4,3,2,1,0:T(8,128)(2,1)} %bitcast.7), custom_call_target="tpu_custom_call" | custom-call | flops 5435817984 | bytes 84934656 | tf_op jit(solution)/shard_map/place_columns/pallas_call | solution.py:772
  650.3 0.0 collective-permute-done.1.refs_2_
  650.3 3.1 collective-permute-done.refs_1_
  653.4 0.0 collective-permute-start.2
  653.4 1.3 collective-permute-start.4
  654.7 25.7 %moments.1 = (f32[2,144,4608]{2,1,0:T(8,128)}, f32[2,144,4608]{2,1,0:T(8,128)}, f32[2,576,1152]{2,1,0:T(8,128)}, f32[2,144,4608]{2,1,0:T(8,128)}, f32[2,144,4608]{2,1,0:T(8,128)}, /*index=5*/f32[2,576,1152]{2,1,0:T(8,128)}) custom-call(f32[2,144,4608]{2,1,0:T(8,128)} %refs_0_.1, f32[2,144,4608]{2,1,0:T(8,128)} %refs_1_.1, f32[2,576,1152]{2,1,0:T(8,128)} %refs_2_.1, ...), custom_call_target="tpu_custom_call" | custom-call | flops 4586471424 | bytes 71663616 | tf_op jit(solution)/shard_map/moments/pallas_call | solution.py:824
  680.3 0.1 collective-permute-start.5
  680.4 0.5 collective-permute-start.6
  680.9 8.0 %place_rows.1.refs_7_ = bf16[2,4608,1152]{2,1,0:T(8,128)(2,1)} custom-call(bf16[1,5,8,1152,128]{4,3,2,1,0:T(8,128)(2,1)} %bitcast.8), custom_call_target="tpu_custom_call" | custom-call | flops 1358954496 | bytes 21233664 | tf_op jit(solution)/shard_map/place_rows/pallas_call | solution.py:875
  688.9 0.0 collective-permute-done.2.refs_6_
  688.9 0.2 collective-permute-start.3
  689.1 0.0 collective-permute-done.4.refs_3_
  689.1 0.0 collective-permute-done.6.refs_5_
  689.1 0.0 collective-permute-done.5.refs_4_
  689.1 7.1 %place_blocks.2.refs_1_ = bf16[2,4608,1152]{2,1,0:T(8,128)(2,1)} custom-call(s32[1]{0:T(128)} %bitcast.3.me_ref, bf16[576,1152]{1,0:T(8,128)(2,1)} %get-tuple-element.36.refs_0_, bf16[576,1152]{1,0:T(8,128)(2,1)} %collective-permute-done.refs_1_, bf16[576,1152]{1,0:T(8,128)(2,1)} %collective-permute-done.1.refs_2_, ...), custom_call_target="tpu_custom_call", output_to_operand_aliasing={{}: (8, {})} | custom-call | flops 1189085184 | bytes 18579456 | tf_op jit(solution)/shard_map/place_blocks/pallas_call | solution.py:911
  696.2 0.0 collective-permute-done.3.refs_0_
  696.2 2.4 place_blocks.3
Async XLA Ops:
  619.2 31.2 %collective-permute-start.1 = (bf16[576,1152]{1,0:T(8,128)(2,1)}, bf16[576,1152]{1,0:T(8,128)(2,1)}, u32[]{:S(2)}, u32[]{:S(2)}) collective-permute-start(bf16[576,1152]{1,0:T(8,128)(2,1)} %get-tuple-element.36.refs_0_), channel_id=1, source_target_pairs={{0,6},{1,7},{2,0},{3,1},{4,2},{5,3},{6,4},{7,5},{8,14},{9,15},{10,... | collective-permute-start | bytes 3981320 | tf_op jit(solution)/shard_map/ppermute | solution.py:937
  621.6 31.8 %collective-permute-start = (bf16[576,1152]{1,0:T(8,128)(2,1)}, bf16[576,1152]{1,0:T(8,128)(2,1)}, u32[]{:S(2)}, u32[]{:S(2)}) collective-permute-start(bf16[576,1152]{1,0:T(8,128)(2,1)} %get-tuple-element.36.refs_0_), channel_id=1, source_target_pairs={{0,2},{1,3},{2,4},{3,5},{4,6},{5,7},{6,0},{7,1},{8,10},{9,11},{10,... | collective-permute-start | bytes 3981320 | tf_op jit(solution)/shard_map/ppermute | solution.py:937
  653.4 35.5 %collective-permute-start.2 = (bf16[576,1152]{1,0:T(8,128)(2,1)}, bf16[576,1152]{1,0:T(8,128)(2,1)}, u32[]{:S(2)}, u32[]{:S(2)}) collective-permute-start(bf16[576,1152]{1,0:T(8,128)(2,1)} %collective-permute-done.refs_1_), channel_id=1, source_target_pairs={{0,2},{1,3},{2,4},{3,5},{4,6},{5,7},{6,0},{7,1},{8,10},{9,11},{10,... | collective-permute-start | bytes 3981320 | tf_op jit(solution)/shard_map/ppermute | solution.py:937
  653.4 35.7 %collective-permute-start.4 = (bf16[576,1152]{1,0:T(8,128)(2,1)}, bf16[576,1152]{1,0:T(8,128)(2,1)}, u32[]{:S(2)}, u32[]{:S(2)}) collective-permute-start(bf16[576,1152]{1,0:T(8,128)(2,1)} %get-tuple-element.36.refs_0_), channel_id=1, source_target_pairs={{0,1},{1,0},{2,3},{3,2},{4,5},{5,4},{6,7},{7,6},{8,9},{9,8},{10,11... | collective-permute-start | bytes 3981320 | tf_op jit(solution)/shard_map/ppermute | solution.py:937
  680.3 8.7 %collective-permute-start.5 = (bf16[576,1152]{1,0:T(8,128)(2,1)}, bf16[576,1152]{1,0:T(8,128)(2,1)}, u32[]{:S(2)}, u32[]{:S(2)}) collective-permute-start(bf16[576,1152]{1,0:T(8,128)(2,1)} %collective-permute-done.refs_1_), channel_id=1, source_target_pairs={{0,1},{1,0},{2,3},{3,2},{4,5},{5,4},{6,7},{7,6},{8,9},{9,8},{10,11... | collective-permute-start | bytes 3981320 | tf_op jit(solution)/shard_map/ppermute | solution.py:937
  680.4 8.6 %collective-permute-start.6 = (bf16[576,1152]{1,0:T(8,128)(2,1)}, bf16[576,1152]{1,0:T(8,128)(2,1)}, u32[]{:S(2)}, u32[]{:S(2)}) collective-permute-start(bf16[576,1152]{1,0:T(8,128)(2,1)} %collective-permute-done.1.refs_2_), channel_id=1, source_target_pairs={{0,1},{1,0},{2,3},{3,2},{4,5},{5,4},{6,7},{7,6},{8,9},{9,8},{10,11... | collective-permute-start | bytes 3981320 | tf_op jit(solution)/shard_map/ppermute | solution.py:937
  688.9 7.3 %collective-permute-start.3 = (bf16[576,1152]{1,0:T(8,128)(2,1)}, bf16[576,1152]{1,0:T(8,128)(2,1)}, u32[]{:S(2)}, u32[]{:S(2)}) collective-permute-start(bf16[576,1152]{1,0:T(8,128)(2,1)} %collective-permute-done.2.refs_6_), channel_id=1, source_target_pairs={{0,1},{1,0},{2,3},{3,2},{4,5},{5,4},{6,7},{7,6},{8,9},{9,8},{10,11... | collective-permute-start | bytes 3981320 | tf_op jit(solution)/shard_map/ppermute | solution.py:937

commit v5 on v4

--- a/solution.py
+++ b/solution.py
@@ -15,6 +15,7 @@
 CORES = 2
 VMEM_BYTES = 67_043_328
 COPY_FLOPS = 64
+LATE = 2
 SIDES = (0, 1), (1, -1)
 
 
@@ -276,7 +277,7 @@
     a_hbm, h_hbm, dy_hbm, wg_hbm, wu_hbm, wd_hbm, mg_hbm, mu_hbm, md_hbm, vg_hbm, vu_hbm, vd_hbm, *refs = refs
     gg_hbm, gu_hbm, gd_hbm, whole_gu, whole_dn, own_hbm, dy0_hbm, *refs = refs
     a_tile, dy_tile, at_ref, dyt_ref, da_ref, wg_ref, wu_ref, wd_ref, z_ref, dgu_ref, m_ref, v_ref, w_ref, *refs = refs
-    tile_sem, w_sem, state_sem, rows_sem, *pools = refs
+    tile_sem, w_sem, state_sem, own_sem, *pools = refs
     tokens, d = dy_hbm.shape
     layers, _, ff = wg_hbm.shape
     width = chips * LANES
@@ -377,10 +378,14 @@
             at = pl.ds(pl.multiple_of(start, LANES // 2), height)
             yield pltpu.make_async_copy(dn.sum.at[here, :], gd_hbm.at[layer, at, there], dn.out_sem.at[b])
 
-    def own_outs(n, size):
-        for b, _, start, height, here, there in dn_parts(n, size):
-            at = pl.ds(pl.multiple_of(start, LANES // 2), height)
-            yield pltpu.make_async_copy(dn.new.at[here, :], own_hbm.at[at, there], rows_sem.at[b])
+    def own_out(pool, at, size, sem):
+        return [pltpu.make_async_copy(pool.new.at[head(size)], own_hbm.at[pl.ds(pl.multiple_of(at, LANES // 2), size)], own_sem.at[sem])]
+
+    def dn_own(n, size):
+        return own_out(dn, (n - (layers - 1) * (pairs + 1)) * full, size, 0)
+
+    def gu_own(n):
+        return own_out(gu, pairs * full + small + (n - steps + LATE) * full, full, 1)
 
     def dn_state(n, size):
         for b, layer, start, height, here, there in dn_parts(n, size):
@@ -396,6 +401,8 @@
         gu.event3(n, size)
         pl.when(n > 0)(lambda: wait(gu_outs(n - 1)))
         wait(gu_state(n))
+        late = n >= steps - LATE
+        pl.when(n > steps - LATE)(lambda: wait(gu_own(n - 1)))
 
         def piece(i, _):
             at = strip(i * some, some)
@@ -407,7 +414,8 @@
         lax.fori_loop(0, size // some, piece, 0)
         gu.after3(n)
         start(gu_outs(n))
-        gu.gather1(n, size)
+        pl.when(~late)(lambda: gu.gather1(n, size))
+        pl.when(late)(lambda: start(gu_own(n)))
 
     def dn_new(n, size):
         half, height = LANES // 2, size // lane_blocks
@@ -420,7 +428,7 @@
             wait(dn_outs(n - 1, full))
         wait(dn_state(n, size))
         upper = n < (layers - 1) * (pairs + 1)
-        pl.when(n > (layers - 1) * (pairs + 1))(lambda: wait(own_outs(n - 1, full)))
+        pl.when(n > (layers - 1) * (pairs + 1))(lambda: wait(dn_own(n - 1, full)))
 
         def finish(at, g):
             dn.sum[at, :] = g.astype(BF16)
@@ -442,7 +450,7 @@
         dn.after3(n)
         start(dn_outs(n, size))
         pl.when(upper)(lambda: dn.gather1(n, size))
-        pl.when(~upper)(lambda: start(own_outs(n, size)))
+        pl.when(~upper)(lambda: start(dn_own(n, size)))
 
     def turn(buf, slot, into, part):
         for b in range(lane_blocks):
@@ -550,6 +558,9 @@
     def on(j, act):
         pl.when((j >= 0) & (j < steps))(lambda: act(j, full))
 
+    def early(j, act):
+        pl.when(j < steps - LATE)(lambda: on(j, act))
+
     def upper_down(j, act):
         pl.when(j < (layers - 1) * blocks)(lambda: for_down(j, act))
 
@@ -560,16 +571,17 @@
         start(dn_state(n, rows))
 
     events = {
-        "tile1": [(for_down, dn_new, 2)],
-        "tile3": [(on, gu.gather3, 3), (on, gu.event2, 1)],
-        "gate0": [(on, gu_load, 1)],
-        "gate3": [(on, gu.event0), (for_down, dn.event2, 1)],
-        "down0": [(on, gu.gather4, 3)],
-        "down1": [(for_down, dn.event0), (upper_down, dn.gather3, 3)],
-        "back0": [(on, gu.gather2, 2)],
-        "back1": [(upper_down, dn.gather2, 2)],
-        "back2": [(on, gu.event1), (for_down, dn.event1)],
-        "back3": [(upper_down, dn.gather4, 3), (on, gu_new, 1), (for_down, dn_load, 1)],
+        "tile0": [(early, gu.gather4, 4), (for_down, dn_new, 2)],
+        "tile2": [(on, gu.event2, 1)],
+        "tile3": [(on, gu_load, 1)],
+        "gate1": [(early, gu.gather3, 3), (for_down, dn.event2, 1)],
+        "gate3": [(on, gu.event0), (upper_down, dn.gather3, 3), (early, gu.gather2, 2)],
+        "down0": [(upper_down, dn.gather2, 2)],
+        "down1": [(for_down, dn.event0)],
+        "back0": [(on, gu.event1)],
+        "back1": [(upper_down, dn.gather4, 3), (for_down, dn.event1)],
+        "back2": [(on, gu_new, 1)],
+        "back3": [(for_down, dn_load, 1)],
     }
     longest = max(sum(ago) for these in events.values() for _, _, *ago in these)
 
@@ -623,7 +635,8 @@
     lax.fori_loop(0, steps + longest, step, 0)
     wait(gu_outs(steps - 1))
     wait(dn_outs(dn.number - 1, small))
-    wait(own_outs(dn.number - 1, small))
+    wait(dn_own(dn.number - 1, small))
+    wait(gu_own(steps - 1))
 
 
 def backward(mesh, a, h, dy, weights, m, v, tile=512):
@@ -643,7 +656,7 @@
         shape(layers, ff // devices, d),
         shape(layers * blocks, devices, d, LANES),
         shape((layers - 1) * (pairs + 1), devices, d, LANES),
-        shape(ff // devices, d),
+        shape(pairs * d + d // 2 + LATE * d, LANES),
         shape(tokens, d),
     ]
 
@@ -686,7 +699,7 @@
             pltpu.SemaphoreType.DMA((2, 3)),
             pltpu.SemaphoreType.DMA((2, 3 * chips)),
             pltpu.SemaphoreType.DMA((max(6 * chips, 3 * (d // LANES)),)),
-            pltpu.SemaphoreType.DMA((d // LANES,)),
+            pltpu.SemaphoreType.DMA((2,)),
             *pool(1, 2 * chips),
             *pool(2, d // LANES),
         ],
@@ -735,20 +748,21 @@
                 copy.wait()
 
 
-def place_columns_kernel(layers, slots, x_hbm, gate_hbm, up_hbm, c_in, c_out, sem):
+def place_columns_kernel(layer, slots, x_hbm, *refs):
+    gate_hbm, up_hbm, c_in, c_out, sem = refs[-5:]
     _, blocks, devices, _, chips, rows, _ = x_hbm.shape
     wide, some = blocks * LANES, c_in.shape[2]
     turns = devices // some
 
     def place(unit):
-        return unit // (chips * turns), lax.rem(unit, chips * turns) // turns, lax.rem(unit, turns) * some
+        return unit // turns, lax.rem(unit, turns) * some
 
     def loads(unit, slot):
-        layer, chip, owners = place(unit)
-        return [pltpu.make_async_copy(x_hbm.at[layers - 1 - layer, :, pl.ds(owners, some), :, chip], c_in.at[slot], sem.at[slot, 0])]
+        chip, owners = place(unit)
+        return [pltpu.make_async_copy(x_hbm.at[x_hbm.shape[0] - 1 - layer, :, pl.ds(owners, some), :, chip], c_in.at[slot], sem.at[slot, 0])]
 
     def stores(unit, slot):
-        layer, chip, owners = place(unit)
+        chip, owners = place(unit)
         at = layer, strip(owners * rows, some * rows), strip(chip * wide, wide)
         return [pltpu.make_async_copy(c_out.at[slot, u], out.at[at], sem.at[slot, 1 + u]) for u, out in enumerate((gate_hbm, up_hbm))]
 
@@ -759,20 +773,21 @@
                 for u in range(2):
                     c_out[slot, u, pl.ds(owner * rows, rows), at] = c_in[slot, j, owner, u]
 
-    ring = Ring(layers * chips * turns, slots, loads, stores, work)
+    ring = Ring(chips * turns, slots, loads, stores, work)
     ring.begin()
     ring.run()
     ring.end()
 
 
-def place_columns(chunks, layers, d, ff, slots=8, some=2):
+def place_columns(chunks, layer, layers, d, ff, into=(), slots=4, some=2):
     devices = chunks.shape[1]
     chips, rows = devices // CORES, d // devices
     x = chunks.reshape(layers, -1, devices, 2, chips, rows, LANES)
     return pl.pallas_call(
-        functools.partial(place_columns_kernel, layers, slots),
-        in_specs=[ANY],
+        functools.partial(place_columns_kernel, layer, slots),
+        in_specs=[ANY] * (1 + len(into)),
         out_specs=[ANY] * 2,
+        input_output_aliases={1 + i: i for i in range(len(into))},
         out_shape=[jax.ShapeDtypeStruct((layers, d, ff), BF16)] * 2,
         scratch_shapes=[
             pltpu.VMEM((slots, x.shape[1], some, 2, rows, LANES), BF16),
@@ -780,9 +795,9 @@
             pltpu.SemaphoreType.DMA((slots, 3)),
         ],
         compiler_params=pltpu.CompilerParams(vmem_limit_bytes=VMEM_BYTES),
-        cost_estimate=cost(COPY_FLOPS * 8 * layers * d * ff, 8 * layers * d * ff),
+        cost_estimate=cost(COPY_FLOPS * 8 * d * ff, 8 * d * ff),
         name="place_columns",
-    )(x)
+    )(x, *into)
 
 
 def moments_kernel(layers, parts, slots, *refs):
@@ -817,7 +832,7 @@
     ring.end()
 
 
-def moments(m, v, g, parts=9, slots=8):
+def moments(m, v, g, parts=9, slots=4):
     layers = m[0].shape[0]
     shapes = [(one.shape[1], one.shape[2] // parts) for one in m[:2]] + [(m[2].shape[1] // parts, m[2].shape[2])]
     size = sum(one.size for one in m)
@@ -838,11 +853,18 @@
     )(*m, *v, *g)
 
 
+def unfold(chunks, out, core):
+    pairs, half = chunks.shape[0] - 1, LANES // 2
+    for b in range(out.shape[1] // LANES):
+        for n in range(pairs):
+            out[pl.ds(pl.multiple_of(n * LANES + core * half, half), LANES), lanes(b)] = chunks[n, lanes(b), :]
+        out[pl.ds(pl.multiple_of(pairs * LANES * (1 - core), half), half), lanes(b)] = chunks[pairs, pl.ds(b * half, half), :]
+
+
 def place_rows_kernel(layers, slots, x_hbm, down_hbm, r_in, r_out, sem):
     devices = x_hbm.shape[2]
     pairs = x_hbm.shape[1] - 1
     height, d = r_out.shape[1:]
-    half = LANES // 2
 
     def loads(unit, slot):
         layer, device = layers - 2 - unit // devices, lax.rem(unit, devices)
@@ -856,11 +878,7 @@
         return [pltpu.make_async_copy(r_out.at[slot], down_hbm.at[layer, strip(device * height, height)], sem.at[slot, 2])]
 
     def work(unit, slot):
-        low = lax.rem(unit, CORES)
-        for b in range(d // LANES):
-            for n in range(pairs):
-                r_out[slot, pl.ds(pl.multiple_of(n * LANES + low * half, half), LANES), lanes(b)] = r_in[slot, n, lanes(b), :]
-            r_out[slot, pl.ds(pl.multiple_of(pairs * LANES * (1 - low), half), half), lanes(b)] = r_in[slot, pairs, pl.ds(b * half, half), :]
+        unfold(r_in.at[slot], r_out.at[slot], lax.rem(unit, CORES))
 
     ring = Ring((layers - 1) * devices, slots, loads, stores, work)
     ring.begin()
@@ -868,7 +886,7 @@
     ring.end()
 
 
-def place_rows(chunks, layers, d, ff, slots=8):
+def place_rows(chunks, layers, d, ff, slots=4):
     devices = chunks.shape[1]
     x = chunks.reshape(layers - 1, -1, devices, d, LANES)
     height = ff // devices
@@ -888,37 +906,74 @@
     )(x)
 
 
-def place_blocks_kernel(wheres, me_ref, *refs):
-    blocks, (down_hbm, held, sem) = refs[:-4], refs[-3:]
-    height = held.shape[1]
-    chips = down_hbm.shape[1] // (height * CORES)
+def place_blocks_kernel(wheres, pieces, me_ref, *refs):
+    blocks, (gate_hbm, up_hbm, down_hbm, held, down, sem) = refs[: pieces * len(wheres)], refs[-6:]
+    layers, d, ff = gate_hbm.shape
+    height = down.shape[1]
+    devices = ff // height
+    chips, rows = devices // CORES, d // devices
+    wide, size = ff // chips, blocks[0].shape[0]
+    pairs = wide // LANES // 2
     chip, core = me_ref[0] // CORES, lax.rem(me_ref[0], CORES)
-    fetch, put = [], []
-    for i, (block, (hops, flip)) in enumerate(zip(blocks, wheres)):
-        owner = lax.rem(chip + hops + chips, chips) * CORES + (1 - core if flip else core)
-        fetch.append(pltpu.make_async_copy(block, held.at[i], sem.at[i, 0]))
-        put.append(pltpu.make_async_copy(held.at[i], down_hbm.at[0, strip(owner * height, height)], sem.at[i, 1]))
-    start(fetch)
-    for one, other in zip(fetch, put):
-        one.wait()
-        other.start()
-    wait(put)
-
-
-def place_blocks(me, blocks, down):
+
+    def fetch(i):
+        for k in range(pieces):
+            yield pltpu.make_async_copy(blocks[pieces * i + k], held.at[i, pl.ds(k * size, size)], sem.at[i, k])
+
+    def put(i):
+        hops, flip = wheres[i]
+        side = 1 - core if flip else core
+        owner = lax.rem(chip + hops + chips, chips) * CORES + side
+        copies = [pltpu.make_async_copy(down.at[i], down_hbm.at[0, strip(owner * height, height)], sem.at[i, 2])]
+        for n in range(LATE):
+            step = 2 * pairs + 1 - LATE + n
+            column = (step // 2 + (pairs + 1) * (step % 2)) * LANES
+            for u, out in enumerate((gate_hbm, up_hbm)):
+                for c in range(chips):
+                    here = pl.ds(pairs * d + d // 2 + n * d + (u * chips + c) * rows, rows)
+                    to = out.at[0, strip(owner * rows, rows), pl.ds(c * wide + column, LANES)]
+                    copies.append(pltpu.make_async_copy(held.at[i, here], to, sem.at[i, 2 + len(copies)]))
+        return side, copies
+
+    number = len(wheres)
+    for i in range(number):
+        start(fetch(i))
+    for i in range(number):
+        wait(fetch(i))
+        side, copies = put(i)
+        start(copies[1:])
+        for n in range(pairs + 1):
+            size_n = d if n < pairs else d // 2
+            for b in range(d // LANES):
+                part = size_n // (d // LANES)
+                at = n * LANES + side * (LANES // 2) if n < pairs else pairs * LANES * (1 - side)
+                down[i, pl.ds(pl.multiple_of(at, LANES // 2), part), lanes(b)] = held[i, pl.ds(n * d + b * part, part), :]
+        copies[0].start()
+    for i in range(number):
+        wait(put(i)[1])
+
+
+def place_blocks(me, blocks, weights):
     wheres, blocks = tuple(blocks), list(blocks.values())
-    size = blocks[0].size * len(blocks)
+    number, pieces = len(blocks), len(blocks[0])
+    rows = pieces * blocks[0][0].shape[0]
+    layers, ff, d = weights[2].shape
+    height = rows * LANES // d - LATE * LANES
     return pl.pallas_call(
-        functools.partial(place_blocks_kernel, wheres),
-        in_specs=[pl.BlockSpec(memory_space=pltpu.SMEM)] + [ANY] * (len(blocks) + 1),
-        out_specs=ANY,
-        out_shape=jax.ShapeDtypeStruct(down.shape, BF16),
-        input_output_aliases={len(blocks) + 1: 0},
-        scratch_shapes=[pltpu.VMEM((len(blocks), *blocks[0].shape), BF16), pltpu.SemaphoreType.DMA((len(blocks), 2))],
+        functools.partial(place_blocks_kernel, wheres, pieces),
+        in_specs=[pl.BlockSpec(memory_space=pltpu.SMEM)] + [ANY] * (number * pieces + 3),
+        out_specs=[ANY] * 3,
+        out_shape=[jax.ShapeDtypeStruct(one.shape, BF16) for one in weights],
+        input_output_aliases={number * pieces + 1 + i: i for i in range(3)},
+        scratch_shapes=[
+            pltpu.VMEM((number, rows, LANES), BF16),
+            pltpu.VMEM((number, height, d), BF16),
+            pltpu.SemaphoreType.DMA((number, 3 + LATE * ff // height)),
+        ],
         compiler_params=pltpu.CompilerParams(vmem_limit_bytes=VMEM_BYTES),
-        cost_estimate=cost(COPY_FLOPS * 4 * size, 4 * size),
+        cost_estimate=cost(COPY_FLOPS * 4 * number * rows * LANES, 4 * number * rows * LANES),
         name="place_blocks",
-    )(me, *blocks, down)
+    )(me, *(piece for block in blocks for piece in block), *weights)
 
 
 def solution(mesh):
@@ -934,21 +989,24 @@
         *sums, columns, rows, own, _ = backward(mesh, *forward(x[0], *weights, 0), dy[0], weights, m, v)
 
         def send(block, to):
-            return lax.ppermute(block, "dp", to)
-
-        from_left, from_right = send(own, right), send(own, left)
-        gate, up = place_columns(columns, layers, d, ff)
-        gate, from_left, from_right = lax.optimization_barrier((gate, from_left, from_right))
-        opposite = send(from_left, right)
-        near = {(0, 0): own, (-1, 0): from_left, (1, 0): from_right}
+            return [lax.ppermute(piece, "dp", to) for piece in block]
+
+        half = own.shape[0] // 2
+        (from_left,), (from_right,) = send([own], right), send([own], left)
+        gate, up = place_columns(columns, 1, layers, d, ff)
+        first, *states = moments(m, v, sums)
+        gate, first, from_left, from_right = lax.optimization_barrier((gate, first, from_left, from_right))
+        opposite = send([from_left[:half]], right) + send([from_right[half:]], left)
+        near = {(0, 0): [own], (-1, 0): [from_left], (1, 0): [from_right]}
         other = {(hops, 1): send(block, swap) for (hops, _), block in near.items()}
-        first, *states = moments(m, v, sums)
-        first, rows = lax.optimization_barrier((first, rows))
+        gate, up = place_columns(columns, 0, layers, d, ff, (gate, up))
+        up, rows = lax.optimization_barrier((up, rows))
         down = place_rows(rows, layers, d, ff)
-        down, opposite = lax.optimization_barrier((down, opposite))
-        last = {(2, 1): send(opposite, swap)}
-        down = place_blocks(me, {**near, **other, (2, 0): opposite}, down)
-        return (gate, up, place_blocks(me, last, down), first, *states)
+        down, *opposite = lax.optimization_barrier((down, *opposite))
+        last = send(opposite, swap)
+        weights = place_blocks(me, {**near, **other}, (gate, up, down))
+        weights = place_blocks(me, {(2, 0): opposite, (2, 1): last}, weights)
+        return (*weights, first, *states)
 
     seq, whole, rows = P(("rep", "dp"), None, None), P(None, None, None), P(None, "dp", None)
     return jax.shard_map(

time: 699 us -> 685 us (0.980)
  Pallas kernels: 690 us -> 668 us
    pallas_call x1, Pallas kernels: 531 us -> 505 us  [backward(): pl.pallas_call(functools.partial(backward_kernel, chips, tile), out_shape...]
    pallas_call x3 -> x4, Pallas kernels: 38.2 us -> 43.4 us  [the longest x2 30 us: place_columns(): pl.pallas_call(functools.partial(place_columns_kernel, layer, slots), in_...]
  transfers between devices with their start and end apart: 7 -> 9, of which waited for: 1 -> 0; matrix products, arithmetic and copies ran while one was open for 0% -> 1% of each run, Pallas kernels for 10% -> 11%
where the time goes in v5:
time: 685 us; the launch traced here: 684 us
  Pallas kernels  668 us (98%)
  starting transfers between devices  10.8 us (2%)
    pallas_call x1, Pallas kernels, backward(): pl.pallas_call(functools.partial(backward_kernel, chips, tile), out_shape...  505 us
    pallas_call x1, Pallas kernels, forward(): pl.pallas_call(functools.partial(forward_kernel, tile), grid=(ff // width...  87.3 us
    pallas_call x2, Pallas kernels, place_columns(): pl.pallas_call(functools.partial(place_columns_kernel, layer, slots), in_...  30 us
    pallas_call x1, Pallas kernels, moments(): pl.pallas_call(functools.partial(moments_kernel, layers, parts, slots), i...  24.6 us
  transfers between devices with their start and end apart: 9, of which 0 were waited for; matrix products, arithmetic and copies ran while one was open for 1% of the time, Pallas kernels for 11%

profile of v5, /device:TPU:113, one launch (start us, length us, event | category | flops | bytes accessed | tf_op | source)
XLA Modules:
  0.0 684.4 jit_solution(15321656246171826133)
XLA Ops:
  0.6 87.3 %forward.1 = (bf16[2,2048,1152]{2,1,0:T(8,128)(2,1)}, bf16[2048,1152]{1,0:T(8,128)(2,1)}) custom-call(bf16[2048,1152]{1,0:T(8,128)(2,1)} %bitcast.7, bf16[2,1152,4608]{2,1,0:T(8,128)(2,1)} %refs_3_.2, bf16[2,1152,4608]{2,1,0:T(8,128)(2,1)} %refs_4_.2, bf16[2,4608,1152]{2,1,0:T(8,128)(2,1)} %refs_5_.2), custom_call_target="tpu_custom_call" | custom-call | flops 65229815808 | bytes 31850496 | tf_op jit(solution)/shard_map/forward/pallas_call | solution.py:117
  88.0 504.9 %backward.1 = (bf16[2,144,4608]{2,1,0:T(8,128)(2,1)}, bf16[2,144,4608]{2,1,0:T(8,128)(2,1)}, bf16[2,576,1152]{2,1,0:T(8,128)(2,1)}, bf16[18,8,1152,128]{3,2,1,0:...) custom-call(bf16[2,2048,1152]{2,1,0:T(8,128)(2,1)} %get-tuple-element.42.ref, ...), custom_call_target="tpu_custom_call" | custom-call | flops 304405807104 | bytes 127401984 | tf_op jit(solution)/shard_map/backward/pallas_call | solution.py:680
  592.9 2.0 collective-permute-start
  594.9 1.3 collective-permute-start.1
  596.3 3.0 collective-permute-start.6
  599.3 15.0 %place_columns.2 = (bf16[2,1152,4608]{2,1,0:T(8,128)(2,1)}, bf16[2,1152,4608]{2,1,0:T(8,128)(2,1)}) custom-call(bf16[2,9,8,2,4,144,128]{6,5,4,3,2,1,0:T(8,128)(2,1)} %bitcast.5), custom_call_target="tpu_custom_call" | custom-call | flops 2717908992 | bytes 42467328 | tf_op jit(solution)/shard_map/place_columns/pallas_call | solution.py:786
  614.3 24.6 %moments.1 = (f32[2,144,4608]{2,1,0:T(8,128)}, f32[2,144,4608]{2,1,0:T(8,128)}, f32[2,576,1152]{2,1,0:T(8,128)}, f32[2,144,4608]{2,1,0:T(8,128)}, f32[2,144,4608]{2,1,0:T(8,128)}, /*index=5*/f32[2,576,1152]{2,1,0:T(8,128)}) custom-call(f32[2,144,4608]{2,1,0:T(8,128)} %refs_0_.1, f32[2,144,4608]{2,1,0:T(8,128)} %refs_1_.1, f32[2,576,1152]{2,1,0:T(8,128)} %refs_2_.1, ...), custom_call_target="tpu_custom_call" | custom-call | flops 4586471424 | bytes 71663616 | tf_op jit(solution)/shard_map/moments/pallas_call | solution.py:839
  638.9 0.0 collective-permute-done.refs_1_
  638.9 0.0 collective-permute-done.1.refs_2_
  639.0 0.5 collective-permute-start.7
  639.4 0.1 collective-permute-start.8
  639.5 2.2 slice.6
  641.8 2.2 slice.7
  644.0 0.6 collective-permute-start.2
  644.6 2.1 collective-permute-start.3
  646.7 15.0 %place_columns.3 = (bf16[2,1152,4608]{2,1,0:T(8,128)(2,1)}, bf16[2,1152,4608]{2,1,0:T(8,128)(2,1)}) custom-call(bf16[2,9,8,2,4,144,128]{6,5,4,3,2,1,0:T(8,128)(2,1)} %bitcast.6, bf16[2,1152,4608]{2,1,0:T(8,128)(2,1)} %get-tuple-element.51.refs_0_, bf16[2,1152,4608]{2,1,0:T(8,128)(2,1)} %get-tuple-element.52.refs_1_), custom_call_target="tpu_custom_call", output_to_operand_aliasing={{0}: (1, {}), {1}: (2, {})} | custom-call | flops 2717908992 | bytes 42467328 | tf_op jit(solution)/shard_map/place_columns/pallas_call | solution.py:786
  661.7 7.9 %place_rows.1.refs_8_ = bf16[2,4608,1152]{2,1,0:T(8,128)(2,1)} custom-call(bf16[1,5,8,1152,128]{4,3,2,1,0:T(8,128)(2,1)} %bitcast.9), custom_call_target="tpu_custom_call" | custom-call | flops 1358954496 | bytes 21233664 | tf_op jit(solution)/shard_map/place_rows/pallas_call | solution.py:893
  669.6 0.0 collective-permute-done.2.refs_0_
  669.6 0.0 collective-permute-done.3.refs_1_
  669.6 1.1 collective-permute-start.4
  670.7 0.1 collective-permute-start.5
  670.8 0.0 collective-permute-done.6.refs_3_
  670.8 0.0 collective-permute-done.7.refs_4_
  670.8 0.0 collective-permute-done.8.refs_5_
  670.8 9.6 %place_blocks.2 = (bf16[2,1152,4608]{2,1,0:T(8,128)(2,1)}, bf16[2,1152,4608]{2,1,0:T(8,128)(2,1)}, bf16[2,4608,1152]{2,1,0:T(8,128)(2,1)}) custom-call(s32[1]{0:T(128)} %bitcast.me_ref, bf16[7488,128]{1,0:T(8,128)(2,1)} %get-tuple-element.50.refs_0_, ...), custom_call_target="tpu_custom_call", output_to_operand_aliasing={{0}: (7, {}), {1}: (8, {}), {2}: (9, {})} | custom-call | flops 1472200704 | bytes 23003136 | tf_op jit(solution)/shard_map/place_blocks/pallas_call | solution.py:962
  680.4 0.0 collective-permute-done.4.refs_2_
  680.4 0.0 collective-permute-done.5.refs_3_
  680.4 3.8 place_blocks.3
Async XLA Ops:
  592.9 46.0 %collective-permute-start = (bf16[7488,128]{1,0:T(8,128)(2,1)}, bf16[7488,128]{1,0:T(8,128)(2,1)}, u32[]{:S(2)}, u32[]{:S(2)}) collective-permute-start(bf16[7488,128]{1,0:T(8,128)(2,1)} %get-tuple-element.50.refs_0_), channel_id=1, source_target_pairs={{0,2},{1,3},{2,4},{3,5},{4,6},{5,7},{6,0},{7,1},{8,10},{9,11},{10,... | collective-permute-start | bytes 5750792 | tf_op jit(solution)/shard_map/ppermute | solution.py:992
  594.9 44.0 %collective-permute-start.1 = (bf16[7488,128]{1,0:T(8,128)(2,1)}, bf16[7488,128]{1,0:T(8,128)(2,1)}, u32[]{:S(2)}, u32[]{:S(2)}) collective-permute-start(bf16[7488,128]{1,0:T(8,128)(2,1)} %get-tuple-element.50.refs_0_), channel_id=1, source_target_pairs={{0,6},{1,7},{2,0},{3,1},{4,2},{5,3},{6,4},{7,5},{8,14},{9,15},{10,... | collective-permute-start | bytes 5750792 | tf_op jit(solution)/shard_map/ppermute | solution.py:992
  596.3 74.5 %collective-permute-start.6 = (bf16[7488,128]{1,0:T(8,128)(2,1)}, bf16[7488,128]{1,0:T(8,128)(2,1)}, u32[]{:S(2)}, u32[]{:S(2)}) collective-permute-start(bf16[7488,128]{1,0:T(8,128)(2,1)} %get-tuple-element.50.refs_0_), channel_id=1, source_target_pairs={{0,1},{1,0},{2,3},{3,2},{4,5},{5,4},{6,7},{7,6},{8,9},{9,8},{10,11... | collective-permute-start | bytes 5750792 | tf_op jit(solution)/shard_map/ppermute | solution.py:992
  639.0 31.8 %collective-permute-start.7 = (bf16[7488,128]{1,0:T(8,128)(2,1)}, bf16[7488,128]{1,0:T(8,128)(2,1)}, u32[]{:S(2)}, u32[]{:S(2)}) collective-permute-start(bf16[7488,128]{1,0:T(8,128)(2,1)} %collective-permute-done.refs_1_), channel_id=1, source_target_pairs={{0,1},{1,0},{2,3},{3,2},{4,5},{5,4},{6,7},{7,6},{8,9},{9,8},{10,11... | collective-permute-start | bytes 5750792 | tf_op jit(solution)/shard_map/ppermute | solution.py:992
  639.4 31.4 %collective-permute-start.8 = (bf16[7488,128]{1,0:T(8,128)(2,1)}, bf16[7488,128]{1,0:T(8,128)(2,1)}, u32[]{:S(2)}, u32[]{:S(2)}) collective-permute-start(bf16[7488,128]{1,0:T(8,128)(2,1)} %collective-permute-done.1.refs_2_), channel_id=1, source_target_pairs={{0,1},{1,0},{2,3},{3,2},{4,5},{5,4},{6,7},{7,6},{8,9},{9,8},{10,11... | collective-permute-start | bytes 5750792 | tf_op jit(solution)/shard_map/ppermute | solution.py:992
  644.0 25.6 %collective-permute-start.2 = (bf16[3744,128]{1,0:T(8,128)(2,1)}, bf16[3744,128]{1,0:T(8,128)(2,1)}, u32[]{:S(2)}, u32[]{:S(2)}) collective-permute-start(bf16[3744,128]{1,0:T(8,128)(2,1)} %slice.6), channel_id=1, source_target_pairs={{0,2},{1,3},{2,4},{3,5},{4,6},{5,7},{6,0},{7,1},{8,10},{9,11},{10,... | collective-permute-start | bytes 2875400 | tf_op jit(solution)/shard_map/ppermute | solution.py:992
  644.6 25.1 %collective-permute-start.3 = (bf16[3744,128]{1,0:T(8,128)(2,1)}, bf16[3744,128]{1,0:T(8,128)(2,1)}, u32[]{:S(2)}, u32[]{:S(2)}) collective-permute-start(bf16[3744,128]{1,0:T(8,128)(2,1)} %slice.7), channel_id=1, source_target_pairs={{0,6},{1,7},{2,0},{3,1},{4,2},{5,3},{6,4},{7,5},{8,14},{9,15},{10,... | collective-permute-start | bytes 2875400 | tf_op jit(solution)/shard_map/ppermute | solution.py:992
  669.6 10.8 %collective-permute-start.4 = (bf16[3744,128]{1,0:T(8,128)(2,1)}, bf16[3744,128]{1,0:T(8,128)(2,1)}, u32[]{:S(2)}, u32[]{:S(2)}) collective-permute-start(bf16[3744,128]{1,0:T(8,128)(2,1)} %collective-permute-done.2.refs_0_), channel_id=1, source_target_pairs={{0,1},{1,0},{2,3},{3,2},{4,5},{5,4},{6,7},{7,6},{8,9},{9,8},{10,11... | collective-permute-start | bytes 2875400 | tf_op jit(solution)/shard_map/ppermute | solution.py:992
  670.7 9.7 %collective-permute-start.5 = (bf16[3744,128]{1,0:T(8,128)(2,1)}, bf16[3744,128]{1,0:T(8,128)(2,1)}, u32[]{:S(2)}, u32[]{:S(2)}) collective-permute-start(bf16[3744,128]{1,0:T(8,128)(2,1)} %collective-permute-done.3.refs_1_), channel_id=1, source_target_pairs={{0,1},{1,0},{2,3},{3,2},{4,5},{5,4},{6,7},{7,6},{8,9},{9,8},{10,11... | collective-permute-start | bytes 2875400 | tf_op jit(solution)/shard_map/ppermute | solution.py:992

commit v6 on v5

--- a/solution.py
+++ b/solution.py
@@ -474,14 +474,16 @@
         wait_tile(t)
         pl.when(t + 1 < tiles)(lambda: start_tile(j, t + 1))
         a, dy = a_tile[here], dy_tile[here]
-        gate = dot(a, wg_ref[slot])
-        up = dot(a, wu_ref[slot])
-        dz = dot(dy, wd_ref[slot], NT).astype(BF16).astype(F32)
-        s = jax.nn.sigmoid(gate)
-        act = s * gate
-        z_ref[part, :] = (act * up).astype(BF16)
-        dgu_ref[1, part, :] = (dz * act).astype(BF16)
-        dgu_ref[0, part, :] = (dz * up * (s + act * (1 - s))).astype(BF16)
+        for c in range(0, chips, 2):
+            some = pl.ds(c * LANES, 2 * LANES)
+            gate = dot(a, wg_ref[slot, :, some])
+            up = dot(a, wu_ref[slot, :, some])
+            dz = dot(dy, wd_ref[slot, some, :], NT).astype(BF16).astype(F32)
+            s = jax.nn.sigmoid(gate)
+            act = s * gate
+            z_ref[part, some] = (act * up).astype(BF16)
+            dgu_ref[1, part, some] = (dz * act).astype(BF16)
+            dgu_ref[0, part, some] = (dz * up * (s + act * (1 - s))).astype(BF16)
 
         @pl.when(j == 0)
         def _():
@@ -489,11 +491,11 @@
             turn(dy_tile, here, dyt_ref, part)
             da_ref[part, :] = jnp.zeros((tile, d), F32)
 
-    def compute_gate_up(j, s):
-        slot, u, h = lax.rem(j, gu.slots), s // (chips // 2), 2 * lax.rem(s, chips // 2)
-        g = dot(at_ref[...], dgu_ref[u, :, strip(h * LANES, 2 * LANES)]).astype(BF16)
-        for c in range(2):
-            at = strip((u * chips + h + c) * rows, rows)
+    def compute_gate_up(j, u):
+        slot = lax.rem(j, gu.slots)
+        g = dot(at_ref[...], dgu_ref[u]).astype(BF16)
+        for c in range(chips):
+            at = strip((u * chips + c) * rows, rows)
             for owner in range(CORES * chips):
                 gu.mine[slot, owner % CORES, owner // CORES, at, :] = g[owner * rows : (owner + 1) * rows, c * LANES : (c + 1) * LANES]
 
@@ -524,18 +526,17 @@
         slot, part = parity(j), strip(t * tile, tile)
         da_ref[part, :] += dot(dgu_ref[0, part, :], wg_ref[slot], NT) + dot(dgu_ref[1, part, :], wu_ref[slot], NT)
 
+    def begin_change(t):
+        load(h_hbm, a_tile, t, 0).start()
+        load(dy_hbm, dy_tile, t, 1).start()
+
     def change_layer():
-        def begin(t):
-            load(h_hbm, a_tile, t, 0).start()
-            load(dy_hbm, dy_tile, t, 1).start()
-
-        begin(0)
-
         def one(t, _):
             slot = parity(t)
             wait_tile(t)
             pl.when(t > 0)(lambda: keep(t - 1).wait())
-            pl.when(t + 1 < tiles)(lambda: begin(t + 1))
+            pl.when(t + 1 < tiles)(lambda: begin_change(t + 1))
+            pl.when(t + 1 == tiles)(lambda: start_tile(blocks, 0))
 
             def piece(i, _):
                 here, there = strip(i * small_tile, small_tile), strip(t * tile + i * small_tile, small_tile)
@@ -571,15 +572,15 @@
         start(dn_state(n, rows))
 
     events = {
-        "tile0": [(early, gu.gather4, 4), (for_down, dn_new, 2)],
+        "tile1": [(for_down, dn_new, 2)],
         "tile2": [(on, gu.event2, 1)],
-        "tile3": [(on, gu_load, 1)],
-        "gate1": [(early, gu.gather3, 3), (for_down, dn.event2, 1)],
-        "gate3": [(on, gu.event0), (upper_down, dn.gather3, 3), (early, gu.gather2, 2)],
+        "tile3": [(upper_down, dn.gather3, 3), (for_down, dn.event2, 1)],
+        "gate0": [(on, gu_load, 1)],
+        "gate1": [(on, gu.event0), (early, gu.gather3, 3)],
         "down0": [(upper_down, dn.gather2, 2)],
-        "down1": [(for_down, dn.event0)],
-        "back0": [(on, gu.event1)],
-        "back1": [(upper_down, dn.gather4, 3), (for_down, dn.event1)],
+        "down1": [(for_down, dn.event0), (upper_down, dn.gather4, 3), (on, gu.event1)],
+        "back0": [(early, gu.gather4, 3)],
+        "back1": [(early, gu.gather2, 2), (for_down, dn.event1)],
         "back2": [(on, gu_new, 1)],
         "back3": [(for_down, dn_load, 1)],
     }
@@ -612,6 +613,7 @@
         def da_tile(j, t):
             fetch = load(a_hbm.at[0], a_tile, t, 0)
             pl.when(changes)(fetch.start)
+            pl.when(changes & (t + 1 == tiles))(lambda: begin_change(0))
             compute_da(j, t)
 
             @pl.when(changes)
@@ -621,14 +623,11 @@
 
         parts("tile", tiles, busy, compute_tile)
         pl.when(busy & (j + 1 < steps) & ~changes)(lambda: start_tile(j + 1, 0))
-        parts("gate", chips, busy, compute_gate_up)
+        parts("gate", 2, busy, compute_gate_up)
         parts("down", chips // 2, busy, compute_down)
         parts("back", tiles, busy & lower, da_tile)
 
-        @pl.when(changes)
-        def _():
-            change_layer()
-            start_tile(j + 1, 0)
+        pl.when(changes)(change_layer)
 
         return 0
 
@@ -906,25 +905,24 @@
     )(x)
 
 
-def place_blocks_kernel(wheres, pieces, me_ref, *refs):
-    blocks, (gate_hbm, up_hbm, down_hbm, held, down, sem) = refs[: pieces * len(wheres)], refs[-6:]
+def place_blocks_kernel(wheres, me_ref, *refs):
+    blocks, (gate_hbm, up_hbm, down_hbm, held, down, sem) = refs[: len(wheres)], refs[-6:]
     layers, d, ff = gate_hbm.shape
     height = down.shape[1]
     devices = ff // height
     chips, rows = devices // CORES, d // devices
-    wide, size = ff // chips, blocks[0].shape[0]
+    wide = ff // chips
     pairs = wide // LANES // 2
     chip, core = me_ref[0] // CORES, lax.rem(me_ref[0], CORES)
 
     def fetch(i):
-        for k in range(pieces):
-            yield pltpu.make_async_copy(blocks[pieces * i + k], held.at[i, pl.ds(k * size, size)], sem.at[i, k])
+        return pltpu.make_async_copy(blocks[i], held.at[i], sem.at[i, 0])
 
     def put(i):
         hops, flip = wheres[i]
         side = 1 - core if flip else core
         owner = lax.rem(chip + hops + chips, chips) * CORES + side
-        copies = [pltpu.make_async_copy(down.at[i], down_hbm.at[0, strip(owner * height, height)], sem.at[i, 2])]
+        copies = [pltpu.make_async_copy(down.at[i], down_hbm.at[0, strip(owner * height, height)], sem.at[i, 1])]
         for n in range(LATE):
             step = 2 * pairs + 1 - LATE + n
             column = (step // 2 + (pairs + 1) * (step % 2)) * LANES
@@ -932,14 +930,14 @@
                 for c in range(chips):
                     here = pl.ds(pairs * d + d // 2 + n * d + (u * chips + c) * rows, rows)
                     to = out.at[0, strip(owner * rows, rows), pl.ds(c * wide + column, LANES)]
-                    copies.append(pltpu.make_async_copy(held.at[i, here], to, sem.at[i, 2 + len(copies)]))
+                    copies.append(pltpu.make_async_copy(held.at[i, here], to, sem.at[i, 1 + len(copies)]))
         return side, copies
 
     number = len(wheres)
     for i in range(number):
-        start(fetch(i))
+        fetch(i).start()
     for i in range(number):
-        wait(fetch(i))
+        fetch(i).wait()
         side, copies = put(i)
         start(copies[1:])
         for n in range(pairs + 1):
@@ -955,25 +953,24 @@
 
 def place_blocks(me, blocks, weights):
     wheres, blocks = tuple(blocks), list(blocks.values())
-    number, pieces = len(blocks), len(blocks[0])
-    rows = pieces * blocks[0][0].shape[0]
+    number, rows = len(blocks), blocks[0].shape[0]
     layers, ff, d = weights[2].shape
     height = rows * LANES // d - LATE * LANES
     return pl.pallas_call(
-        functools.partial(place_blocks_kernel, wheres, pieces),
-        in_specs=[pl.BlockSpec(memory_space=pltpu.SMEM)] + [ANY] * (number * pieces + 3),
+        functools.partial(place_blocks_kernel, wheres),
+        in_specs=[pl.BlockSpec(memory_space=pltpu.SMEM)] + [ANY] * (number + 3),
         out_specs=[ANY] * 3,
         out_shape=[jax.ShapeDtypeStruct(one.shape, BF16) for one in weights],
-        input_output_aliases={number * pieces + 1 + i: i for i in range(3)},
+        input_output_aliases={number + 1 + i: i for i in range(3)},
         scratch_shapes=[
             pltpu.VMEM((number, rows, LANES), BF16),
             pltpu.VMEM((number, height, d), BF16),
-            pltpu.SemaphoreType.DMA((number, 3 + LATE * ff // height)),
+            pltpu.SemaphoreType.DMA((number, 2 + LATE * ff // height)),
         ],
         compiler_params=pltpu.CompilerParams(vmem_limit_bytes=VMEM_BYTES),
         cost_estimate=cost(COPY_FLOPS * 4 * number * rows * LANES, 4 * number * rows * LANES),
         name="place_blocks",
-    )(me, *(piece for block in blocks for piece in block), *weights)
+    )(me, *blocks, *weights)
 
 
 def solution(mesh):
@@ -989,20 +986,19 @@
         *sums, columns, rows, own, _ = backward(mesh, *forward(x[0], *weights, 0), dy[0], weights, m, v)
 
         def send(block, to):
-            return [lax.ppermute(piece, "dp", to) for piece in block]
-
-        half = own.shape[0] // 2
-        (from_left,), (from_right,) = send([own], right), send([own], left)
+            return lax.ppermute(block, "dp", to)
+
+        from_left, from_right = send(own, right), send(own, left)
         gate, up = place_columns(columns, 1, layers, d, ff)
         first, *states = moments(m, v, sums)
         gate, first, from_left, from_right = lax.optimization_barrier((gate, first, from_left, from_right))
-        opposite = send([from_left[:half]], right) + send([from_right[half:]], left)
-        near = {(0, 0): [own], (-1, 0): [from_left], (1, 0): [from_right]}
+        opposite = send(jnp.where(lax.rem(lax.axis_index("dp"), CORES) == 0, from_left, from_right), [(right, left)[i % CORES][i] for i in range(group)])
+        near = {(0, 0): own, (-1, 0): from_left, (1, 0): from_right}
         other = {(hops, 1): send(block, swap) for (hops, _), block in near.items()}
         gate, up = place_columns(columns, 0, layers, d, ff, (gate, up))
         up, rows = lax.optimization_barrier((up, rows))
         down = place_rows(rows, layers, d, ff)
-        down, *opposite = lax.optimization_barrier((down, *opposite))
+        down, opposite = lax.optimization_barrier((down, opposite))
         last = send(opposite, swap)
         weights = place_blocks(me, {**near, **other}, (gate, up, down))
         weights = place_blocks(me, {(2, 0): opposite, (2, 1): last}, weights)

time: 685 us -> 677 us (0.988)
  transfers between devices with their start and end apart: 9 -> 7, of which waited for: 0 -> 1; matrix products, arithmetic and copies ran while one was open for 1% -> 0% of each run, Pallas kernels for 11% -> 11%
where the time goes in v6:
time: 677 us
  Pallas kernels  664 us (98%)
  starting transfers between devices  7.29 us (1%)
    pallas_call x1, Pallas kernels, backward(): pl.pallas_call(functools.partial(backward_kernel, chips, tile), out_shape...  501 us
    pallas_call x1, Pallas kernels, forward(): pl.pallas_call(functools.partial(forward_kernel, tile), grid=(ff // width...  87.3 us
    pallas_call x2, Pallas kernels, place_columns(): pl.pallas_call(functools.partial(place_columns_kernel, layer, slots), in_...  30 us
    pallas_call x1, Pallas kernels, moments(): pl.pallas_call(functools.partial(moments_kernel, layers, parts, slots), i...  24.6 us
  transfers between devices with their start and end apart: 7, of which 1 were waited for; matrix products, arithmetic and copies ran while one was open for 0% of the time, Pallas kernels for 11%

profile of v6, /device:TPU:113, one launch (start us, length us, event | category | flops | bytes accessed | tf_op | source)
XLA Modules:
  0.0 677.0 jit_solution(10324099735760067212)
XLA Ops:
  0.6 87.3 %forward.1 = (bf16[2,2048,1152]{2,1,0:T(8,128)(2,1)}, bf16[2048,1152]{1,0:T(8,128)(2,1)}) custom-call(bf16[2048,1152]{1,0:T(8,128)(2,1)} %bitcast.7, bf16[2,1152,4608]{2,1,0:T(8,128)(2,1)} %refs_3_.2, bf16[2,1152,4608]{2,1,0:T(8,128)(2,1)} %refs_4_.2, bf16[2,4608,1152]{2,1,0:T(8,128)(2,1)} %refs_5_.2), custom_call_target="tpu_custom_call" | custom-call | flops 65229815808 | bytes 31850496 | tf_op jit(solution)/shard_map/forward/pallas_call | solution.py:117
  88.0 501.1 %backward.1 = (bf16[2,144,4608]{2,1,0:T(8,128)(2,1)}, bf16[2,144,4608]{2,1,0:T(8,128)(2,1)}, bf16[2,576,1152]{2,1,0:T(8,128)(2,1)}, bf16[18,8,1152,128]{3,2,1,0:...) custom-call(bf16[2,2048,1152]{2,1,0:T(8,128)(2,1)} %get-tuple-element.41.ref, ...), custom_call_target="tpu_custom_call" | custom-call | flops 304405807104 | bytes 127401984 | tf_op jit(solution)/shard_map/backward/pallas_call | solution.py:679
  589.1 0.7 collective-permute-start
  589.8 2.0 collective-permute-start.1
  591.8 15.0 %place_columns.2 = (bf16[2,1152,4608]{2,1,0:T(8,128)(2,1)}, bf16[2,1152,4608]{2,1,0:T(8,128)(2,1)}) custom-call(bf16[2,9,8,2,4,144,128]{6,5,4,3,2,1,0:T(8,128)(2,1)} %bitcast.5), custom_call_target="tpu_custom_call" | custom-call | flops 2717908992 | bytes 42467328 | tf_op jit(solution)/shard_map/place_columns/pallas_call | solution.py:785
  606.8 24.6 %moments.1 = (f32[2,144,4608]{2,1,0:T(8,128)}, f32[2,144,4608]{2,1,0:T(8,128)}, f32[2,576,1152]{2,1,0:T(8,128)}, f32[2,144,4608]{2,1,0:T(8,128)}, f32[2,144,4608]{2,1,0:T(8,128)}, /*index=5*/f32[2,576,1152]{2,1,0:T(8,128)}) custom-call(f32[2,144,4608]{2,1,0:T(8,128)} %refs_0_.1, f32[2,144,4608]{2,1,0:T(8,128)} %refs_1_.1, f32[2,576,1152]{2,1,0:T(8,128)} %refs_2_.1, ...), custom_call_target="tpu_custom_call" | custom-call | flops 4586471424 | bytes 71663616 | tf_op jit(solution)/shard_map/moments/pallas_call | solution.py:838
  631.4 1.5 collective-permute-done.refs_1_
  633.0 0.0 collective-permute-done.1.refs_2_
  633.0 3.0 broadcast_select_fusion
  636.0 2.4 collective-permute-start.2
  638.4 0.0 collective-permute-start.4
  638.4 0.5 collective-permute-start.5
  638.9 0.0 collective-permute-start.6
  638.9 15.0 %place_columns.3 = (bf16[2,1152,4608]{2,1,0:T(8,128)(2,1)}, bf16[2,1152,4608]{2,1,0:T(8,128)(2,1)}) custom-call(bf16[2,9,8,2,4,144,128]{6,5,4,3,2,1,0:T(8,128)(2,1)} %bitcast.6, bf16[2,1152,4608]{2,1,0:T(8,128)(2,1)} %get-tuple-element.50.refs_0_, bf16[2,1152,4608]{2,1,0:T(8,128)(2,1)} %get-tuple-element.51.refs_1_), custom_call_target="tpu_custom_call", output_to_operand_aliasing={{0}: (1, {}), {1}: (2, {})} | custom-call | flops 2717908992 | bytes 42467328 | tf_op jit(solution)/shard_map/place_columns/pallas_call | solution.py:785
  653.9 7.9 %place_rows.1.refs_8_ = bf16[2,4608,1152]{2,1,0:T(8,128)(2,1)} custom-call(bf16[1,5,8,1152,128]{4,3,2,1,0:T(8,128)(2,1)} %bitcast.9), custom_call_target="tpu_custom_call" | custom-call | flops 1358954496 | bytes 21233664 | tf_op jit(solution)/shard_map/place_rows/pallas_call | solution.py:892
  661.8 0.0 collective-permute-done.2.refs_0_
  661.8 1.6 collective-permute-start.3
  663.5 0.0 collective-permute-done.4.refs_3_
  663.5 0.0 collective-permute-done.5.refs_4_
  663.5 0.0 collective-permute-done.6.refs_5_
  663.5 9.5 %place_blocks.2 = (bf16[2,1152,4608]{2,1,0:T(8,128)(2,1)}, bf16[2,1152,4608]{2,1,0:T(8,128)(2,1)}, bf16[2,4608,1152]{2,1,0:T(8,128)(2,1)}) custom-call(s32[1]{0:T(128)} %bitcast.me_ref, bf16[7488,128]{1,0:T(8,128)(2,1)} %get-tuple-element.49.refs_0_, ...), custom_call_target="tpu_custom_call", output_to_operand_aliasing={{0}: (7, {}), {1}: (8, {}), {2}: (9, {})} | custom-call | flops 1472200704 | bytes 23003136 | tf_op jit(solution)/shard_map/place_blocks/pallas_call | solution.py:959
  673.0 0.0 collective-permute-done.3.refs_1_
  673.0 3.8 place_blocks.3
Async XLA Ops:
  589.1 43.9 %collective-permute-start = (bf16[7488,128]{1,0:T(8,128)(2,1)}, bf16[7488,128]{1,0:T(8,128)(2,1)}, u32[]{:S(2)}, u32[]{:S(2)}) collective-permute-start(bf16[7488,128]{1,0:T(8,128)(2,1)} %get-tuple-element.49.refs_0_), channel_id=1, source_target_pairs={{0,2},{1,3},{2,4},{3,5},{4,6},{5,7},{6,0},{7,1},{8,10},{9,11},{10,... | collective-permute-start | bytes 5750792 | tf_op jit(solution)/shard_map/ppermute | solution.py:989
  589.8 43.2 %collective-permute-start.1 = (bf16[7488,128]{1,0:T(8,128)(2,1)}, bf16[7488,128]{1,0:T(8,128)(2,1)}, u32[]{:S(2)}, u32[]{:S(2)}) collective-permute-start(bf16[7488,128]{1,0:T(8,128)(2,1)} %get-tuple-element.49.refs_0_), channel_id=1, source_target_pairs={{0,6},{1,7},{2,0},{3,1},{4,2},{5,3},{6,4},{7,5},{8,14},{9,15},{10,... | collective-permute-start | bytes 5750792 | tf_op jit(solution)/shard_map/ppermute | solution.py:989
  636.0 25.9 %collective-permute-start.2 = (bf16[7488,128]{1,0:T(8,128)(2,1)}, bf16[7488,128]{1,0:T(8,128)(2,1)}, u32[]{:S(2)}, u32[]{:S(2)}) collective-permute-start(bf16[7488,128]{1,0:T(8,128)(2,1)} %broadcast_select_fusion), channel_id=1, source_target_pairs={{0,2},{1,7},{2,4},{3,1},{4,6},{5,3},{6,0},{7,5},{8,10},{9,15},{10,... | collective-permute-start | bytes 5750792 | tf_op jit(solution)/shard_map/ppermute | solution.py:989
  638.4 25.1 %collective-permute-start.4 = (bf16[7488,128]{1,0:T(8,128)(2,1)}, bf16[7488,128]{1,0:T(8,128)(2,1)}, u32[]{:S(2)}, u32[]{:S(2)}) collective-permute-start(bf16[7488,128]{1,0:T(8,128)(2,1)} %get-tuple-element.49.refs_0_), channel_id=1, source_target_pairs={{0,1},{1,0},{2,3},{3,2},{4,5},{5,4},{6,7},{7,6},{8,9},{9,8},{10,11... | collective-permute-start | bytes 5750792 | tf_op jit(solution)/shard_map/ppermute | solution.py:989
  638.4 25.1 %collective-permute-start.5 = (bf16[7488,128]{1,0:T(8,128)(2,1)}, bf16[7488,128]{1,0:T(8,128)(2,1)}, u32[]{:S(2)}, u32[]{:S(2)}) collective-permute-start(bf16[7488,128]{1,0:T(8,128)(2,1)} %collective-permute-done.refs_1_), channel_id=1, source_target_pairs={{0,1},{1,0},{2,3},{3,2},{4,5},{5,4},{6,7},{7,6},{8,9},{9,8},{10,11... | collective-permute-start | bytes 5750792 | tf_op jit(solution)/shard_map/ppermute | solution.py:989
  638.9 24.6 %collective-permute-start.6 = (bf16[7488,128]{1,0:T(8,128)(2,1)}, bf16[7488,128]{1,0:T(8,128)(2,1)}, u32[]{:S(2)}, u32[]{:S(2)}) collective-permute-start(bf16[7488,128]{1,0:T(8,128)(2,1)} %collective-permute-done.1.refs_2_), channel_id=1, source_target_pairs={{0,1},{1,0},{2,3},{3,2},{4,5},{5,4},{6,7},{7,6},{8,9},{9,8},{10,11... | collective-permute-start | bytes 5750792 | tf_op jit(solution)/shard_map/ppermute | solution.py:989
  661.8 11.2 %collective-permute-start.3 = (bf16[7488,128]{1,0:T(8,128)(2,1)}, bf16[7488,128]{1,0:T(8,128)(2,1)}, u32[]{:S(2)}, u32[]{:S(2)}) collective-permute-start(bf16[7488,128]{1,0:T(8,128)(2,1)} %collective-permute-done.2.refs_0_), channel_id=1, source_target_pairs={{0,1},{1,0},{2,3},{3,2},{4,5},{5,4},{6,7},{7,6},{8,9},{9,8},{10,11... | collective-permute-start | bytes 5750792 | tf_op jit(solution)/shard_map/ppermute | solution.py:989

commit v7 on v6

--- a/solution.py
+++ b/solution.py
@@ -52,6 +52,10 @@
 def wait(copies):
     for copy in copies:
         copy.wait()
+
+
+def moves(moved):
+    return cost(COPY_FLOPS * moved, moved)
 
 
 def cost(flops, moved):
@@ -499,32 +503,37 @@
             for owner in range(CORES * chips):
                 gu.mine[slot, owner % CORES, owner // CORES, at, :] = g[owner * rows : (owner + 1) * rows, c * LANES : (c + 1) * LANES]
 
-    def compute_down(j, h):
-        slot = lax.rem(down_of(j), dn.slots)
-        owner = parity(lax.rem(j, blocks))
-        chips_here = [2 * h, 2 * h + 1]
-        z = strip(chips_here[0] * LANES, 2 * LANES)
+    def compute_down(j, _):
+        slot, owner = lax.rem(down_of(j), dn.slots), parity(lax.rem(j, blocks))
 
         @pl.when(~is_last(j))
         def _():
-            g = dot(dyt_ref[...], z_ref[:, z]).astype(BF16)
-            for c, at in enumerate(chips_here):
-                dn.mine[slot, owner, at, :, :] = g[:, c * LANES : (c + 1) * LANES]
+            g = dot(dyt_ref[...], z_ref[...]).astype(BF16)
+            for c in range(chips):
+                dn.mine[slot, owner, c, :, :] = g[:, c * LANES : (c + 1) * LANES]
 
         @pl.when(is_last(j))
         def _():
-            g = dot(dyt_ref[...], z_ref[:, z])
             half = LANES // 2
             low = lax.broadcasted_iota(jnp.int32, (small, LANES), 1) < half
-            for c, at in enumerate(chips_here):
-                both = g[:, c * LANES : (c + 1) * LANES]
-                turned = pltpu.roll(both, half, 1)
-                dn.mine[slot, 0, at, head(small), :] = jnp.where(low, both[:small], turned[small:]).astype(BF16)
-                dn.mine[slot, 1, at, head(small), :] = jnp.where(low, turned[:small], both[small:]).astype(BF16)
+
+            def one(h, _):
+                both = dot(dyt_ref[...], z_ref[:, strip(h * 2 * LANES, 2 * LANES)])
+                for c in range(2):
+                    straight = both[:, c * LANES : (c + 1) * LANES]
+                    turned = pltpu.roll(straight, half, 1)
+                    dn.mine[slot, 0, 2 * h + c, head(small), :] = jnp.where(low, straight[:small], turned[small:]).astype(BF16)
+                    dn.mine[slot, 1, 2 * h + c, head(small), :] = jnp.where(low, turned[:small], straight[small:]).astype(BF16)
+                return h
+
+            lax.fori_loop(0, chips // 2, one, 0)
 
     def compute_da(j, t):
-        slot, part = parity(j), strip(t * tile, tile)
-        da_ref[part, :] += dot(dgu_ref[0, part, :], wg_ref[slot], NT) + dot(dgu_ref[1, part, :], wu_ref[slot], NT)
+        slot, part = parity(j), strip(t * 2 * tile, 2 * tile)
+        middle = lane_blocks // 2 * LANES
+        for begin, end in ((0, middle), (middle, d)):
+            some = pl.ds(begin, end - begin)
+            da_ref[part, some] += dot(dgu_ref[0, part, :], wg_ref[slot, some, :], NT) + dot(dgu_ref[1, part, :], wu_ref[slot, some, :], NT)
 
     def begin_change(t):
         load(h_hbm, a_tile, t, 0).start()
@@ -572,17 +581,14 @@
         start(dn_state(n, rows))
 
     events = {
-        "tile1": [(for_down, dn_new, 2)],
-        "tile2": [(on, gu.event2, 1)],
-        "tile3": [(upper_down, dn.gather3, 3), (for_down, dn.event2, 1)],
-        "gate0": [(on, gu_load, 1)],
-        "gate1": [(on, gu.event0), (early, gu.gather3, 3)],
-        "down0": [(upper_down, dn.gather2, 2)],
-        "down1": [(for_down, dn.event0), (upper_down, dn.gather4, 3), (on, gu.event1)],
-        "back0": [(early, gu.gather4, 3)],
-        "back1": [(early, gu.gather2, 2), (for_down, dn.event1)],
-        "back2": [(on, gu_new, 1)],
-        "back3": [(for_down, dn_load, 1)],
+        "tile0": [(on, gu_new, 2)],
+        "tile1": [(upper_down, dn.gather2, 2), (for_down, dn_load, 1)],
+        "tile3": [(upper_down, dn.gather3, 3), (on, gu.event2, 1)],
+        "down0": [(for_down, dn.event0)],
+        "gate0": [(early, gu.gather3, 3), (for_down, dn.event1)],
+        "gate1": [(on, gu.event0), (early, gu.gather4, 3), (early, gu.gather2, 2), (for_down, dn_new, 1)],
+        "back0": [(upper_down, dn.gather4, 3), (on, gu.event1), (on, gu_load, 1)],
+        "back1": [(for_down, dn.event2)],
     }
     longest = max(sum(ago) for these in events.values() for _, _, *ago in these)
 
@@ -610,22 +616,23 @@
 
             lax.fori_loop(0, number, one, 0)
 
-        def da_tile(j, t):
-            fetch = load(a_hbm.at[0], a_tile, t, 0)
-            pl.when(changes)(fetch.start)
-            pl.when(changes & (t + 1 == tiles))(lambda: begin_change(0))
+        def da_tiles(j, t):
+            fetch = [load(a_hbm.at[0], a_tile, 2 * t + i, 0) for i in range(2)]
+            pl.when(changes)(lambda: start(fetch))
             compute_da(j, t)
 
             @pl.when(changes)
             def _():
-                fetch.wait()
-                turn(a_tile, parity(t), at_ref, strip(t * tile, tile))
+                for i, one in enumerate(fetch):
+                    one.wait()
+                    turn(a_tile, i, at_ref, strip((2 * t + i) * tile, tile))
+                pl.when(t > 0)(lambda: begin_change(0))
 
         parts("tile", tiles, busy, compute_tile)
         pl.when(busy & (j + 1 < steps) & ~changes)(lambda: start_tile(j + 1, 0))
+        parts("down", 1, busy, compute_down)
         parts("gate", 2, busy, compute_gate_up)
-        parts("down", chips // 2, busy, compute_down)
-        parts("back", tiles, busy & lower, da_tile)
+        parts("back", tiles // 2, busy & lower, da_tiles)
 
         pl.when(changes)(change_layer)
 
@@ -750,7 +757,11 @@
 def place_columns_kernel(layer, slots, x_hbm, *refs):
     gate_hbm, up_hbm, c_in, c_out, sem = refs[-5:]
     _, blocks, devices, _, chips, rows, _ = x_hbm.shape
-    wide, some = blocks * LANES, c_in.shape[2]
+    wide, there, some = blocks * LANES, *c_in.shape[1:3]
+    spots = [j // 2 + (blocks // 2 + 1) * (j % 2) for j in range(there)]
+    begins = [at for at in spots if at - 1 not in spots]
+    ends = [at + 1 for at in spots if at + 1 not in spots]
+    spans = list(zip(sorted(begins), sorted(ends)))
     turns = devices // some
 
     def place(unit):
@@ -758,19 +769,23 @@
 
     def loads(unit, slot):
         chip, owners = place(unit)
-        return [pltpu.make_async_copy(x_hbm.at[x_hbm.shape[0] - 1 - layer, :, pl.ds(owners, some), :, chip], c_in.at[slot], sem.at[slot, 0])]
+        return [pltpu.make_async_copy(x_hbm.at[x_hbm.shape[0] - 1 - layer, head(there), pl.ds(owners, some), :, chip], c_in.at[slot], sem.at[slot, 0])]
 
     def stores(unit, slot):
         chip, owners = place(unit)
-        at = layer, strip(owners * rows, some * rows), strip(chip * wide, wide)
-        return [pltpu.make_async_copy(c_out.at[slot, u], out.at[at], sem.at[slot, 1 + u]) for u, out in enumerate((gate_hbm, up_hbm))]
+        copies = []
+        for begin, end in spans:
+            size = (end - begin) * LANES
+            to = layer, strip(owners * rows, some * rows), pl.ds(pl.multiple_of(chip * wide + begin * LANES, LANES), size)
+            for u, out in enumerate((gate_hbm, up_hbm)):
+                copies.append(pltpu.make_async_copy(c_out.at[slot, u, :, pl.ds(begin * LANES, size)], out.at[to], sem.at[slot, 1 + len(copies)]))
+        return copies
 
     def work(unit, slot):
-        for j in range(blocks):
-            at = pl.ds((j // 2 + (blocks // 2 + 1) * (j % 2)) * LANES, LANES)
+        for j, at in enumerate(spots):
             for owner in range(some):
                 for u in range(2):
-                    c_out[slot, u, pl.ds(owner * rows, rows), at] = c_in[slot, j, owner, u]
+                    c_out[slot, u, pl.ds(owner * rows, rows), lanes(at)] = c_in[slot, j, owner, u]
 
     ring = Ring(chips * turns, slots, loads, stores, work)
     ring.begin()
@@ -782,6 +797,7 @@
     devices = chunks.shape[1]
     chips, rows = devices // CORES, d // devices
     x = chunks.reshape(layers, -1, devices, 2, chips, rows, LANES)
+    there = x.shape[1] - LATE * (layer == 0)
     return pl.pallas_call(
         functools.partial(place_columns_kernel, layer, slots),
         in_specs=[ANY] * (1 + len(into)),
@@ -789,12 +805,12 @@
         input_output_aliases={1 + i: i for i in range(len(into))},
         out_shape=[jax.ShapeDtypeStruct((layers, d, ff), BF16)] * 2,
         scratch_shapes=[
-            pltpu.VMEM((slots, x.shape[1], some, 2, rows, LANES), BF16),
+            pltpu.VMEM((slots, there, some, 2, rows, LANES), BF16),
             pltpu.VMEM((slots, 2, some * rows, ff // chips), BF16),
-            pltpu.SemaphoreType.DMA((slots, 3)),
+            pltpu.SemaphoreType.DMA((slots, devices)),
         ],
         compiler_params=pltpu.CompilerParams(vmem_limit_bytes=VMEM_BYTES),
-        cost_estimate=cost(COPY_FLOPS * 8 * d * ff, 8 * d * ff),
+        cost_estimate=moves(8 * d * ff),
         name="place_columns",
     )(x, *into)
 
@@ -847,7 +863,7 @@
             pltpu.SemaphoreType.DMA((slots, 15)),
         ],
         compiler_params=pltpu.CompilerParams(vmem_limit_bytes=VMEM_BYTES),
-        cost_estimate=cost(COPY_FLOPS * 18 * size, 18 * size),
+        cost_estimate=moves(18 * size),
         name="moments",
     )(*m, *v, *g)
 
@@ -900,7 +916,7 @@
             pltpu.SemaphoreType.DMA((slots, 3)),
         ],
         compiler_params=pltpu.CompilerParams(vmem_limit_bytes=VMEM_BYTES),
-        cost_estimate=cost(COPY_FLOPS * 4 * d * ff, 4 * d * ff),
+        cost_estimate=moves(4 * d * ff),
         name="place_rows",
     )(x)
 
@@ -968,7 +984,6 @@
             pltpu.SemaphoreType.DMA((number, 2 + LATE * ff // height)),
         ],
         compiler_params=pltpu.CompilerParams(vmem_limit_bytes=VMEM_BYTES),
-        cost_estimate=cost(COPY_FLOPS * 4 * number * rows * LANES, 4 * number * rows * LANES),
         name="place_blocks",
     )(me, *blocks, *weights)
 

time: 677 us -> 673 us (level)
  Pallas kernels: 664 us -> 657 us
  transfers between devices with their start and end apart: 7 -> 7, of which waited for: 1 -> 2; matrix products, arithmetic and copies ran while one was open for 0% -> 0% of each run, Pallas kernels for 11% -> 10%
where the time goes in v7:
time: 673 us
  Pallas kernels  657 us (98%)
  starting transfers between devices  11.3 us (2%)
    pallas_call x1, Pallas kernels, backward(): pl.pallas_call(functools.partial(backward_kernel, chips, tile), out_shape...  496 us
    pallas_call x1, Pallas kernels, forward(): pl.pallas_call(functools.partial(forward_kernel, tile), grid=(ff // width...  87.3 us
    pallas_call x2, Pallas kernels, place_columns(): pl.pallas_call(functools.partial(place_columns_kernel, layer, slots), in_...  27.9 us
    pallas_call x1, Pallas kernels, moments(): pl.pallas_call(functools.partial(moments_kernel, layers, parts, slots), i...  24.6 us
  transfers between devices with their start and end apart: 7, of which 2 were waited for; matrix products, arithmetic and copies ran while one was open for 0% of the time, Pallas kernels for 10%

profile of v7, /device:TPU:113, one launch (start us, length us, event | category | flops | bytes accessed | tf_op | source)
XLA Modules:
  0.0 672.7 jit_solution(17459674385804176767)
XLA Ops:
  0.6 87.3 %forward.1 = (bf16[2,2048,1152]{2,1,0:T(8,128)(2,1)}, bf16[2048,1152]{1,0:T(8,128)(2,1)}) custom-call(bf16[2048,1152]{1,0:T(8,128)(2,1)} %bitcast.7, bf16[2,1152,4608]{2,1,0:T(8,128)(2,1)} %refs_3_.2, bf16[2,1152,4608]{2,1,0:T(8,128)(2,1)} %refs_4_.2, bf16[2,4608,1152]{2,1,0:T(8,128)(2,1)} %refs_5_.2), custom_call_target="tpu_custom_call" | custom-call | flops 65229815808 | bytes 31850496 | tf_op jit(solution)/shard_map/forward/pallas_call | solution.py:121
  88.0 495.9 %backward.1 = (bf16[2,144,4608]{2,1,0:T(8,128)(2,1)}, bf16[2,144,4608]{2,1,0:T(8,128)(2,1)}, bf16[2,576,1152]{2,1,0:T(8,128)(2,1)}, bf16[18,8,1152,128]{3,2,1,0:...) custom-call(bf16[2,2048,1152]{2,1,0:T(8,128)(2,1)} %get-tuple-element.41.ref, ...), custom_call_target="tpu_custom_call" | custom-call | flops 304405807104 | bytes 127401984 | tf_op jit(solution)/shard_map/backward/pallas_call | solution.py:686
  583.8 2.2 collective-permute-start
  586.0 1.3 collective-permute-start.1
  587.4 15.2 %place_columns.2 = (bf16[2,1152,4608]{2,1,0:T(8,128)(2,1)}, bf16[2,1152,4608]{2,1,0:T(8,128)(2,1)}) custom-call(bf16[2,9,8,2,4,144,128]{6,5,4,3,2,1,0:T(8,128)(2,1)} %bitcast.5), custom_call_target="tpu_custom_call" | custom-call | flops 2717908992 | bytes 42467328 | tf_op jit(solution)/shard_map/place_columns/pallas_call | solution.py:801
  602.5 24.6 %moments.1 = (f32[2,144,4608]{2,1,0:T(8,128)}, f32[2,144,4608]{2,1,0:T(8,128)}, f32[2,576,1152]{2,1,0:T(8,128)}, f32[2,144,4608]{2,1,0:T(8,128)}, f32[2,144,4608]{2,1,0:T(8,128)}, /*index=5*/f32[2,576,1152]{2,1,0:T(8,128)}) custom-call(f32[2,144,4608]{2,1,0:T(8,128)} %refs_0_.1, f32[2,144,4608]{2,1,0:T(8,128)} %refs_1_.1, f32[2,576,1152]{2,1,0:T(8,128)} %refs_2_.1, ...), custom_call_target="tpu_custom_call" | custom-call | flops 4586471424 | bytes 71663616 | tf_op jit(solution)/shard_map/moments/pallas_call | solution.py:854
  627.2 0.2 collective-permute-done.refs_1_
  627.4 0.3 collective-permute-done.1.refs_2_
  627.7 3.0 broadcast_select_fusion
  630.6 2.3 collective-permute-start.2
  632.9 1.5 collective-permute-start.4
  634.4 0.0 collective-permute-start.5
  634.4 0.5 collective-permute-start.6
  635.0 12.8 %place_columns.3 = (bf16[2,1152,4608]{2,1,0:T(8,128)(2,1)}, bf16[2,1152,4608]{2,1,0:T(8,128)(2,1)}) custom-call(bf16[2,9,8,2,4,144,128]{6,5,4,3,2,1,0:T(8,128)(2,1)} %bitcast.6, bf16[2,1152,4608]{2,1,0:T(8,128)(2,1)} %get-tuple-element.50.refs_0_, bf16[2,1152,4608]{2,1,0:T(8,128)(2,1)} %get-tuple-element.51.refs_1_), custom_call_target="tpu_custom_call", output_to_operand_aliasing={{0}: (1, {}), {1}: (2, {})} | custom-call | flops 2717908992 | bytes 42467328 | tf_op jit(solution)/shard_map/place_columns/pallas_call | solution.py:801
  647.7 7.9 %place_rows.1.refs_8_ = bf16[2,4608,1152]{2,1,0:T(8,128)(2,1)} custom-call(bf16[1,5,8,1152,128]{4,3,2,1,0:T(8,128)(2,1)} %bitcast.9), custom_call_target="tpu_custom_call" | custom-call | flops 1358954496 | bytes 21233664 | tf_op jit(solution)/shard_map/place_rows/pallas_call | solution.py:908
  655.7 0.0 collective-permute-done.2.refs_0_
  655.7 3.4 collective-permute-start.3
  659.1 0.0 collective-permute-done.4.refs_3_
  659.1 0.0 collective-permute-done.5.refs_4_
  659.1 0.0 collective-permute-done.6.refs_5_
  659.1 9.5 %place_blocks.2 = (bf16[2,1152,4608]{2,1,0:T(8,128)(2,1)}, bf16[2,1152,4608]{2,1,0:T(8,128)(2,1)}, bf16[2,4608,1152]{2,1,0:T(8,128)(2,1)}) custom-call(s32[1]{0:T(128)} %bitcast.me_ref, bf16[7488,128]{1,0:T(8,128)(2,1)} %get-tuple-element.49.refs_0_, ...), custom_call_target="tpu_custom_call", output_to_operand_aliasing={{0}: (7, {}), {1}: (8, {}), {2}: (9, {})} | custom-call | tf_op jit(solution)/shard_map/place_blocks/pallas_call | solution.py:975
  668.7 0.0 collective-permute-done.3.refs_1_
  668.7 3.8 place_blocks.3
Async XLA Ops:
  583.8 43.5 %collective-permute-start = (bf16[7488,128]{1,0:T(8,128)(2,1)}, bf16[7488,128]{1,0:T(8,128)(2,1)}, u32[]{:S(2)}, u32[]{:S(2)}) collective-permute-start(bf16[7488,128]{1,0:T(8,128)(2,1)} %get-tuple-element.49.refs_0_), channel_id=1, source_target_pairs={{0,2},{1,3},{2,4},{3,5},{4,6},{5,7},{6,0},{7,1},{8,10},{9,11},{10,... | collective-permute-start | bytes 5750792 | tf_op jit(solution)/shard_map/ppermute | solution.py:1004
  586.0 41.6 %collective-permute-start.1 = (bf16[7488,128]{1,0:T(8,128)(2,1)}, bf16[7488,128]{1,0:T(8,128)(2,1)}, u32[]{:S(2)}, u32[]{:S(2)}) collective-permute-start(bf16[7488,128]{1,0:T(8,128)(2,1)} %get-tuple-element.49.refs_0_), channel_id=1, source_target_pairs={{0,6},{1,7},{2,0},{3,1},{4,2},{5,3},{6,4},{7,5},{8,14},{9,15},{10,... | collective-permute-start | bytes 5750792 | tf_op jit(solution)/shard_map/ppermute | solution.py:1004
  630.6 25.1 %collective-permute-start.2 = (bf16[7488,128]{1,0:T(8,128)(2,1)}, bf16[7488,128]{1,0:T(8,128)(2,1)}, u32[]{:S(2)}, u32[]{:S(2)}) collective-permute-start(bf16[7488,128]{1,0:T(8,128)(2,1)} %broadcast_select_fusion), channel_id=1, source_target_pairs={{0,2},{1,7},{2,4},{3,1},{4,6},{5,3},{6,0},{7,5},{8,10},{9,15},{10,... | collective-permute-start | bytes 5750792 | tf_op jit(solution)/shard_map/ppermute | solution.py:1004
  632.9 26.2 %collective-permute-start.4 = (bf16[7488,128]{1,0:T(8,128)(2,1)}, bf16[7488,128]{1,0:T(8,128)(2,1)}, u32[]{:S(2)}, u32[]{:S(2)}) collective-permute-start(bf16[7488,128]{1,0:T(8,128)(2,1)} %get-tuple-element.49.refs_0_), channel_id=1, source_target_pairs={{0,1},{1,0},{2,3},{3,2},{4,5},{5,4},{6,7},{7,6},{8,9},{9,8},{10,11... | collective-permute-start | bytes 5750792 | tf_op jit(solution)/shard_map/ppermute | solution.py:1004
  634.4 24.7 %collective-permute-start.5 = (bf16[7488,128]{1,0:T(8,128)(2,1)}, bf16[7488,128]{1,0:T(8,128)(2,1)}, u32[]{:S(2)}, u32[]{:S(2)}) collective-permute-start(bf16[7488,128]{1,0:T(8,128)(2,1)} %collective-permute-done.refs_1_), channel_id=1, source_target_pairs={{0,1},{1,0},{2,3},{3,2},{4,5},{5,4},{6,7},{7,6},{8,9},{9,8},{10,11... | collective-permute-start | bytes 5750792 | tf_op jit(solution)/shard_map/ppermute | solution.py:1004
  634.4 24.7 %collective-permute-start.6 = (bf16[7488,128]{1,0:T(8,128)(2,1)}, bf16[7488,128]{1,0:T(8,128)(2,1)}, u32[]{:S(2)}, u32[]{:S(2)}) collective-permute-start(bf16[7488,128]{1,0:T(8,128)(2,1)} %collective-permute-done.1.refs_2_), channel_id=1, source_target_pairs={{0,1},{1,0},{2,3},{3,2},{4,5},{5,4},{6,7},{7,6},{8,9},{9,8},{10,11... | collective-permute-start | bytes 5750792 | tf_op jit(solution)/shard_map/ppermute | solution.py:1004
  655.7 13.0 %collective-permute-start.3 = (bf16[7488,128]{1,0:T(8,128)(2,1)}, bf16[7488,128]{1,0:T(8,128)(2,1)}, u32[]{:S(2)}, u32[]{:S(2)}) collective-permute-start(bf16[7488,128]{1,0:T(8,128)(2,1)} %collective-permute-done.2.refs_0_), channel_id=1, source_target_pairs={{0,1},{1,0},{2,3},{3,2},{4,5},{5,4},{6,7},{7,6},{8,9},{9,8},{10,11... | collective-permute-start | bytes 5750792 | tf_op jit(solution)/shard_map/ppermute | solution.py:1004

commit v8 on v7

--- a/solution.py
+++ b/solution.py
@@ -937,7 +937,7 @@
     def put(i):
         hops, flip = wheres[i]
         side = 1 - core if flip else core
-        owner = lax.rem(chip + hops + chips, chips) * CORES + side
+        owner = lax.rem(chip + hops * (1 - 2 * side) + chips, chips) * CORES + side
         copies = [pltpu.make_async_copy(down.at[i], down_hbm.at[0, strip(owner * height, height)], sem.at[i, 1])]
         for n in range(LATE):
             step = 2 * pairs + 1 - LATE + n
@@ -991,8 +991,8 @@
 def solution(mesh):
     group = mesh.shape["dp"]
     swap = [(i, i ^ 1) for i in range(group)]
-    right = [(i, (i + CORES) % group) for i in range(group)]
-    left = [(i, (i - CORES) % group) for i in range(group)]
+    onward = [(i, (i + CORES * (1 - 2 * (i % CORES))) % group) for i in range(group)]
+    back = [(to, i) for i, to in onward]
 
     def step(x, dy, *arrays):
         weights, m, v = (arrays[i : i + 3] for i in (0, 3, 6))
@@ -1003,19 +1003,20 @@
         def send(block, to):
             return lax.ppermute(block, "dp", to)
 
-        from_left, from_right = send(own, right), send(own, left)
+        behind, ahead = send(own, onward), send(own, back)
         gate, up = place_columns(columns, 1, layers, d, ff)
         first, *states = moments(m, v, sums)
-        gate, first, from_left, from_right = lax.optimization_barrier((gate, first, from_left, from_right))
-        opposite = send(jnp.where(lax.rem(lax.axis_index("dp"), CORES) == 0, from_left, from_right), [(right, left)[i % CORES][i] for i in range(group)])
-        near = {(0, 0): own, (-1, 0): from_left, (1, 0): from_right}
+        gate, first, behind, ahead = lax.optimization_barrier((gate, first, behind, ahead))
+        opposite = send(behind, onward)
+        near = {(0, 0): own, (-1, 0): behind, (1, 0): ahead}
         other = {(hops, 1): send(block, swap) for (hops, _), block in near.items()}
         gate, up = place_columns(columns, 0, layers, d, ff, (gate, up))
         up, rows = lax.optimization_barrier((up, rows))
         down = place_rows(rows, layers, d, ff)
+        gate, up, down = place_blocks(me, near, (gate, up, down))
         down, opposite = lax.optimization_barrier((down, opposite))
         last = send(opposite, swap)
-        weights = place_blocks(me, {**near, **other}, (gate, up, down))
+        weights = place_blocks(me, other, (gate, up, down))
         weights = place_blocks(me, {(2, 0): opposite, (2, 1): last}, weights)
         return (*weights, first, *states)
 

time: 673 us -> 668 us (level)
    pallas_call x2 -> x3, Pallas kernels: 13.4 us -> 13.6 us  [place_blocks(): pl.pallas_call(functools.partial(place_blocks_kernel, wheres), in_specs=[...]
  transfers between devices with their start and end apart: 7 -> 7, of which waited for: 2 -> 1; matrix products, arithmetic and copies ran while one was open for 0% -> 0% of each run, Pallas kernels for 10% -> 11%
where the time goes in v8:
time: 668 us
  Pallas kernels  657 us (98%)
    pallas_call x1, Pallas kernels, backward(): pl.pallas_call(functools.partial(backward_kernel, chips, tile), out_shape...  496 us
    pallas_call x1, Pallas kernels, forward(): pl.pallas_call(functools.partial(forward_kernel, tile), grid=(ff // width...  87.3 us
    pallas_call x2, Pallas kernels, place_columns(): pl.pallas_call(functools.partial(place_columns_kernel, layer, slots), in_...  27.9 us
    pallas_call x1, Pallas kernels, moments(): pl.pallas_call(functools.partial(moments_kernel, layers, parts, slots), i...  24.6 us
    pallas_call x3, Pallas kernels, place_blocks(): pl.pallas_call(functools.partial(place_blocks_kernel, wheres), in_specs=[...  13.6 us
  transfers between devices with their start and end apart: 7, of which 1 were waited for; matrix products, arithmetic and copies ran while one was open for 0% of the time, Pallas kernels for 11%

profile of v8, /device:TPU:113, one launch (start us, length us, event | category | flops | bytes accessed | tf_op | source)
XLA Modules:
  0.0 668.0 jit_solution(13220698210465411432)
XLA Ops:
  0.6 87.3 %forward.1 = (bf16[2,2048,1152]{2,1,0:T(8,128)(2,1)}, bf16[2048,1152]{1,0:T(8,128)(2,1)}) custom-call(bf16[2048,1152]{1,0:T(8,128)(2,1)} %bitcast.7, bf16[2,1152,4608]{2,1,0:T(8,128)(2,1)} %refs_3_.2, bf16[2,1152,4608]{2,1,0:T(8,128)(2,1)} %refs_4_.2, bf16[2,4608,1152]{2,1,0:T(8,128)(2,1)} %refs_5_.2), custom_call_target="tpu_custom_call" | custom-call | flops 65229815808 | bytes 31850496 | tf_op jit(solution)/shard_map/forward/pallas_call | solution.py:121
  88.0 495.8 %backward.1 = (bf16[2,144,4608]{2,1,0:T(8,128)(2,1)}, bf16[2,144,4608]{2,1,0:T(8,128)(2,1)}, bf16[2,576,1152]{2,1,0:T(8,128)(2,1)}, bf16[18,8,1152,128]{3,2,1,0:...) custom-call(bf16[2,2048,1152]{2,1,0:T(8,128)(2,1)} %get-tuple-element.44.ref, ...), custom_call_target="tpu_custom_call" | custom-call | flops 304405807104 | bytes 127401984 | tf_op jit(solution)/shard_map/backward/pallas_call | solution.py:686
  583.8 3.5 collective-permute-start
  587.2 0.0 collective-permute-start.1
  587.2 15.2 %place_columns.2 = (bf16[2,1152,4608]{2,1,0:T(8,128)(2,1)}, bf16[2,1152,4608]{2,1,0:T(8,128)(2,1)}) custom-call(bf16[2,9,8,2,4,144,128]{6,5,4,3,2,1,0:T(8,128)(2,1)} %bitcast.5), custom_call_target="tpu_custom_call" | custom-call | flops 2717908992 | bytes 42467328 | tf_op jit(solution)/shard_map/place_columns/pallas_call | solution.py:801
  602.4 24.6 %moments.1 = (f32[2,144,4608]{2,1,0:T(8,128)}, f32[2,144,4608]{2,1,0:T(8,128)}, f32[2,576,1152]{2,1,0:T(8,128)}, f32[2,144,4608]{2,1,0:T(8,128)}, f32[2,144,4608]{2,1,0:T(8,128)}, /*index=5*/f32[2,576,1152]{2,1,0:T(8,128)}) custom-call(f32[2,144,4608]{2,1,0:T(8,128)} %refs_0_.1, f32[2,144,4608]{2,1,0:T(8,128)} %refs_1_.1, f32[2,576,1152]{2,1,0:T(8,128)} %refs_2_.1, ...), custom_call_target="tpu_custom_call" | custom-call | flops 4586471424 | bytes 71663616 | tf_op jit(solution)/shard_map/moments/pallas_call | solution.py:854
  627.0 0.0 collective-permute-done.refs_1_
  627.1 5.2 collective-permute-done.1.refs_2_
  632.3 0.0 collective-permute-start.2
  632.3 0.4 collective-permute-start.4
  632.7 0.1 collective-permute-start.5
  632.8 12.8 %place_columns.3 = (bf16[2,1152,4608]{2,1,0:T(8,128)(2,1)}, bf16[2,1152,4608]{2,1,0:T(8,128)(2,1)}) custom-call(bf16[2,9,8,2,4,144,128]{6,5,4,3,2,1,0:T(8,128)(2,1)} %bitcast.6, bf16[2,1152,4608]{2,1,0:T(8,128)(2,1)} %get-tuple-element.55.refs_0_, bf16[2,1152,4608]{2,1,0:T(8,128)(2,1)} %get-tuple-element.56.refs_1_), custom_call_target="tpu_custom_call", output_to_operand_aliasing={{0}: (1, {}), {1}: (2, {})} | custom-call | flops 2717908992 | bytes 42467328 | tf_op jit(solution)/shard_map/place_columns/pallas_call | solution.py:801
  645.6 0.5 collective-permute-start.6
  646.1 7.9 %place_rows.1.refs_5_ = bf16[2,4608,1152]{2,1,0:T(8,128)(2,1)} custom-call(bf16[1,5,8,1152,128]{4,3,2,1,0:T(8,128)(2,1)} %bitcast.9), custom_call_target="tpu_custom_call" | custom-call | flops 1358954496 | bytes 21233664 | tf_op jit(solution)/shard_map/place_rows/pallas_call | solution.py:908
  654.0 4.9 place_blocks.3
  658.9 0.0 collective-permute-done.2.refs_0_
  658.9 0.2 collective-permute-start.3
  659.1 0.0 collective-permute-done.4.refs_0_
  659.1 0.0 collective-permute-done.5.refs_1_
  659.1 0.0 collective-permute-done.6.refs_2_
  659.1 4.9 place_blocks.4
  664.0 0.0 collective-permute-done.3.refs_1_
  664.0 3.8 place_blocks.5
Async XLA Ops:
  583.8 43.3 %collective-permute-start = (bf16[7488,128]{1,0:T(8,128)(2,1)}, bf16[7488,128]{1,0:T(8,128)(2,1)}, u32[]{:S(2)}, u32[]{:S(2)}) collective-permute-start(bf16[7488,128]{1,0:T(8,128)(2,1)} %get-tuple-element.46.refs_0_), channel_id=1, source_target_pairs={{0,2},{1,7},{2,4},{3,1},{4,6},{5,3},{6,0},{7,5},{8,10},{9,15},{10,... | collective-permute-start | bytes 5750792 | tf_op jit(solution)/shard_map/ppermute | solution.py:1004
  587.2 45.1 %collective-permute-start.1 = (bf16[7488,128]{1,0:T(8,128)(2,1)}, bf16[7488,128]{1,0:T(8,128)(2,1)}, u32[]{:S(2)}, u32[]{:S(2)}) collective-permute-start(bf16[7488,128]{1,0:T(8,128)(2,1)} %get-tuple-element.46.refs_0_), channel_id=1, source_target_pairs={{2,0},{7,1},{4,2},{1,3},{6,4},{3,5},{0,6},{5,7},{10,8},{15,9},{12,... | collective-permute-start | bytes 5750792 | tf_op jit(solution)/shard_map/ppermute | solution.py:1004
  632.3 26.6 %collective-permute-start.2 = (bf16[7488,128]{1,0:T(8,128)(2,1)}, bf16[7488,128]{1,0:T(8,128)(2,1)}, u32[]{:S(2)}, u32[]{:S(2)}) collective-permute-start(bf16[7488,128]{1,0:T(8,128)(2,1)} %collective-permute-done.refs_1_), channel_id=1, source_target_pairs={{0,2},{1,7},{2,4},{3,1},{4,6},{5,3},{6,0},{7,5},{8,10},{9,15},{10,... | collective-permute-start | bytes 5750792 | tf_op jit(solution)/shard_map/ppermute | solution.py:1004
  632.3 26.8 %collective-permute-start.4 = (bf16[7488,128]{1,0:T(8,128)(2,1)}, bf16[7488,128]{1,0:T(8,128)(2,1)}, u32[]{:S(2)}, u32[]{:S(2)}) collective-permute-start(bf16[7488,128]{1,0:T(8,128)(2,1)} %get-tuple-element.46.refs_0_), channel_id=1, source_target_pairs={{0,1},{1,0},{2,3},{3,2},{4,5},{5,4},{6,7},{7,6},{8,9},{9,8},{10,11... | collective-permute-start | bytes 5750792 | tf_op jit(solution)/shard_map/ppermute | solution.py:1004
  632.7 26.4 %collective-permute-start.5 = (bf16[7488,128]{1,0:T(8,128)(2,1)}, bf16[7488,128]{1,0:T(8,128)(2,1)}, u32[]{:S(2)}, u32[]{:S(2)}) collective-permute-start(bf16[7488,128]{1,0:T(8,128)(2,1)} %collective-permute-done.refs_1_), channel_id=1, source_target_pairs={{0,1},{1,0},{2,3},{3,2},{4,5},{5,4},{6,7},{7,6},{8,9},{9,8},{10,11... | collective-permute-start | bytes 5750792 | tf_op jit(solution)/shard_map/ppermute | solution.py:1004
  645.6 13.5 %collective-permute-start.6 = (bf16[7488,128]{1,0:T(8,128)(2,1)}, bf16[7488,128]{1,0:T(8,128)(2,1)}, u32[]{:S(2)}, u32[]{:S(2)}) collective-permute-start(bf16[7488,128]{1,0:T(8,128)(2,1)} %collective-permute-done.1.refs_2_), channel_id=1, source_target_pairs={{0,1},{1,0},{2,3},{3,2},{4,5},{5,4},{6,7},{7,6},{8,9},{9,8},{10,11... | collective-permute-start | bytes 5750792 | tf_op jit(solution)/shard_map/ppermute | solution.py:1004
  658.9 5.1 collective-permute-start.3

commit v9 on v8

--- a/solution.py
+++ b/solution.py
@@ -489,10 +489,11 @@
             dgu_ref[1, part, some] = (dz * act).astype(BF16)
             dgu_ref[0, part, some] = (dz * up * (s + act * (1 - s))).astype(BF16)
 
+        turn(a_tile, here, at_ref, part)
+        turn(dy_tile, here, dyt_ref, part)
+
         @pl.when(j == 0)
         def _():
-            turn(a_tile, here, at_ref, part)
-            turn(dy_tile, here, dyt_ref, part)
             da_ref[part, :] = jnp.zeros((tile, d), F32)
 
     def compute_gate_up(j, u):
@@ -559,7 +560,6 @@
 
             lax.fori_loop(0, tile // small_tile, piece, 0)
             keep(t).start()
-            turn(dy_tile, slot, dyt_ref, strip(t * tile, tile))
             return 0
 
         lax.fori_loop(0, tiles, one, 0)
@@ -616,23 +616,15 @@
 
             lax.fori_loop(0, number, one, 0)
 
-        def da_tiles(j, t):
-            fetch = [load(a_hbm.at[0], a_tile, 2 * t + i, 0) for i in range(2)]
-            pl.when(changes)(lambda: start(fetch))
+        def da_halves(j, t):
+            pl.when(changes & (t == 0))(lambda: begin_change(0))
             compute_da(j, t)
-
-            @pl.when(changes)
-            def _():
-                for i, one in enumerate(fetch):
-                    one.wait()
-                    turn(a_tile, i, at_ref, strip((2 * t + i) * tile, tile))
-                pl.when(t > 0)(lambda: begin_change(0))
 
         parts("tile", tiles, busy, compute_tile)
         pl.when(busy & (j + 1 < steps) & ~changes)(lambda: start_tile(j + 1, 0))
         parts("down", 1, busy, compute_down)
         parts("gate", 2, busy, compute_gate_up)
-        parts("back", tiles // 2, busy & lower, da_tiles)
+        parts("back", tiles // 2, busy & lower, da_halves)
 
         pl.when(changes)(change_layer)
 

time: 668 us -> 665 us (level)
  transfers between devices with their start and end apart: 7 -> 7, of which waited for: 1 -> 2; matrix products, arithmetic and copies ran while one was open for 0% -> 0% of each run, Pallas kernels for 11% -> 11%
where the time goes in v9:
time: 665 us
  Pallas kernels  657 us (99%)
    pallas_call x1, Pallas kernels, backward(): pl.pallas_call(functools.partial(backward_kernel, chips, tile), out_shape...  495 us
    pallas_call x1, Pallas kernels, forward(): pl.pallas_call(functools.partial(forward_kernel, tile), grid=(ff // width...  87.3 us
    pallas_call x2, Pallas kernels, place_columns(): pl.pallas_call(functools.partial(place_columns_kernel, layer, slots), in_...  27.9 us
    pallas_call x1, Pallas kernels, moments(): pl.pallas_call(functools.partial(moments_kernel, layers, parts, slots), i...  24.6 us
    pallas_call x3, Pallas kernels, place_blocks(): pl.pallas_call(functools.partial(place_blocks_kernel, wheres), in_specs=[...  13.6 us
  transfers between devices with their start and end apart: 7, of which 2 were waited for; matrix products, arithmetic and copies ran while one was open for 0% of the time, Pallas kernels for 11%

profile of v9, /device:TPU:113, one launch (start us, length us, event | category | flops | bytes accessed | tf_op | source)
XLA Modules:
  0.0 664.8 jit_solution(12050332371205211712)
XLA Ops:
  0.6 87.3 %forward.1 = (bf16[2,2048,1152]{2,1,0:T(8,128)(2,1)}, bf16[2048,1152]{1,0:T(8,128)(2,1)}) custom-call(bf16[2048,1152]{1,0:T(8,128)(2,1)} %bitcast.7, bf16[2,1152,4608]{2,1,0:T(8,128)(2,1)} %refs_3_.2, bf16[2,1152,4608]{2,1,0:T(8,128)(2,1)} %refs_4_.2, bf16[2,4608,1152]{2,1,0:T(8,128)(2,1)} %refs_5_.2), custom_call_target="tpu_custom_call" | custom-call | flops 65229815808 | bytes 31850496 | tf_op jit(solution)/shard_map/forward/pallas_call | solution.py:121
  88.0 495.3 %backward.1 = (bf16[2,144,4608]{2,1,0:T(8,128)(2,1)}, bf16[2,144,4608]{2,1,0:T(8,128)(2,1)}, bf16[2,576,1152]{2,1,0:T(8,128)(2,1)}, bf16[18,8,1152,128]{3,2,1,0:...) custom-call(bf16[2,2048,1152]{2,1,0:T(8,128)(2,1)} %get-tuple-element.44.ref, ...), custom_call_target="tpu_custom_call" | custom-call | flops 304405807104 | bytes 127401984 | tf_op jit(solution)/shard_map/backward/pallas_call | solution.py:678
  583.3 0.5 collective-permute-start
  583.8 1.0 collective-permute-start.1
  584.8 15.2 %place_columns.2 = (bf16[2,1152,4608]{2,1,0:T(8,128)(2,1)}, bf16[2,1152,4608]{2,1,0:T(8,128)(2,1)}) custom-call(bf16[2,9,8,2,4,144,128]{6,5,4,3,2,1,0:T(8,128)(2,1)} %bitcast.5), custom_call_target="tpu_custom_call" | custom-call | flops 2717908992 | bytes 42467328 | tf_op jit(solution)/shard_map/place_columns/pallas_call | solution.py:793
  600.0 24.6 %moments.1 = (f32[2,144,4608]{2,1,0:T(8,128)}, f32[2,144,4608]{2,1,0:T(8,128)}, f32[2,576,1152]{2,1,0:T(8,128)}, f32[2,144,4608]{2,1,0:T(8,128)}, f32[2,144,4608]{2,1,0:T(8,128)}, /*index=5*/f32[2,576,1152]{2,1,0:T(8,128)}) custom-call(f32[2,144,4608]{2,1,0:T(8,128)} %refs_0_.1, f32[2,144,4608]{2,1,0:T(8,128)} %refs_1_.1, f32[2,576,1152]{2,1,0:T(8,128)} %refs_2_.1, ...), custom_call_target="tpu_custom_call" | custom-call | flops 4586471424 | bytes 71663616 | tf_op jit(solution)/shard_map/moments/pallas_call | solution.py:846
  624.6 1.5 collective-permute-done.refs_1_
  626.1 2.2 collective-permute-done.1.refs_2_
  628.2 0.3 collective-permute-start.2
  628.5 1.0 collective-permute-start.4
  629.5 0.1 collective-permute-start.5
  629.6 12.8 %place_columns.3 = (bf16[2,1152,4608]{2,1,0:T(8,128)(2,1)}, bf16[2,1152,4608]{2,1,0:T(8,128)(2,1)}) custom-call(bf16[2,9,8,2,4,144,128]{6,5,4,3,2,1,0:T(8,128)(2,1)} %bitcast.6, bf16[2,1152,4608]{2,1,0:T(8,128)(2,1)} %get-tuple-element.55.refs_0_, bf16[2,1152,4608]{2,1,0:T(8,128)(2,1)} %get-tuple-element.56.refs_1_), custom_call_target="tpu_custom_call", output_to_operand_aliasing={{0}: (1, {}), {1}: (2, {})} | custom-call | flops 2717908992 | bytes 42467328 | tf_op jit(solution)/shard_map/place_columns/pallas_call | solution.py:793
  642.4 0.5 collective-permute-start.6
  642.8 7.9 %place_rows.1.refs_5_ = bf16[2,4608,1152]{2,1,0:T(8,128)(2,1)} custom-call(bf16[1,5,8,1152,128]{4,3,2,1,0:T(8,128)(2,1)} %bitcast.9), custom_call_target="tpu_custom_call" | custom-call | flops 1358954496 | bytes 21233664 | tf_op jit(solution)/shard_map/place_rows/pallas_call | solution.py:900
  650.8 4.9 place_blocks.3
  655.7 0.0 collective-permute-done.2.refs_0_
  655.7 0.2 collective-permute-start.3
  655.9 0.0 collective-permute-done.4.refs_0_
  655.9 0.0 collective-permute-done.5.refs_1_
  655.9 0.0 collective-permute-done.6.refs_2_
  655.9 4.9 place_blocks.4
  660.8 0.0 collective-permute-done.3.refs_1_
  660.8 3.8 place_blocks.5
Async XLA Ops:
  583.3 42.8 %collective-permute-start = (bf16[7488,128]{1,0:T(8,128)(2,1)}, bf16[7488,128]{1,0:T(8,128)(2,1)}, u32[]{:S(2)}, u32[]{:S(2)}) collective-permute-start(bf16[7488,128]{1,0:T(8,128)(2,1)} %get-tuple-element.46.refs_0_), channel_id=1, source_target_pairs={{0,2},{1,7},{2,4},{3,1},{4,6},{5,3},{6,0},{7,5},{8,10},{9,15},{10,... | collective-permute-start | bytes 5750792 | tf_op jit(solution)/shard_map/ppermute | solution.py:996
  583.8 44.5 %collective-permute-start.1 = (bf16[7488,128]{1,0:T(8,128)(2,1)}, bf16[7488,128]{1,0:T(8,128)(2,1)}, u32[]{:S(2)}, u32[]{:S(2)}) collective-permute-start(bf16[7488,128]{1,0:T(8,128)(2,1)} %get-tuple-element.46.refs_0_), channel_id=1, source_target_pairs={{2,0},{7,1},{4,2},{1,3},{6,4},{3,5},{0,6},{5,7},{10,8},{15,9},{12,... | collective-permute-start | bytes 5750792 | tf_op jit(solution)/shard_map/ppermute | solution.py:996
  628.2 27.5 %collective-permute-start.2 = (bf16[7488,128]{1,0:T(8,128)(2,1)}, bf16[7488,128]{1,0:T(8,128)(2,1)}, u32[]{:S(2)}, u32[]{:S(2)}) collective-permute-start(bf16[7488,128]{1,0:T(8,128)(2,1)} %collective-permute-done.refs_1_), channel_id=1, source_target_pairs={{0,2},{1,7},{2,4},{3,1},{4,6},{5,3},{6,0},{7,5},{8,10},{9,15},{10,... | collective-permute-start | bytes 5750792 | tf_op jit(solution)/shard_map/ppermute | solution.py:996
  628.5 27.4 %collective-permute-start.4 = (bf16[7488,128]{1,0:T(8,128)(2,1)}, bf16[7488,128]{1,0:T(8,128)(2,1)}, u32[]{:S(2)}, u32[]{:S(2)}) collective-permute-start(bf16[7488,128]{1,0:T(8,128)(2,1)} %get-tuple-element.46.refs_0_), channel_id=1, source_target_pairs={{0,1},{1,0},{2,3},{3,2},{4,5},{5,4},{6,7},{7,6},{8,9},{9,8},{10,11... | collective-permute-start | bytes 5750792 | tf_op jit(solution)/shard_map/ppermute | solution.py:996
  629.5 26.4 %collective-permute-start.5 = (bf16[7488,128]{1,0:T(8,128)(2,1)}, bf16[7488,128]{1,0:T(8,128)(2,1)}, u32[]{:S(2)}, u32[]{:S(2)}) collective-permute-start(bf16[7488,128]{1,0:T(8,128)(2,1)} %collective-permute-done.refs_1_), channel_id=1, source_target_pairs={{0,1},{1,0},{2,3},{3,2},{4,5},{5,4},{6,7},{7,6},{8,9},{9,8},{10,11... | collective-permute-start | bytes 5750792 | tf_op jit(solution)/shard_map/ppermute | solution.py:996
  642.4 13.5 %collective-permute-start.6 = (bf16[7488,128]{1,0:T(8,128)(2,1)}, bf16[7488,128]{1,0:T(8,128)(2,1)}, u32[]{:S(2)}, u32[]{:S(2)}) collective-permute-start(bf16[7488,128]{1,0:T(8,128)(2,1)} %collective-permute-done.1.refs_2_), channel_id=1, source_target_pairs={{0,1},{1,0},{2,3},{3,2},{4,5},{5,4},{6,7},{7,6},{8,9},{9,8},{10,11... | collective-permute-start | bytes 5750792 | tf_op jit(solution)/shard_map/ppermute | solution.py:996
  655.7 5.1 collective-permute-start.3

commit v10 on v9

--- a/solution.py
+++ b/solution.py
@@ -785,7 +785,7 @@
     ring.end()
 
 
-def place_columns(chunks, layer, layers, d, ff, into=(), slots=4, some=2):
+def place_columns(chunks, layer, layers, d, ff, into=(), slots=3, some=4):
     devices = chunks.shape[1]
     chips, rows = devices // CORES, d // devices
     x = chunks.reshape(layers, -1, devices, 2, chips, rows, LANES)
@@ -1008,8 +1008,8 @@
         gate, up, down = place_blocks(me, near, (gate, up, down))
         down, opposite = lax.optimization_barrier((down, opposite))
         last = send(opposite, swap)
-        weights = place_blocks(me, other, (gate, up, down))
-        weights = place_blocks(me, {(2, 0): opposite, (2, 1): last}, weights)
+        weights = place_blocks(me, {**other, (2, 0): opposite}, (gate, up, down))
+        weights = place_blocks(me, {(2, 1): last}, weights)
         return (*weights, first, *states)
 
     seq, whole, rows = P(("rep", "dp"), None, None), P(None, None, None), P(None, "dp", None)

time: 665 us -> 666 us (level)
  no operation moved by 1% of the time
where the time goes in v10:
time: 666 us
  Pallas kernels  657 us (99%)
    pallas_call x1, Pallas kernels, backward(): pl.pallas_call(functools.partial(backward_kernel, chips, tile), out_shape...  495 us
    pallas_call x1, Pallas kernels, forward(): pl.pallas_call(functools.partial(forward_kernel, tile), grid=(ff // width...  87.3 us
    pallas_call x2, Pallas kernels, place_columns(): pl.pallas_call(functools.partial(place_columns_kernel, layer, slots), in_...  27.4 us
    pallas_call x1, Pallas kernels, moments(): pl.pallas_call(functools.partial(moments_kernel, layers, parts, slots), i...  24.6 us
    pallas_call x3, Pallas kernels, place_blocks(): pl.pallas_call(functools.partial(place_blocks_kernel, wheres), in_specs=[...  14.9 us
  transfers between devices with their start and end apart: 7, of which 2 were waited for; matrix products, arithmetic and copies ran while one was open for 0% of the time, Pallas kernels for 11%

profile of v10, /device:TPU:113, one launch (start us, length us, event | category | flops | bytes accessed | tf_op | source)
XLA Modules:
  0.0 665.6 jit_solution(9236232227808038682)
XLA Ops:
  0.6 87.3 %forward.1 = (bf16[2,2048,1152]{2,1,0:T(8,128)(2,1)}, bf16[2048,1152]{1,0:T(8,128)(2,1)}) custom-call(bf16[2048,1152]{1,0:T(8,128)(2,1)} %bitcast.7, bf16[2,1152,4608]{2,1,0:T(8,128)(2,1)} %refs_3_.2, bf16[2,1152,4608]{2,1,0:T(8,128)(2,1)} %refs_4_.2, bf16[2,4608,1152]{2,1,0:T(8,128)(2,1)} %refs_5_.2), custom_call_target="tpu_custom_call" | custom-call | flops 65229815808 | bytes 31850496 | tf_op jit(solution)/shard_map/forward/pallas_call | solution.py:121
  88.0 495.3 %backward.1 = (bf16[2,144,4608]{2,1,0:T(8,128)(2,1)}, bf16[2,144,4608]{2,1,0:T(8,128)(2,1)}, bf16[2,576,1152]{2,1,0:T(8,128)(2,1)}, bf16[18,8,1152,128]{3,2,1,0:...) custom-call(bf16[2,2048,1152]{2,1,0:T(8,128)(2,1)} %get-tuple-element.44.ref, ...), custom_call_target="tpu_custom_call" | custom-call | flops 304405807104 | bytes 127401984 | tf_op jit(solution)/shard_map/backward/pallas_call | solution.py:678
  583.3 0.5 collective-permute-start
  583.8 1.0 collective-permute-start.1
  584.8 15.1 %place_columns.2 = (bf16[2,1152,4608]{2,1,0:T(8,128)(2,1)}, bf16[2,1152,4608]{2,1,0:T(8,128)(2,1)}) custom-call(bf16[2,9,8,2,4,144,128]{6,5,4,3,2,1,0:T(8,128)(2,1)} %bitcast.5), custom_call_target="tpu_custom_call" | custom-call | flops 2717908992 | bytes 42467328 | tf_op jit(solution)/shard_map/place_columns/pallas_call | solution.py:793
  599.9 24.6 %moments.1 = (f32[2,144,4608]{2,1,0:T(8,128)}, f32[2,144,4608]{2,1,0:T(8,128)}, f32[2,576,1152]{2,1,0:T(8,128)}, f32[2,144,4608]{2,1,0:T(8,128)}, f32[2,144,4608]{2,1,0:T(8,128)}, /*index=5*/f32[2,576,1152]{2,1,0:T(8,128)}) custom-call(f32[2,144,4608]{2,1,0:T(8,128)} %refs_0_.1, f32[2,144,4608]{2,1,0:T(8,128)} %refs_1_.1, f32[2,576,1152]{2,1,0:T(8,128)} %refs_2_.1, ...), custom_call_target="tpu_custom_call" | custom-call | flops 4586471424 | bytes 71663616 | tf_op jit(solution)/shard_map/moments/pallas_call | solution.py:846
  624.6 1.5 collective-permute-done.refs_1_
  626.1 2.2 collective-permute-done.1.refs_2_
  628.2 0.3 collective-permute-start.2
  628.5 1.0 collective-permute-start.4
  629.5 0.1 collective-permute-start.5
  629.6 12.3 %place_columns.3 = (bf16[2,1152,4608]{2,1,0:T(8,128)(2,1)}, bf16[2,1152,4608]{2,1,0:T(8,128)(2,1)}) custom-call(bf16[2,9,8,2,4,144,128]{6,5,4,3,2,1,0:T(8,128)(2,1)} %bitcast.6, bf16[2,1152,4608]{2,1,0:T(8,128)(2,1)} %get-tuple-element.55.refs_0_, bf16[2,1152,4608]{2,1,0:T(8,128)(2,1)} %get-tuple-element.56.refs_1_), custom_call_target="tpu_custom_call", output_to_operand_aliasing={{0}: (1, {}), {1}: (2, {})} | custom-call | flops 2717908992 | bytes 42467328 | tf_op jit(solution)/shard_map/place_columns/pallas_call | solution.py:793
  641.9 0.5 collective-permute-start.6
  642.4 7.9 %place_rows.1.refs_5_ = bf16[2,4608,1152]{2,1,0:T(8,128)(2,1)} custom-call(bf16[1,5,8,1152,128]{4,3,2,1,0:T(8,128)(2,1)} %bitcast.9), custom_call_target="tpu_custom_call" | custom-call | flops 1358954496 | bytes 21233664 | tf_op jit(solution)/shard_map/place_rows/pallas_call | solution.py:900
  650.4 4.9 place_blocks.3
  655.3 0.0 collective-permute-done.2.refs_3_
  655.3 0.2 collective-permute-start.3
  655.4 0.0 collective-permute-done.4.refs_0_
  655.4 0.0 collective-permute-done.5.refs_1_
  655.5 0.0 collective-permute-done.6.refs_2_
  655.5 7.0 %place_blocks.4 = (bf16[2,1152,4608]{2,1,0:T(8,128)(2,1)}, bf16[2,1152,4608]{2,1,0:T(8,128)(2,1)}, bf16[2,4608,1152]{2,1,0:T(8,128)(2,1)}) custom-call(s32[1]{0:T(128)} %bitcast.me_ref, bf16[7488,128]{1,0:T(8,128)(2,1)} %collective-permute-done.4.refs_0_, ...), custom_call_target="tpu_custom_call", output_to_operand_aliasing={{0}: (5, {}), {1}: (6, {}), {2}: (7, {})} | custom-call | tf_op jit(solution)/shard_map/place_blocks/pallas_call | solution.py:967
  662.4 0.0 collective-permute-done.3.refs_0_
  662.4 3.0 place_blocks.5
Async XLA Ops:
  583.3 42.8 %collective-permute-start = (bf16[7488,128]{1,0:T(8,128)(2,1)}, bf16[7488,128]{1,0:T(8,128)(2,1)}, u32[]{:S(2)}, u32[]{:S(2)}) collective-permute-start(bf16[7488,128]{1,0:T(8,128)(2,1)} %get-tuple-element.46.refs_0_), channel_id=1, source_target_pairs={{0,2},{1,7},{2,4},{3,1},{4,6},{5,3},{6,0},{7,5},{8,10},{9,15},{10,... | collective-permute-start | bytes 5750792 | tf_op jit(solution)/shard_map/ppermute | solution.py:996
  583.8 44.5 %collective-permute-start.1 = (bf16[7488,128]{1,0:T(8,128)(2,1)}, bf16[7488,128]{1,0:T(8,128)(2,1)}, u32[]{:S(2)}, u32[]{:S(2)}) collective-permute-start(bf16[7488,128]{1,0:T(8,128)(2,1)} %get-tuple-element.46.refs_0_), channel_id=1, source_target_pairs={{2,0},{7,1},{4,2},{1,3},{6,4},{3,5},{0,6},{5,7},{10,8},{15,9},{12,... | collective-permute-start | bytes 5750792 | tf_op jit(solution)/shard_map/ppermute | solution.py:996
  628.2 27.0 %collective-permute-start.2 = (bf16[7488,128]{1,0:T(8,128)(2,1)}, bf16[7488,128]{1,0:T(8,128)(2,1)}, u32[]{:S(2)}, u32[]{:S(2)}) collective-permute-start(bf16[7488,128]{1,0:T(8,128)(2,1)} %collective-permute-done.refs_1_), channel_id=1, source_target_pairs={{0,2},{1,7},{2,4},{3,1},{4,6},{5,3},{6,0},{7,5},{8,10},{9,15},{10,... | collective-permute-start | bytes 5750792 | tf_op jit(solution)/shard_map/ppermute | solution.py:996
  628.5 26.9 %collective-permute-start.4 = (bf16[7488,128]{1,0:T(8,128)(2,1)}, bf16[7488,128]{1,0:T(8,128)(2,1)}, u32[]{:S(2)}, u32[]{:S(2)}) collective-permute-start(bf16[7488,128]{1,0:T(8,128)(2,1)} %get-tuple-element.46.refs_0_), channel_id=1, source_target_pairs={{0,1},{1,0},{2,3},{3,2},{4,5},{5,4},{6,7},{7,6},{8,9},{9,8},{10,11... | collective-permute-start | bytes 5750792 | tf_op jit(solution)/shard_map/ppermute | solution.py:996
  629.5 26.0 %collective-permute-start.5 = (bf16[7488,128]{1,0:T(8,128)(2,1)}, bf16[7488,128]{1,0:T(8,128)(2,1)}, u32[]{:S(2)}, u32[]{:S(2)}) collective-permute-start(bf16[7488,128]{1,0:T(8,128)(2,1)} %collective-permute-done.refs_1_), channel_id=1, source_target_pairs={{0,1},{1,0},{2,3},{3,2},{4,5},{5,4},{6,7},{7,6},{8,9},{9,8},{10,11... | collective-permute-start | bytes 5750792 | tf_op jit(solution)/shard_map/ppermute | solution.py:996
  641.9 13.5 %collective-permute-start.6 = (bf16[7488,128]{1,0:T(8,128)(2,1)}, bf16[7488,128]{1,0:T(8,128)(2,1)}, u32[]{:S(2)}, u32[]{:S(2)}) collective-permute-start(bf16[7488,128]{1,0:T(8,128)(2,1)} %collective-permute-done.1.refs_2_), channel_id=1, source_target_pairs={{0,1},{1,0},{2,3},{3,2},{4,5},{5,4},{6,7},{7,6},{8,9},{9,8},{10,11... | collective-permute-start | bytes 5750792 | tf_op jit(solution)/shard_map/ppermute | solution.py:996
  655.3 7.1 %collective-permute-start.3 = (bf16[7488,128]{1,0:T(8,128)(2,1)}, bf16[7488,128]{1,0:T(8,128)(2,1)}, u32[]{:S(2)}, u32[]{:S(2)}) collective-permute-start(bf16[7488,128]{1,0:T(8,128)(2,1)} %collective-permute-done.2.refs_3_), channel_id=1, source_target_pairs={{0,1},{1,0},{2,3},{3,2},{4,5},{5,4},{6,7},{7,6},{8,9},{9,8},{10,11... | collective-permute-start | bytes 5750792 | tf_op jit(solution)/shard_map/ppermute | solution.py:996
